TPU v7x, 32 devices: a whole 2x2x4 slice. The times are simulated.
32 devices in a mesh: dom: 4 (over y, core), rep: 8 (over z, x).
Axes of the slice: x: 2, y: 2, z: 4, core: 2. Of those that a mesh axis runs over, the one named last changes fastest.
Arguments:
- facts: float32 [131072, 256], P(('dom', 'rep')), may hold values from -6 to 6
- row_owner: int32 [131072, 1], P(('dom', 'rep')), may hold values from 0 to 3; in each aligned block of 4096 rows (0 to 4095, 4096 to 8191, ...) at most 2048 rows name the same one
- key_offset: int32 [131072], P(('dom', 'rep')), may hold values from 0 to 1023
Outputs:
- key_means: float32 [4096, 256], P(('dom', 'rep'))
- key_counts: float32 [4096], P(('dom', 'rep'))
Inputs may be any that keep to these rules, and one draw needn't show every extreme that they name: `row_owner`: in the rows of one device no key range is named by more than 2048 rows, a bound that some block reaches.
All inputs are finite; a program needn't handle non-finite values.
Results may differ from a plain program's by a relative error of at most 0.0003.
Values sent between devices are 32-bit elements; how exact they have to be, the bound alone decides.
No kernel may reach another device: no remote copies, remote signals or barrier semaphores. Data moves between devices by JAX's collectives and lax.ppermute only.
A program may use at most 64 MiB of HBM per device.

v0:
```python
import jax
import jax.numpy as jnp
from jax import lax
from jax.sharding import PartitionSpec as P

KEYS = 4096


def block_table(offsets, high_part, low_part, start, key_step):
    wanted = start + jnp.arange(key_step, dtype=jnp.int32)
    onehot = (offsets[:, :, None] == wanted[None, None, :]).astype(jnp.bfloat16)
    upper = jnp.einsum("grk,grm->gkm", onehot, high_part, preferred_element_type=jnp.float32)
    lower = jnp.einsum("grk,grm->gkm", onehot, low_part, preferred_element_type=jnp.float32)
    return (upper + lower, jnp.sum(onehot, axis=1, dtype=jnp.float32))


def grouped_table(offsets, values, key_span):
    width = values.shape[-1]
    groups = offsets.shape[0]
    high_part = lax.optimization_barrier(values.astype(jnp.bfloat16))
    low_part = (values - high_part.astype(jnp.float32)).astype(jnp.bfloat16)
    key_step = min(512, key_span)
    blocks = key_span // key_step
    if blocks == 1:
        table_sums, table_counts = block_table(offsets, high_part, low_part, 0, key_step)
        return (
            table_sums.reshape(groups * key_span, width),
            table_counts.reshape(groups * key_span),
        )

    def one_block(block_index):
        return block_table(offsets, high_part, low_part, block_index * key_step, key_step)

    table_sums, table_counts = lax.map(one_block, jnp.arange(blocks, dtype=jnp.int32))
    table_sums = jnp.moveaxis(table_sums, 0, 1).reshape(groups * key_span, width)
    table_counts = jnp.moveaxis(table_counts, 0, 1).reshape(groups * key_span)
    return (table_sums, table_counts)


def bucket_rows(row_range, n_dom, capacity):
    rows_here = row_range.shape[0]
    range_hot = (row_range[:, None] == jnp.arange(n_dom, dtype=jnp.int32)[None, :]).astype(
        jnp.int32
    )
    before = jnp.cumsum(range_hot, axis=0) - range_hot
    slot_of = jnp.sum(range_hot * before, axis=1)
    position = row_range * capacity + slot_of
    empty = jnp.full((n_dom * capacity,), rows_here, jnp.int32)
    return empty.at[position].set(
        jnp.arange(rows_here, dtype=jnp.int32), unique_indices=True, mode="drop"
    )


def finish(table_sums, table_counts):
    return (table_sums / jnp.maximum(table_counts, 1.0)[:, None], table_counts)


def per_device(facts, row_owner, key_offset):
    row_range = row_owner[:, 0]
    n_dom = lax.axis_size("dom")
    key_span = KEYS // n_dom
    capacity = 2 * facts.shape[0] // n_dom
    measures = facts.shape[1]
    source = bucket_rows(row_range, n_dom, capacity)
    picked = jnp.take(facts, source, axis=0, mode="fill", fill_value=0.0)
    offsets = jnp.take(key_offset, source, axis=0, mode="fill", fill_value=-1)
    local_sums, local_counts = grouped_table(
        offsets.reshape(n_dom, capacity), picked.reshape(n_dom, capacity, measures), key_span
    )
    range_sums, range_counts = (
        lax.psum_scatter(local_sums, "dom", scatter_dimension=0, tiled=True),
        lax.psum_scatter(local_counts, "dom", scatter_dimension=0, tiled=True),
    )
    table_sums, table_counts = (
        lax.psum_scatter(range_sums, "rep", scatter_dimension=0, tiled=True),
        lax.psum_scatter(range_counts, "rep", scatter_dimension=0, tiled=True),
    )
    return finish(table_sums, table_counts)


def solution(mesh):
    placed = (P(("dom", "rep"), None), P(("dom", "rep"), None), P(("dom", "rep")))
    return jax.shard_map(
        per_device,
        mesh=mesh,
        in_specs=placed,
        out_specs=(P(("dom", "rep"), None), P(("dom", "rep"))),
        check_vma=False,
    )
```

profile of v0, /device:TPU:0, one launch (start us, length us, event | category | flops | bytes accessed | tf_op | source)
XLA Modules:
  0.0 269.2 jit_solution(16950049690493843657)
XLA Ops:
  8.0 1.1 reduce-window.6
  9.6 0.8 fusion.12
  10.5 0.7 compare_select_fusion
  11.2 15.5 %scatter_custom_fusion = s32[8192]{0:T(1024)S(1)} fusion(s32[4096]{0:T(1024)S(1)} %bitcast.64, s32[4096]{0:T(1024)S(1)} %iota.19, s32[]{:T(128)} %constant.39.clone.1), kind=kCustom, calls=%fused_computation.34 | custom fusion | bytes 32772 | tf_op jit(solution)/shard_map/scatter | solution.py:49
  26.8 45.5 %gather_fusion = s32[8192]{0:T(1024)S(1)} fusion(s32[4096]{0:T(1024)S(1)} %copy-done, s32[8192]{0:T(1024)S(1)} %fusion.14), kind=kCustom, calls=%fused_computation | custom fusion | bytes 98304 | tf_op jit(solution)/shard_map/jit(_take)/gather | solution.py:66
  72.4 33.6 %gather_fusion.1 = f32[8192,256]{1,0:T(8,128)} fusion(f32[4096,256]{1,0:T(8,128)} %param.5, s32[8192]{0:T(1024)S(1)} %fusion.14), kind=kCustom, calls=%fused_computation.1 | custom fusion | bytes 16809984 | tf_op jit(solution)/shard_map/jit(_take)/gather | solution.py:65
  106.0 4.9 %select_convert_fusion = bf16[4,2048,256]{2,1,0:T(8,128)(2,1)S(1)} fusion(f32[4,2048,256]{2,1,0:T(8,128)} %bitcast.55, pred[4,2048]{1,0:T(4,128)(4,1)S(1)} %broadcast_in_dim.46), kind=kLoop, calls=%fused_computation.17 | loop fusion | flops 2097152 | bytes 12591104 | tf_op jit(solution)/shard_map/convert_element_type | solution.py:20
  110.9 1.0 copy-done.1
  111.9 4.1 %subtract_convert_fusion = bf16[4,2048,256]{2,1,0:T(8,128)(2,1)} fusion(bf16[4,2048,256]{2,1,0:T(8,128)(2,1)S(1)} %select_convert_fusion, f32[4,2048,256]{2,1,0:T(8,128)S(1)} %bitcast.56, pred[4,2048]{1,0:T(4,128)(4,1)S(1)} %broadcast_in_dim.46), kind=kLoop, calls=%fused_computation.16 | loop fusion | flops 8388608 | bytes 16785408 | tf_op jit(solution)/shard_map/convert_element_type | solution.py:21
  116.0 24.6 %while.13 = (s32[]{:T(128)}, f32[2,4,512,256]{3,2,1,0:T(8,128)}, f32[2,4,512]{2,1,0:T(4,128)S(1)}, s32[8192]{0:T(1024)}, s32[2]{0:T(128)S(1)}, /*index=5*/bf16[4...) while((s32[]{:T(128)}, f32[2,4,512,256]{3,2,1,0:T(8,128)}, ...), condition=%wide.wide.region_6.7_spmd, body=%wide.wide.region_4.6_spmd.sunk | while | flops 4320655872 | bytes 65143004 | solution.py:34
  117.2 4.7 %fusion.33 = f32[4,512,256]{2,1,0:T(8,128)S(1)} fusion(bf16[4,2048,256]{2,1,0:T(8,128)(2,1)} %get-tuple-element.163, s32[4,2048]{1,0:T(4,128)S(1)} %get-tuple-element.164, s32[512]{0:T(512)S(1)} %iota_add_fusion.3), kind=kOutput, calls=%fused_computation.4.clone.clone.1 | convolution fusion | flops 2151677952 | bytes 6326272 | tf_op jit(solution)/shard_map/while/body/eval_jaxpr/grk,grm->gkm/dot_general | solution.py:13
  122.0 2.4 bitcast_dynamic-update-slice_fusion.6
  124.4 2.0 copy-done.5
  126.4 1.9 convert_reduce_fusion.3
  129.6 4.7 %fusion.33 = f32[4,512,256]{2,1,0:T(8,128)S(1)} fusion(bf16[4,2048,256]{2,1,0:T(8,128)(2,1)} %get-tuple-element.163, s32[4,2048]{1,0:T(4,128)S(1)} %get-tuple-element.164, s32[512]{0:T(512)S(1)} %iota_add_fusion.3), kind=kOutput, calls=%fused_computation.4.clone.clone.1 | convolution fusion | flops 2151677952 | bytes 6326272 | tf_op jit(solution)/shard_map/while/body/eval_jaxpr/grk,grm->gkm/dot_general | solution.py:13
  134.3 2.4 bitcast_dynamic-update-slice_fusion.6
  136.8 2.0 copy-done.5
  138.7 1.9 convert_reduce_fusion.3
  140.6 4.4 %copy.8 = f32[4,2,512,256]{3,2,1,0:T(8,128)} copy(f32[4,2,512,256]{3,2,0,1:T(8,128)} %bitcast.58) | data formatting | bytes 8388608 | tf_op jit(solution)/shard_map/transpose | solution.py:35
  145.1 47.4 %reduce-scatter.3.cloned.1.call-done = f32[1024,256]{1,0:T(8,128)} async-done(((f32[4096,256]{1,0:T(8,128)}), f32[1024,256]{1,0:T(8,128)}) %reduce-scatter.3.cloned.1.call-update) | async-done | bytes 1048592 | tf_op jit(solution)/shard_map/reduce_scatter | solution.py:71
  194.4 10.1 %all-reduce = f32[4096]{0:T(1024)S(1)} all-reduce(f32[4096]{0:T(1024)S(1)} %bitcast.61), channel_id=4, replica_groups=mesh['dom'=4,'rep'=8] {'dom'}, use_global_device_ids=true, to_apply=%region_9.10.clone | all-reduce | flops 4096 | bytes 32768
  205.2 21.7 %all-reduce.1 = f32[1024]{0:T(1024)S(1)} all-reduce(f32[1024]{0:T(1024)S(1)} %dynamic-slice.1), channel_id=5, replica_groups=mesh['dom'=4,'rep'=8] {'rep'}, use_global_device_ids=true, to_apply=%region_10.11.clone | all-reduce | flops 1024 | bytes 8192
  227.4 33.3 %reduce-scatter.5.cloned.1.call-done = f32[128,256]{1,0:T(8,128)} async-done(((f32[1024,256]{1,0:T(8,128)}), f32[128,256]{1,0:T(8,128)}) %reduce-scatter.5.cloned.1.call-update) | async-done | bytes 131088 | tf_op jit(solution)/shard_map/reduce_scatter | solution.py:75
  260.8 1.6 broadcast_divide_fusion
  (49 shorter events, 4.5 us)
Async XLA Ops:
  7.2 19.6 %copy-start = (s32[4096]{0:T(1024)S(1)}, s32[4096]{0:T(1024)}, u32[]{:S(2)}) copy-start(s32[4096]{0:T(1024)} %param.7) | copy-start | bytes 49156
  7.2 185.3 %reduce-scatter.3.cloned.1.call-start = ((), (), s32[]{:S(2)}) async-start(), calls=%async_computation.2 | async-start | bytes 5242880 | tf_op jit(solution)/shard_map/reduce_scatter | solution.py:71
  72.4 43.6 %copy-start.6 = (s32[8192]{0:T(1024)}, s32[8192]{0:T(1024)S(1)}, u32[]{:S(2)}) copy-start(s32[8192]{0:T(1024)S(1)} %get-tuple-element.140) | copy-start | bytes 98308
  106.0 5.9 %copy-start.1 = (f32[8192,256]{1,0:T(8,128)S(1)}, f32[8192,256]{1,0:T(8,128)}, u32[]{:S(2)}) copy-start(f32[8192,256]{1,0:T(8,128)} %gather_fusion.1) | copy-start | bytes 25165828
  111.9 4.1 %copy-start.2 = (bf16[4,2048,256]{2,1,0:T(8,128)(2,1)}, bf16[4,2048,256]{2,1,0:T(8,128)(2,1)S(1)}, u32[]{:S(2)}) copy-start(bf16[4,2048,256]{2,1,0:T(8,128)(2,1)S(1)} %select_convert_fusion) | copy-start | bytes 12582916
  117.2 4.7 %copy-start.3 = (bf16[4,2048,256]{2,1,0:T(8,128)(2,1)S(1)}, bf16[4,2048,256]{2,1,0:T(8,128)(2,1)}, u32[]{:S(2)}) copy-start(bf16[4,2048,256]{2,1,0:T(8,128)(2,1)} %get-tuple-element.162) | copy-start | bytes 12582916 | tf_op jit(solution)/shard_map/while
  117.2 4.7 %copy-start.4 = (f32[2,4,512,256]{3,2,1,0:T(8,128)S(1)}, f32[2,4,512,256]{3,2,1,0:T(8,128)}, u32[]{:S(2)}) copy-start(f32[2,4,512,256]{3,2,1,0:T(8,128)} %get-tuple-element.148) | copy-start | bytes 12582916 | tf_op jit(solution)/shard_map/while
  124.4 2.0 copy-start.5
  129.5 4.7 %copy-start.3 = (bf16[4,2048,256]{2,1,0:T(8,128)(2,1)S(1)}, bf16[4,2048,256]{2,1,0:T(8,128)(2,1)}, u32[]{:S(2)}) copy-start(bf16[4,2048,256]{2,1,0:T(8,128)(2,1)} %get-tuple-element.162) | copy-start | bytes 12582916 | tf_op jit(solution)/shard_map/while
  129.5 4.7 %copy-start.4 = (f32[2,4,512,256]{3,2,1,0:T(8,128)S(1)}, f32[2,4,512,256]{3,2,1,0:T(8,128)}, u32[]{:S(2)}) copy-start(f32[2,4,512,256]{3,2,1,0:T(8,128)} %get-tuple-element.148) | copy-start | bytes 12582916 | tf_op jit(solution)/shard_map/while
  136.7 2.0 copy-start.5
  145.0 47.5 %copy-start.8 = (u32[32]{0:T(128)S(1)}, u32[32]{0:T(128)}, u32[]{:S(2)}) copy-start(u32[32]{0:T(128)} %constant.60) | copy-start | bytes 388
  145.0 48.1 %copy-start.7 = (u32[32]{0:T(128)S(1)}, u32[32]{0:T(128)}, u32[]{:S(2)}) copy-start(u32[32]{0:T(128)} %constant.64) | copy-start | bytes 388
  145.1 115.7 %reduce-scatter.5.cloned.1.call-start = ((), (), s32[]{:S(2)}) async-start(), calls=%async_computation.3 | async-start | bytes 1179648 | tf_op jit(solution)/shard_map/reduce_scatter | solution.py:75
Sparse Core Ops, SparseCore 0:
  145.2 47.2 reduce-scatter.2
  195.9 64.8 reduce-scatter.4
where the time goes:
time: 270 us; the launch traced here: 269 us
  local copies, waits for them, and re-layouts  107 us (40%)
  waiting for transfers between devices  80.7 us (30%)
  blocking collectives  31.8 us (12%)
  other arithmetic  18.7 us (7%)
  between operations  15.5 us (6%)
  matrix products  14.3 us (5%)
    reduce_scatter x1, waiting for transfers between devices, per_device(): lax.psum_scatter(local_sums, 'dom', scatter_dimension=0, tiled=True)  47.4 us
    gather x1, local copies, waits for them, and re-layouts, per_device(): offsets = jnp.take(key_offset, source, axis=0, mode='fill', fill_value=-1)  45.5 us
    gather x1, local copies, waits for them, and re-layouts, per_device(): picked = jnp.take(facts, source, axis=0, mode='fill', fill_value=0.0)  33.6 us
    reduce_scatter x1, waiting for transfers between devices, per_device(): lax.psum_scatter(range_sums, 'rep', scatter_dimension=0, tiled=True)  33.3 us
    unnamed x2, blocking collectives  31.8 us
    scatter x1, local copies, waits for them, and re-layouts, bucket_rows(): empty.at[position]  15.5 us
    dot_general x2, matrix products, block_table(): jnp.einsum('grk,grm->gkm', onehot, low_part, preferred_element_type=jnp.f...  9.42 us
  transfers between devices with their start and end apart: 2, of which 2 were waited for; matrix products, arithmetic and copies ran while one was open for 1% of the time, Pallas kernels for 0%

commit v1 on v0

v1 whole, which is shorter than its diff:
```python
import functools

import jax
import jax.numpy as jnp
from jax import lax
from jax.experimental import pallas as pl
from jax.experimental.pallas import tpu as pltpu
from jax.sharding import PartitionSpec as P

KEYS = 4096
LANES = 128
SUB = 8
TABLES = 4
CHUNKS = 8
AXES = ("dom", "rep")


def bits_of(size):
    return [1 << b for b in range(size.bit_length() - 1)]


def local_kernel(me_ref, owner_ref, offset_ref, facts, *rest, outs, span, block, tiles):
    out_refs = rest[: len(outs)]
    tables = rest[len(outs) : len(outs) + TABLES]
    buf, addr_v, addr_s, sem, addr_sem = rest[len(outs) + TABLES :]
    rows = buf.shape[0]
    step = rows // CHUNKS
    copies = [
        pltpu.make_async_copy(
            facts.at[pl.ds(i * step, step)], buf.at[pl.ds(i * step, step)], sem.at[i]
        )
        for i in range(CHUNKS)
    ]
    for copy in copies:
        copy.start()
    key = (owner_ref[...] * span + offset_ref[...]) ^ (me_ref[0] * block)
    addr_v[...] = (key >> 3) * (SUB * tiles) + (key & (SUB - 1))
    addr_copy = pltpu.make_async_copy(addr_v, addr_s, addr_sem)
    addr_copy.start()

    n_blocks = KEYS // block
    groups = owner_ref.shape[0]

    def count(i, total):
        k = (owner_ref[pl.ds(i, 1), :] * span + offset_ref[pl.ds(i, 1), :]) ^ (me_ref[0] * block)
        high = (k // block == lax.broadcasted_iota(jnp.int32, (n_blocks, LANES), 0))
        low = (k % block == lax.broadcasted_iota(jnp.int32, (LANES, LANES), 0))
        return total + lax.dot_general(
            high.astype(jnp.float32).astype(jnp.bfloat16),
            low.astype(jnp.float32).astype(jnp.bfloat16),
            (((1,), (1,)), ((), ())),
            preferred_element_type=jnp.float32,
        )

    counts = lax.fori_loop(0, groups, count, jnp.zeros((n_blocks, LANES), jnp.float32))

    zero_rows = 8 * SUB

    def zero(i, _):
        for t in tables:
            t[pl.ds(pl.multiple_of(i * zero_rows, zero_rows), zero_rows), :] = jnp.zeros(
                (zero_rows, LANES), jnp.float32
            )
        return 0

    lax.fori_loop(0, KEYS * tiles // zero_rows, zero, 0)
    addr_copy.wait()
    per_group = SUB * tiles
    groups_step = step // per_group
    for c in range(CHUNKS):
        copies[c].wait()

        def add_rows(g, _):
            base = c * step + g * per_group
            first = (c * groups_step + g) * SUB
            for j in range(SUB):
                table = tables[j % TABLES]
                r = first + j
                at = pl.ds(addr_s[r // LANES, r % LANES], tiles, stride=SUB)
                table[at, :] = table[at, :] + buf[pl.ds(base + j, tiles, stride=SUB), :]
            return 0

        lax.fori_loop(0, groups_step, add_rows, 0, unroll=2)

    part = block * tiles
    for out, ids in zip(out_refs, outs):
        for at, b in enumerate(ids):
            size = min(part, 64)

            def total(i, _):
                d = pl.multiple_of(i * size, size)
                s = tables[0][pl.ds(b * part + d, size), :]
                for t in tables[1:]:
                    s = s + t[pl.ds(b * part + d, size), :]
                out[at, pl.ds(d, size), :] = s
                return 0

            lax.fori_loop(0, part // size, total, 0)
            out[at, pl.ds(part, SUB), :] = jnp.broadcast_to(counts[b : b + 1, :], (SUB, LANES))


def local_table(facts, owner, offset, me, outs, span, block):
    rows, width = facts.shape
    tiles = width // LANES
    view = facts.reshape(rows // SUB, SUB, tiles, LANES).transpose(0, 2, 1, 3)
    view = view.reshape(rows * tiles, LANES)
    lanes = (rows // LANES, LANES)
    vmem = pl.BlockSpec(memory_space=pltpu.VMEM)
    unit = block * tiles + SUB
    return pl.pallas_call(
        functools.partial(local_kernel, outs=outs, span=span, block=block, tiles=tiles),
        out_shape=[jax.ShapeDtypeStruct((len(ids), unit, LANES), jnp.float32) for ids in outs],
        in_specs=[
            pl.BlockSpec(memory_space=pltpu.SMEM),
            vmem,
            vmem,
            pl.BlockSpec(memory_space=pl.ANY),
        ],
        out_specs=[vmem] * len(outs),
        scratch_shapes=[pltpu.VMEM((KEYS * tiles, LANES), jnp.float32)] * TABLES
        + [
            pltpu.VMEM((rows * tiles, LANES), jnp.float32),
            pltpu.VMEM(lanes, jnp.int32),
            pltpu.SMEM(lanes, jnp.int32),
            pltpu.SemaphoreType.DMA((CHUNKS,)),
            pltpu.SemaphoreType.DMA,
        ],
        compiler_params=pltpu.CompilerParams(vmem_limit_bytes=32 << 20),
        name="local_table",
    )(me, owner.reshape(lanes), offset.reshape(lanes), view)


def route_kernel(*refs, n_in, outs):
    ins, out_refs = refs[:n_in], refs[n_in:]
    unit = ins[0].shape[1]
    for out, blocks in zip(out_refs, outs):
        for at, terms in enumerate(blocks):
            total = ins[terms[0][0]][terms[0][1]]
            for which, where in terms[1:]:
                total = total + ins[which][where]
            out[at] = total


def route(ins, outs):
    unit = ins[0].shape[1]
    vmem = pl.BlockSpec(memory_space=pltpu.VMEM)
    return pl.pallas_call(
        functools.partial(route_kernel, n_in=len(ins), outs=outs),
        out_shape=[jax.ShapeDtypeStruct((len(b), unit, LANES), jnp.float32) for b in outs],
        in_specs=[vmem] * len(ins),
        out_specs=[vmem] * len(outs),
        compiler_params=pltpu.CompilerParams(vmem_limit_bytes=16 << 20),
        name="route",
    )(*ins)


def finish_kernel(kept, arrived, means, counts, *, block, tiles):
    part = block * tiles
    row = kept[0, part : part + 1, :] + arrived[0, part : part + 1, :]
    counts[...] = row[:, :block]
    diagonal = lax.broadcasted_iota(jnp.int32, (block, LANES), 0) == lax.broadcasted_iota(
        jnp.int32, (block, LANES), 1
    )
    column = jnp.sum(jnp.where(diagonal, row, 0.0), axis=1, keepdims=True)
    column = jnp.maximum(column, 1.0)
    for g in range(block // SUB):
        for t in range(tiles):
            at = (g * tiles + t) * SUB
            total = kept[0, at : at + SUB, :] + arrived[0, at : at + SUB, :]
            means[g * SUB : (g + 1) * SUB, t * LANES : (t + 1) * LANES] = (
                total / column[g * SUB : (g + 1) * SUB, :]
            )


def finish(kept, arrived, block, tiles):
    vmem = pl.BlockSpec(memory_space=pltpu.VMEM)
    means, counts = pl.pallas_call(
        functools.partial(finish_kernel, block=block, tiles=tiles),
        out_shape=[
            jax.ShapeDtypeStruct((block, tiles * LANES), jnp.float32),
            jax.ShapeDtypeStruct((1, block), jnp.float32),
        ],
        in_specs=[vmem] * 2,
        out_specs=[vmem] * 2,
        compiler_params=pltpu.CompilerParams(vmem_limit_bytes=16 << 20),
        name="finish",
    )(kept, arrived)
    return means, counts.reshape(block)


def ordered(bits):
    ids = [0]
    for b in reversed(bits):
        ids = ids + [i | b for i in ids]
    return ids


def per_device(facts, row_owner, key_offset):
    n_dom, n_rep = lax.axis_size("dom"), lax.axis_size("rep")
    block = KEYS // (n_dom * n_rep)
    span = KEYS // n_dom
    tiles = facts.shape[1] // LANES
    me = (lax.axis_index("dom") * n_rep + lax.axis_index("rep")).astype(jnp.int32).reshape(1)
    devices = n_dom * n_rep

    def swap(x, bit):
        return lax.ppermute(x, AXES, [(i, i ^ bit) for i in range(devices)])

    bits = [n_rep * b for b in bits_of(n_dom)] + bits_of(n_rep)
    first, second, third, *middle, last = bits
    ids_a = ordered([second, third, *middle])
    ids_b = [i | last for i in ordered([third, second, *middle])]
    half = len(ids_a) // 2
    keep_ids = ids_a[half:] + ids_b[half:] + ids_a[:half] + ids_b[:half]
    send_ids = [i | first for i in keep_ids]
    sent, kept = local_table(
        facts, row_owner[:, 0], key_offset, me, (send_ids, keep_ids), span, block
    )
    got = swap(sent, first)

    def both(which):
        return [(0, which), (1, which)]

    send_a, send_b, keep = route(
        (kept, got),
        (
            [both(i) for i in range(half)],
            [both(half + i) for i in range(half)],
            [both(2 * half + i) for i in range(2 * half)],
        ),
    )
    got_a, got_b = swap(send_a, second), swap(send_b, third)
    quarter = half // 2
    send_a, send_b, keep = route(
        (keep, got_a, got_b),
        (
            [[(0, quarter + i), (1, quarter + i)] for i in range(quarter)],
            [[(0, half + quarter + i), (2, quarter + i)] for i in range(quarter)],
            [[(0, i), (1, i)] for i in range(quarter)]
            + [[(0, half + i), (2, i)] for i in range(quarter)],
        ),
    )
    got_a, got_b = swap(send_a, third), swap(send_b, second)
    pieces = [[(0, i), (1, i)] for i in range(quarter)] + [
        [(0, quarter + i), (2, i)] for i in range(quarter)
    ]
    ins = (keep, got_a, got_b)
    n = quarter
    for bit in middle:
        n = n // 2
        sent, keep = route(
            ins,
            (
                pieces[n : 2 * n] + pieces[3 * n : 4 * n],
                pieces[:n] + pieces[2 * n : 3 * n],
            ),
        )
        ins = (keep, swap(sent, bit))
        pieces = [both(i) for i in range(2 * n)]
    sent, keep = route(ins, (pieces[1:], pieces[:1]))
    return finish(keep, swap(sent, last), block, tiles)


def solution(mesh):
    placed = (P(AXES, None), P(AXES, None), P(AXES))
    return jax.shard_map(
        per_device,
        mesh=mesh,
        in_specs=placed,
        out_specs=(P(AXES, None), P(AXES)),
        check_vma=False,
    )
```

time: 270 us -> 89.5 us (0.33)
  local copies, waits for them, and re-layouts: 107 us -> 3.61 us
  waiting for transfers between devices: 80.7 us -> 32.3 us
  Pallas kernels: 0 us -> 40.5 us
  blocking collectives: 31.8 us -> 0 us
  other arithmetic: 18.7 us -> 0 us
  between operations: 15.5 us -> 0.67 us
  matrix products: 14.3 us -> 0 us
  starting transfers between devices: 0.08 us -> 12.1 us
    reduce_scatter x2 -> x0, waiting for transfers between devices: 80.7 us -> none  [the longest x1 47.4 us: per_device(): lax.psum_scatter(local_sums, 'dom', scatter_dimension=0, tiled=True)]
    gather x2 -> x0, local copies, waits for them, and re-layouts: 79.1 us -> none  [the longest x1 45.5 us: per_device(): offsets = jnp.take(key_offset, source, axis=0, mode='fill', fill_value=-1)]
    pallas_call x0 -> x6, Pallas kernels: none -> 40.5 us  [the longest x1 39.3 us: local_table(): pl.pallas_call(functools.partial(local_kernel, outs=outs, span=span, bloc...]
    ppermute x0 -> x7, waiting for transfers between devices: none -> 32.3 us  [swap(): return lax.ppermute(x, AXES, [(i, i ^ bit) for i in range(devices)])]
    unnamed x2 -> x0, blocking collectives: 31.8 us -> none
    scatter x1 -> x0, local copies, waits for them, and re-layouts: 15.5 us -> none  [bucket_rows(): empty.at[position]]
    dot_general x4 -> x0, matrix products: 14.3 us -> none  [the longest x2 9.42 us: block_table(): jnp.einsum('grk,grm->gkm', onehot, low_part, preferred_element_type=jnp.f...]
    ppermute x0 -> x7, starting transfers between devices: none -> 12.1 us  [swap(): return lax.ppermute(x, AXES, [(i, i ^ bit) for i in range(devices)])]
  transfers between devices with their start and end apart: 2 -> 7, of which waited for: 2 -> 7; matrix products, arithmetic and copies ran while one was open for 1% -> 0% of each run, Pallas kernels for 0% -> 0%
where the time goes in v1:
time: 89.5 us; the launch traced here: 89.1 us
  Pallas kernels  40.5 us (45%)
  waiting for transfers between devices  32.3 us (36%)
  starting transfers between devices  12.1 us (14%)
  local copies, waits for them, and re-layouts  3.61 us (4%)
    pallas_call x1, Pallas kernels, local_table(): pl.pallas_call(functools.partial(local_kernel, outs=outs, span=span, bloc...  39.3 us
    ppermute x7, waiting for transfers between devices, swap(): return lax.ppermute(x, AXES, [(i, i ^ bit) for i in range(devices)])  32.3 us
    ppermute x7, starting transfers between devices, swap(): return lax.ppermute(x, AXES, [(i, i ^ bit) for i in range(devices)])  12.1 us
    unnamed x6, local copies, waits for them, and re-layouts  3.61 us
  transfers between devices with their start and end apart: 7, of which 7 were waited for; matrix products, arithmetic and copies ran while one was open for 0% of the time, Pallas kernels for 0%

profile of v1, /device:TPU:0, one launch (start us, length us, event | category | flops | bytes accessed | tf_op | source)
XLA Modules:
  0.0 89.1 jit_solution(4473110359264681942)
XLA Ops:
  0.6 0.0 copy-start
  0.6 2.2 %copy-done = f32[4096,256]{1,0:T(8,128)S(1)} copy-done((f32[4096,256]{1,0:T(8,128)S(1)}, f32[4096,256]{1,0:T(8,128)}, u32[]{:S(2)}) %copy-start) | copy-done | bytes 4194328
  2.8 0.0 copy-start.1
  2.8 0.7 copy-done.1
  3.5 0.7 copy-done.2
  4.3 39.3 %local_table.1 = (f32[16,264,128]{2,1,0:T(8,128)S(1)}, f32[16,264,128]{2,1,0:T(8,128)S(1)}) custom-call(s32[1]{0:T(128)} %bitcast.me_ref, s32[32,128]{1,0:T(8,128)S(1)} %bitcast.10, s32[32,128]{1,0:T(8,128)S(1)} %bitcast.11, f32[8192,128]{1,0:T(8,128)S(1)} %bitcast.9), custom_call_target="tpu_custom_call" | custom-call | tf_op jit(solution)/shard_map/local_table/pallas_call | solution.py:110
  43.5 0.6 collective-permute-start
  44.1 3.9 %collective-permute-done.refs_1_ = f32[16,264,128]{2,1,0:T(8,128)S(1)} collective-permute-done((f32[16,264,128]{2,1,0:T(8,128)S(1)}, f32[16,264,128]{2,1,0:T(8,128)S(1)}, u32[]{:S(2)}, u32[]{:S(2)}) %collective-permute-start) | collective-permute-done | bytes 2162720 | tf_op jit(solution)/shard_map/ppermute | solution.py:207
  48.0 0.2 route.4
  48.2 2.9 %collective-permute-start.1 = (f32[4,264,128]{2,1,0:T(8,128)S(1)}, f32[4,264,128]{2,1,0:T(8,128)S(1)}, u32[]{:S(2)}, u32[]{:S(2)}) collective-permute-start(f32[4,264,128]{2,1,0:T(8,128)S(1)} %get-tuple-element.19), channel_id=1, source_target_pairs={{0,16},{1,17},{2,18},{3,19},{4,20},{5,21},{6,22},{7,23},{8,24},{9,... | collective-permute-start | bytes 1622024 | tf_op jit(solution)/shard_map/ppermute | solution.py:207
  51.1 1.5 %collective-permute-start.2 = (f32[4,264,128]{2,1,0:T(8,128)S(1)}, f32[4,264,128]{2,1,0:T(8,128)S(1)}, u32[]{:S(2)}, u32[]{:S(2)}) collective-permute-start(f32[4,264,128]{2,1,0:T(8,128)S(1)} %get-tuple-element.20), channel_id=1, source_target_pairs={{0,1},{1,0},{2,3},{3,2},{4,5},{5,4},{6,7},{7,6},{8,9},{9,8},{10,11... | collective-permute-start | bytes 1622024 | tf_op jit(solution)/shard_map/ppermute | solution.py:207
  52.6 11.1 %collective-permute-done.1.refs_1_ = f32[4,264,128]{2,1,0:T(8,128)S(1)} collective-permute-done((f32[4,264,128]{2,1,0:T(8,128)S(1)}, f32[4,264,128]{2,1,0:T(8,128)S(1)}, u32[]{:S(2)}, u32[]{:S(2)}) %collective-permute-start.1) | collective-permute-done | bytes 540704 | tf_op jit(solution)/shard_map/ppermute | solution.py:207
  63.7 1.5 %collective-permute-done.2.refs_2_ = f32[4,264,128]{2,1,0:T(8,128)S(1)} collective-permute-done((f32[4,264,128]{2,1,0:T(8,128)S(1)}, f32[4,264,128]{2,1,0:T(8,128)S(1)}, u32[]{:S(2)}, u32[]{:S(2)}) %collective-permute-start.2) | collective-permute-done | bytes 540704 | tf_op jit(solution)/shard_map/ppermute | solution.py:207
  65.2 0.1 route.5
  65.3 1.6 %collective-permute-start.3 = (f32[2,264,128]{2,1,0:T(8,128)S(1)}, f32[2,264,128]{2,1,0:T(8,128)S(1)}, u32[]{:S(2)}, u32[]{:S(2)}) collective-permute-start(f32[2,264,128]{2,1,0:T(8,128)S(1)} %get-tuple-element.22), channel_id=1, source_target_pairs={{0,1},{1,0},{2,3},{3,2},{4,5},{5,4},{6,7},{7,6},{8,9},{9,8},{10,11... | collective-permute-start | bytes 811016 | tf_op jit(solution)/shard_map/ppermute | solution.py:207
  66.8 0.5 collective-permute-start.4
  67.4 5.4 %collective-permute-done.3.refs_1_ = f32[2,264,128]{2,1,0:T(8,128)S(1)} collective-permute-done((f32[2,264,128]{2,1,0:T(8,128)S(1)}, f32[2,264,128]{2,1,0:T(8,128)S(1)}, u32[]{:S(2)}, u32[]{:S(2)}) %collective-permute-start.3) | collective-permute-done | bytes 270368 | tf_op jit(solution)/shard_map/ppermute | solution.py:207
  72.7 1.2 %collective-permute-done.4.refs_2_ = f32[2,264,128]{2,1,0:T(8,128)S(1)} collective-permute-done((f32[2,264,128]{2,1,0:T(8,128)S(1)}, f32[2,264,128]{2,1,0:T(8,128)S(1)}, u32[]{:S(2)}, u32[]{:S(2)}) %collective-permute-start.4) | collective-permute-done | bytes 270368 | tf_op jit(solution)/shard_map/ppermute | solution.py:207
  74.0 0.1 route.6
  74.0 1.6 %collective-permute-start.5 = (f32[2,264,128]{2,1,0:T(8,128)S(1)}, f32[2,264,128]{2,1,0:T(8,128)S(1)}, u32[]{:S(2)}, u32[]{:S(2)}) collective-permute-start(f32[2,264,128]{2,1,0:T(8,128)S(1)} %get-tuple-element.25), channel_id=1, source_target_pairs={{0,2},{1,3},{2,0},{3,1},{4,6},{5,7},{6,4},{7,5},{8,10},{9,11},{10,... | collective-permute-start | bytes 811016 | tf_op jit(solution)/shard_map/ppermute | solution.py:207
  75.7 4.9 %collective-permute-done.5.refs_1_ = f32[2,264,128]{2,1,0:T(8,128)S(1)} collective-permute-done((f32[2,264,128]{2,1,0:T(8,128)S(1)}, f32[2,264,128]{2,1,0:T(8,128)S(1)}, u32[]{:S(2)}, u32[]{:S(2)}) %collective-permute-start.5) | collective-permute-done | bytes 270368 | tf_op jit(solution)/shard_map/ppermute | solution.py:207
  80.6 3.4 %collective-permute-start.6 = (f32[1,264,128]{2,1,0:T(8,128)S(1)}, f32[1,264,128]{2,1,0:T(8,128)S(1)}, u32[]{:S(2)}, u32[]{:S(2)}) collective-permute-start(f32[1,264,128]{2,1,0:T(8,128)S(1)} %get-tuple-element.27), channel_id=1, source_target_pairs={{0,4},{1,5},{2,6},{3,7},{4,0},{5,1},{6,2},{7,3},{8,12},{9,13},{10,... | collective-permute-start | bytes 405512 | tf_op jit(solution)/shard_map/ppermute | solution.py:207
  83.9 4.4 %collective-permute-done.6.arrived = f32[1,264,128]{2,1,0:T(8,128)S(1)} collective-permute-done((f32[1,264,128]{2,1,0:T(8,128)S(1)}, f32[1,264,128]{2,1,0:T(8,128)S(1)}, u32[]{:S(2)}, u32[]{:S(2)}) %collective-permute-start.6) | collective-permute-done | bytes 135200 | tf_op jit(solution)/shard_map/ppermute | solution.py:207
  88.4 0.8 finish.1
  (2 shorter events, 0.0 us)
Async XLA Ops:
  0.6 2.2 %copy-start = (f32[4096,256]{1,0:T(8,128)S(1)}, f32[4096,256]{1,0:T(8,128)}, u32[]{:S(2)}) copy-start(f32[4096,256]{1,0:T(8,128)} %param.3) | copy-start | bytes 12582916
  2.8 0.7 copy-start.1
  3.5 0.7 copy-start.2
  43.5 4.4 %collective-permute-start = (f32[16,264,128]{2,1,0:T(8,128)S(1)}, f32[16,264,128]{2,1,0:T(8,128)S(1)}, u32[]{:S(2)}, u32[]{:S(2)}) collective-permute-start(f32[16,264,128]{2,1,0:T(8,128)S(1)} %get-tuple-element.17), channel_id=1, source_target_pairs={{0,8},{1,9},{2,10},{3,11},{4,12},{5,13},{6,14},{7,15},{8,0},{9,1},... | collective-permute-start | bytes 6488072 | tf_op jit(solution)/shard_map/ppermute | solution.py:207
  48.2 15.5 %collective-permute-start.1 = (f32[4,264,128]{2,1,0:T(8,128)S(1)}, f32[4,264,128]{2,1,0:T(8,128)S(1)}, u32[]{:S(2)}, u32[]{:S(2)}) collective-permute-start(f32[4,264,128]{2,1,0:T(8,128)S(1)} %get-tuple-element.19), channel_id=1, source_target_pairs={{0,16},{1,17},{2,18},{3,19},{4,20},{5,21},{6,22},{7,23},{8,24},{9,... | collective-permute-start | bytes 1622024 | tf_op jit(solution)/shard_map/ppermute | solution.py:207
  51.1 14.0 %collective-permute-start.2 = (f32[4,264,128]{2,1,0:T(8,128)S(1)}, f32[4,264,128]{2,1,0:T(8,128)S(1)}, u32[]{:S(2)}, u32[]{:S(2)}) collective-permute-start(f32[4,264,128]{2,1,0:T(8,128)S(1)} %get-tuple-element.20), channel_id=1, source_target_pairs={{0,1},{1,0},{2,3},{3,2},{4,5},{5,4},{6,7},{7,6},{8,9},{9,8},{10,11... | collective-permute-start | bytes 1622024 | tf_op jit(solution)/shard_map/ppermute | solution.py:207
  65.3 7.4 %collective-permute-start.3 = (f32[2,264,128]{2,1,0:T(8,128)S(1)}, f32[2,264,128]{2,1,0:T(8,128)S(1)}, u32[]{:S(2)}, u32[]{:S(2)}) collective-permute-start(f32[2,264,128]{2,1,0:T(8,128)S(1)} %get-tuple-element.22), channel_id=1, source_target_pairs={{0,1},{1,0},{2,3},{3,2},{4,5},{5,4},{6,7},{7,6},{8,9},{9,8},{10,11... | collective-permute-start | bytes 811016 | tf_op jit(solution)/shard_map/ppermute | solution.py:207
  66.8 7.1 %collective-permute-start.4 = (f32[2,264,128]{2,1,0:T(8,128)S(1)}, f32[2,264,128]{2,1,0:T(8,128)S(1)}, u32[]{:S(2)}, u32[]{:S(2)}) collective-permute-start(f32[2,264,128]{2,1,0:T(8,128)S(1)} %get-tuple-element.23), channel_id=1, source_target_pairs={{0,16},{1,17},{2,18},{3,19},{4,20},{5,21},{6,22},{7,23},{8,24},{9,... | collective-permute-start | bytes 811016 | tf_op jit(solution)/shard_map/ppermute | solution.py:207
  74.0 6.5 %collective-permute-start.5 = (f32[2,264,128]{2,1,0:T(8,128)S(1)}, f32[2,264,128]{2,1,0:T(8,128)S(1)}, u32[]{:S(2)}, u32[]{:S(2)}) collective-permute-start(f32[2,264,128]{2,1,0:T(8,128)S(1)} %get-tuple-element.25), channel_id=1, source_target_pairs={{0,2},{1,3},{2,0},{3,1},{4,6},{5,7},{6,4},{7,5},{8,10},{9,11},{10,... | collective-permute-start | bytes 811016 | tf_op jit(solution)/shard_map/ppermute | solution.py:207
  80.6 7.8 %collective-permute-start.6 = (f32[1,264,128]{2,1,0:T(8,128)S(1)}, f32[1,264,128]{2,1,0:T(8,128)S(1)}, u32[]{:S(2)}, u32[]{:S(2)}) collective-permute-start(f32[1,264,128]{2,1,0:T(8,128)S(1)} %get-tuple-element.27), channel_id=1, source_target_pairs={{0,4},{1,5},{2,6},{3,7},{4,0},{5,1},{6,2},{7,3},{8,12},{9,13},{10,... | collective-permute-start | bytes 405512 | tf_op jit(solution)/shard_map/ppermute | solution.py:207

commit v2 on v0

v2 whole, which is shorter than its diff:
```python
import functools

import jax
import jax.numpy as jnp
from jax import lax
from jax.experimental import pallas as pl
from jax.experimental.pallas import tpu as pltpu
from jax.sharding import PartitionSpec as P

KEYS = 4096
LANES = 128
SUB = 8
TABLES = 4
AXES = ("dom", "rep")
VMEM = pl.BlockSpec(memory_space=pltpu.VMEM)


def bits_of(size):
    return [b for b in range(size.bit_length() - 1)]


class Plan:
    def __init__(self, n_dom, n_rep, rows, width):
        self.devices = n_dom * n_rep
        self.block = KEYS // self.devices
        self.span = KEYS // n_dom
        self.tiles = width // LANES
        self.rows = rows
        self.group = SUB * (self.tiles + 1)
        self.groups = self.block // SUB
        self.part = self.block * self.tiles
        self.unit = self.part + SUB
        rep = bits_of(n_rep)
        dom = [len(rep) + b for b in bits_of(n_dom)]
        self.core, self.second, self.third, *self.middle, self.last = dom + rep
        self.even = [self.core, self.last, self.second, self.third, *self.middle]
        self.odd = [self.core, self.last, self.third, self.second, *self.middle]
        self.chunk = self.devices // 4

    def virtual(self, place, order):
        out = jnp.zeros_like(place)
        for at, bit in enumerate(reversed(order)):
            out = out | (((place >> bit) & 1) << at)
        return out

    def pairs(self, even_bit, odd_bit):
        odd = 1 << self.core
        return [
            (i, i ^ (1 << (odd_bit if i & odd else even_bit))) for i in range(self.devices)
        ]


def sum_block(plan, tables, base, out, at, arrived):
    row = lax.broadcasted_iota(jnp.int32, (SUB, LANES), 0)
    lane = lax.broadcasted_iota(jnp.int32, (SUB, LANES), 1)
    first = pl.multiple_of(base * (plan.groups * plan.group), SUB)
    counts = jnp.zeros((SUB, LANES), jnp.float32)
    for g in range(plan.groups):
        for t in range(plan.tiles + 1):
            d = pl.ds(first + g * plan.group + t * SUB, SUB)
            total = tables[0][d, :]
            for table in tables[1:]:
                total = total + table[d, :]
            if t == plan.tiles:
                counts = jnp.where(lane == row + g * SUB, total, counts)
                continue
            to = pl.ds((g * plan.tiles + t) * SUB, SUB)
            for ref, where in arrived:
                total = total + ref[where, to, :]
            out[at, to, :] = total
    to = pl.ds(plan.part, SUB)
    total = jnp.broadcast_to(jnp.sum(counts, axis=0, keepdims=True), (SUB, LANES))
    for ref, where in arrived:
        total = total + ref[where, to, :]
    out[at, to, :] = total


def table_kernel(plan, me_ref, owner, offset, facts, sent, *rest):
    tables = rest[:TABLES]
    buf, owner_v, offset_v, addr_v, addr_s, same_v, same_s, sem, small = rest[TABLES:]
    n = plan.rows // LANES
    half = n // 2
    per = LANES // SUB
    wide = plan.tiles * SUB

    def fetch(i):
        d = pl.ds(i * per, per)
        return pltpu.make_async_copy(facts.at[d], buf.at[d, pl.ds(0, wide)], sem.at[i])

    copies = [
        pltpu.make_async_copy(owner, owner_v, small.at[0]),
        pltpu.make_async_copy(offset, offset_v, small.at[1]),
    ]
    for copy in copies:
        copy.start()
    for i in range(half):
        fetch(i).start()
        fetch(half + i).start()

    def zero(refs):
        step = SUB * SUB

        def body(i, _):
            for t in refs:
                t[pl.ds(pl.multiple_of(i * step, step), step), :] = jnp.zeros(
                    (step, LANES), jnp.float32
                )
            return 0

        lax.fori_loop(0, refs[0].shape[0] // step, body, 0)

    zero(tables[: TABLES // 2])
    for copy in copies:
        copy.wait()
    me = me_ref[0]
    key = owner_v[...] * plan.span + offset_v[...]
    shift = plan.block.bit_length() - 1
    owner_core = (key >> (shift + plan.core)) & 1
    place = (key >> shift) ^ me
    place = jnp.where(
        owner_core == 1, plan.virtual(place, plan.odd), plan.virtual(place, plan.even)
    )
    key = (place << shift) | (key & (plan.block - 1))
    addr = (key >> 3) * plan.group + (key & (SUB - 1))
    addr_v[...] = addr
    same_v[...] = jnp.where(addr[:half] == addr[half:], 1.0, 0.0)
    copies = [
        pltpu.make_async_copy(addr_v, addr_s, small.at[2]),
        pltpu.make_async_copy(same_v, same_s, small.at[3]),
    ]
    for copy in copies:
        copy.start()
    zero(tables[TABLES // 2 :])

    def ones(i, _):
        for j in range(per):
            buf[i * per + j, pl.ds(wide, SUB), :] = jnp.ones((SUB, LANES), jnp.float32)
        return 0

    lax.fori_loop(0, n, ones, 0)
    for copy in copies:
        copy.wait()

    def add_rows(i, _):
        fetch(i).wait()
        fetch(half + i).wait()
        for j in range(LANES):
            table = tables[j % TABLES]
            one = pl.ds(addr_s[i, j], plan.tiles + 1, stride=SUB)
            two = pl.ds(addr_s[half + i, j], plan.tiles + 1, stride=SUB)
            lines = pl.ds(j % SUB, plan.tiles + 1, stride=SUB)
            row_one = buf[i * per + j // SUB, lines, :]
            row_two = buf[(half + i) * per + j // SUB, lines, :]
            old_one = table[one, :]
            old_two = table[two, :]
            table[one, :] = old_one + row_one
            table[two, :] = old_two + (row_two + same_s[i, j] * row_one)
        return 0

    lax.fori_loop(0, half, add_rows, 0)

    def send(i, _):
        sum_block(plan, tables, 3 * plan.chunk + i, sent, i, ())
        return 0

    lax.fori_loop(0, plan.chunk, send, 0)


def make_table(plan, me, owner, offset, facts):
    rows = plan.rows
    view = facts.reshape(rows // SUB, SUB, plan.tiles, LANES).transpose(0, 2, 1, 3)
    view = view.reshape(rows // SUB, plan.tiles * SUB, LANES)
    lanes = (rows // LANES, LANES)
    half = (rows // LANES // 2, LANES)
    far = [
        pltpu.with_memory_space_constraint(x, pltpu.HBM)
        for x in (owner.reshape(lanes), offset.reshape(lanes), view)
    ]
    hbm = pl.BlockSpec(memory_space=pltpu.HBM)
    table = jax.ShapeDtypeStruct((KEYS // SUB * plan.group, LANES), jnp.float32)
    return pl.pallas_call(
        functools.partial(table_kernel, plan),
        out_shape=[jax.ShapeDtypeStruct((plan.chunk, plan.unit, LANES), jnp.float32)]
        + [table] * TABLES,
        in_specs=[pl.BlockSpec(memory_space=pltpu.SMEM), hbm, hbm, hbm],
        out_specs=[VMEM] * (1 + TABLES),
        scratch_shapes=[
            pltpu.VMEM((rows // SUB, plan.group, LANES), jnp.float32),
            pltpu.VMEM(lanes, jnp.int32),
            pltpu.VMEM(lanes, jnp.int32),
            pltpu.VMEM(lanes, jnp.int32),
            pltpu.SMEM(lanes, jnp.int32),
            pltpu.VMEM(half, jnp.float32),
            pltpu.SMEM(half, jnp.float32),
            pltpu.SemaphoreType.DMA((rows // LANES,)),
            pltpu.SemaphoreType.DMA((4,)),
        ],
        compiler_params=pltpu.CompilerParams(vmem_limit_bytes=12 << 20),
        name="make_table",
    )(me, *far)


def send_kernel(plan, base, first, n_got, *refs):
    tables, got, out = refs[:TABLES], refs[TABLES : TABLES + n_got], refs[-1]

    def body(i, _):
        sum_block(plan, tables, base + first + i, out, i, [(g, first + i) for g in got])
        return 0

    lax.fori_loop(0, out.shape[0], body, 0)


def send_blocks(plan, tables, got, base, first, count):
    n = len(tables) + len(got)
    return pl.pallas_call(
        functools.partial(send_kernel, plan, base, first, len(got)),
        out_shape=jax.ShapeDtypeStruct((count, plan.unit, LANES), jnp.float32),
        in_specs=[VMEM] * n,
        out_specs=VMEM,
        compiler_params=pltpu.CompilerParams(vmem_limit_bytes=4 << 20),
        name="send_blocks",
    )(*tables, *got)


def finish_kernel(plan, n_got, *refs):
    tables, got = refs[:TABLES], refs[TABLES : TABLES + n_got]
    means, counts, total = refs[TABLES + n_got :]
    sum_block(plan, tables, 0, total, 0, [(g, 0) for g in got])
    row = total[0, pl.ds(plan.part, 1), :]
    counts[...] = row[:, : plan.block]
    shape = (plan.block, LANES)
    diagonal = lax.broadcasted_iota(jnp.int32, shape, 0) == lax.broadcasted_iota(
        jnp.int32, shape, 1
    )
    column = jnp.sum(jnp.where(diagonal, row, 0.0), axis=1, keepdims=True)
    column = jnp.maximum(column, 1.0)
    for g in range(plan.groups):
        for t in range(plan.tiles):
            means[g * SUB : (g + 1) * SUB, t * LANES : (t + 1) * LANES] = (
                total[0, pl.ds((g * plan.tiles + t) * SUB, SUB), :]
                / column[g * SUB : (g + 1) * SUB, :]
            )


def finish(plan, tables, got):
    means, counts = pl.pallas_call(
        functools.partial(finish_kernel, plan, len(got)),
        out_shape=[
            jax.ShapeDtypeStruct((plan.block, plan.tiles * LANES), jnp.float32),
            jax.ShapeDtypeStruct((1, plan.block), jnp.float32),
        ],
        in_specs=[VMEM] * (len(tables) + len(got)),
        out_specs=[VMEM] * 2,
        scratch_shapes=[pltpu.VMEM((1, plan.unit, LANES), jnp.float32)],
        compiler_params=pltpu.CompilerParams(vmem_limit_bytes=4 << 20),
        name="finish",
    )(*tables, *got)
    return means, counts.reshape(plan.block)


def per_device(facts, row_owner, key_offset):
    n_dom, n_rep = lax.axis_size("dom"), lax.axis_size("rep")
    plan = Plan(n_dom, n_rep, *facts.shape)
    me = (lax.axis_index("dom") * n_rep + lax.axis_index("rep")).astype(jnp.int32).reshape(1)

    def swap(x, even_bit, odd_bit=None):
        odd_bit = even_bit if odd_bit is None else odd_bit
        return lax.ppermute(x, AXES, plan.pairs(even_bit, odd_bit))

    sent, *tables = make_table(plan, me, row_owner[:, 0], key_offset, facts)
    chunk = plan.chunk
    got_q = [swap(sent, plan.core)]
    got_p = [swap(send_blocks(plan, tables, [], 2 * chunk, 0, chunk), plan.core)]
    stages = [(plan.second, plan.third), (plan.third, plan.second)]
    stages += [(bit, bit) for bit in plan.middle]
    size = chunk
    for stage in stages:
        size //= 2
        for got, base in ((got_q, chunk), (got_p, 0)):
            got.append(swap(send_blocks(plan, tables, got, base, size, size), *stage))
    got_p.append(swap(send_blocks(plan, tables, got_q, chunk, 0, 1), plan.last))
    return finish(plan, tables, got_p)


def solution(mesh):
    placed = (P(AXES, None), P(AXES, None), P(AXES))
    return jax.shard_map(
        per_device,
        mesh=mesh,
        in_specs=placed,
        out_specs=(P(AXES, None), P(AXES)),
        check_vma=False,
    )
```

time: 270 us -> 49 us (0.18)
  local copies, waits for them, and re-layouts: 107 us -> 0 us
  waiting for transfers between devices: 80.7 us -> 21.5 us
  blocking collectives: 31.8 us -> 0 us
  other arithmetic: 18.7 us -> 0 us
  starting transfers between devices: 0.08 us -> 15.4 us
  between operations: 15.5 us -> 0.66 us
  matrix products: 14.3 us -> 0 us
  Pallas kernels: 0 us -> 11.3 us
    reduce_scatter x2 -> x0, waiting for transfers between devices: 80.7 us -> none  [the longest x1 47.4 us: per_device(): lax.psum_scatter(local_sums, 'dom', scatter_dimension=0, tiled=True)]
    gather x2 -> x0, local copies, waits for them, and re-layouts: 79.1 us -> none  [the longest x1 45.5 us: per_device(): offsets = jnp.take(key_offset, source, axis=0, mode='fill', fill_value=-1)]
    unnamed x2 -> x0, blocking collectives: 31.8 us -> none
    ppermute x0 -> x9, waiting for transfers between devices: none -> 21.5 us  [swap(): return lax.ppermute(x, AXES, plan.pairs(even_bit, odd_bit))]
    scatter x1 -> x0, local copies, waits for them, and re-layouts: 15.5 us -> none  [bucket_rows(): empty.at[position]]
    ppermute x0 -> x9, starting transfers between devices: none -> 15.4 us  [swap(): return lax.ppermute(x, AXES, plan.pairs(even_bit, odd_bit))]
    dot_general x4 -> x0, matrix products: 14.3 us -> none  [the longest x2 9.42 us: block_table(): jnp.einsum('grk,grm->gkm', onehot, low_part, preferred_element_type=jnp.f...]
    pallas_call x0 -> x10, Pallas kernels: none -> 11.3 us  [the longest x1 8.78 us: make_table(): pl.pallas_call(functools.partial(table_kernel, plan), out_shape=[jax.Shap...]
  transfers between devices with their start and end apart: 2 -> 9, of which waited for: 2 -> 6; matrix products, arithmetic and copies ran while one was open for 1% -> 0% of each run, Pallas kernels for 0% -> 4%
where the time goes in v2:
time: 49 us; the launch traced here: 48.8 us
  waiting for transfers between devices  21.5 us (44%)
  starting transfers between devices  15.4 us (31%)
  Pallas kernels  11.3 us (23%)
  between operations  0.66 us (1%)
    ppermute x9, waiting for transfers between devices, swap(): return lax.ppermute(x, AXES, plan.pairs(even_bit, odd_bit))  21.5 us
    ppermute x9, starting transfers between devices, swap(): return lax.ppermute(x, AXES, plan.pairs(even_bit, odd_bit))  15.4 us
    pallas_call x1, Pallas kernels, make_table(): pl.pallas_call(functools.partial(table_kernel, plan), out_shape=[jax.Shap...  8.78 us
    pallas_call x8, Pallas kernels, send_blocks(): pl.pallas_call(functools.partial(send_kernel, plan, base, first, len(got)...  1.72 us
  transfers between devices with their start and end apart: 9, of which 6 were waited for; matrix products, arithmetic and copies ran while one was open for 0% of the time, Pallas kernels for 4%

profile of v2, /device:TPU:0, one launch (start us, length us, event | category | flops | bytes accessed | tf_op | source)
XLA Modules:
  0.0 48.8 jit_solution(3368403172667622312)
XLA Ops:
  0.6 8.8 %make_table.1 = (f32[8,264,128]{2,1,0:T(8,128)S(1)}, f32[12288,128]{1,0:T(8,128)S(1)}, f32[12288,128]{1,0:T(8,128)S(1)}, f32[12288,128]{1,0:T(8,128)S(1)}, f32[12288,128]{1,0:T(8,128)S(1)}) custom-call(s32[1]{0:T(128)} %bitcast.me_ref, s32[32,128]{1,0:T(8,128)} %bitcast.10, s32[32,128]{1,0:T(8,128)} %bitcast.11, f32[512,16,128]{2,1,0:T(8,128)} %bitcast.9), custom_call_target="tpu_custom_call" | custom-call | tf_op jit(solution)/shard_map/make_table/pallas_call | solution.py:181
  9.4 0.6 %collective-permute-start.4 = (f32[8,264,128]{2,1,0:T(8,128)S(1)}, f32[8,264,128]{2,1,0:T(8,128)S(1)}, u32[]{:S(2)}, u32[]{:S(2)}) collective-permute-start(f32[8,264,128]{2,1,0:T(8,128)S(1)} %get-tuple-element.13), channel_id=1, source_target_pairs={{0,8},{1,9},{2,10},{3,11},{4,12},{5,13},{6,14},{7,15},{8,0},{9,1},... | collective-permute-start | bytes 3244040 | tf_op jit(solution)/shard_map/ppermute | solution.py:268
  10.0 0.5 %send_blocks.8 = f32[8,264,128]{2,1,0:T(8,128)S(1)} custom-call(f32[12288,128]{1,0:T(8,128)S(1)} %get-tuple-element.9.refs_0_, f32[12288,128]{1,0:T(8,128)S(1)} %get-tuple-element.10.refs_1_, f32[12288,128]{1,0:T(8,128)S(1)} %get-tuple-element.11.refs_2_, f32[12288,128]{1,0:T(8,128)S(1)} %get-tuple-element.12.refs_3_), custom_call_target="tpu_custom_call" | custom-call | tf_op jit(solution)/shard_map/send_blocks/pallas_call | solution.py:215
  10.6 1.7 %collective-permute-done.4.refs_4_ = f32[8,264,128]{2,1,0:T(8,128)S(1)} collective-permute-done((f32[8,264,128]{2,1,0:T(8,128)S(1)}, f32[8,264,128]{2,1,0:T(8,128)S(1)}, u32[]{:S(2)}, u32[]{:S(2)}) %collective-permute-start.4) | collective-permute-done | bytes 1081376 | tf_op jit(solution)/shard_map/ppermute | solution.py:268
  12.3 0.3 send_blocks.12
  12.6 2.9 %collective-permute-start.5 = (f32[4,264,128]{2,1,0:T(8,128)S(1)}, f32[4,264,128]{2,1,0:T(8,128)S(1)}, u32[]{:S(2)}, u32[]{:S(2)}) collective-permute-start(f32[4,264,128]{2,1,0:T(8,128)S(1)} %send_blocks.12), channel_id=1, source_target_pairs={{0,16},{1,17},{2,18},{3,19},{4,20},{5,21},{6,22},{7,23},{8,9},{9,8... | collective-permute-start | bytes 1622024 | tf_op jit(solution)/shard_map/ppermute | solution.py:268
  15.6 0.3 send_blocks.9
  15.8 1.3 %collective-permute-start.1 = (f32[4,264,128]{2,1,0:T(8,128)S(1)}, f32[4,264,128]{2,1,0:T(8,128)S(1)}, u32[]{:S(2)}, u32[]{:S(2)}) collective-permute-start(f32[4,264,128]{2,1,0:T(8,128)S(1)} %send_blocks.9), channel_id=1, source_target_pairs={{0,16},{1,17},{2,18},{3,19},{4,20},{5,21},{6,22},{7,23},{8,9},{9,8... | collective-permute-start | bytes 1622024 | tf_op jit(solution)/shard_map/ppermute | solution.py:268
  17.1 5.8 %collective-permute-done.5.refs_5_ = f32[4,264,128]{2,1,0:T(8,128)S(1)} collective-permute-done((f32[4,264,128]{2,1,0:T(8,128)S(1)}, f32[4,264,128]{2,1,0:T(8,128)S(1)}, u32[]{:S(2)}, u32[]{:S(2)}) %collective-permute-start.5) | collective-permute-done | bytes 540704 | tf_op jit(solution)/shard_map/ppermute | solution.py:268
  22.9 0.2 send_blocks.13
  23.1 2.1 %collective-permute-start.6 = (f32[2,264,128]{2,1,0:T(8,128)S(1)}, f32[2,264,128]{2,1,0:T(8,128)S(1)}, u32[]{:S(2)}, u32[]{:S(2)}) collective-permute-start(f32[2,264,128]{2,1,0:T(8,128)S(1)} %send_blocks.13), channel_id=1, source_target_pairs={{0,1},{1,0},{2,3},{3,2},{4,5},{5,4},{6,7},{7,6},{8,24},{9,25},{10,... | collective-permute-start | bytes 811016 | tf_op jit(solution)/shard_map/ppermute | solution.py:268
  25.1 6.5 %collective-permute-done.1.refs_5_ = f32[4,264,128]{2,1,0:T(8,128)S(1)} collective-permute-done((f32[4,264,128]{2,1,0:T(8,128)S(1)}, f32[4,264,128]{2,1,0:T(8,128)S(1)}, u32[]{:S(2)}, u32[]{:S(2)}) %collective-permute-start.1) | collective-permute-done | bytes 540704 | tf_op jit(solution)/shard_map/ppermute | solution.py:268
  31.6 0.2 send_blocks.10
  31.7 2.1 %collective-permute-start.2 = (f32[2,264,128]{2,1,0:T(8,128)S(1)}, f32[2,264,128]{2,1,0:T(8,128)S(1)}, u32[]{:S(2)}, u32[]{:S(2)}) collective-permute-start(f32[2,264,128]{2,1,0:T(8,128)S(1)} %send_blocks.10), channel_id=1, source_target_pairs={{0,1},{1,0},{2,3},{3,2},{4,5},{5,4},{6,7},{7,6},{8,24},{9,25},{10,... | collective-permute-start | bytes 811016 | tf_op jit(solution)/shard_map/ppermute | solution.py:268
  33.8 0.1 send_blocks.14
  33.9 1.6 %collective-permute-start.7 = (f32[1,264,128]{2,1,0:T(8,128)S(1)}, f32[1,264,128]{2,1,0:T(8,128)S(1)}, u32[]{:S(2)}, u32[]{:S(2)}) collective-permute-start(f32[1,264,128]{2,1,0:T(8,128)S(1)} %send_blocks.14), channel_id=1, source_target_pairs={{0,2},{1,3},{2,0},{3,1},{4,6},{5,7},{6,4},{7,5},{8,10},{9,11},{10,... | collective-permute-start | bytes 405512 | tf_op jit(solution)/shard_map/ppermute | solution.py:268
  35.5 2.7 %collective-permute-done.2.refs_6_ = f32[2,264,128]{2,1,0:T(8,128)S(1)} collective-permute-done((f32[2,264,128]{2,1,0:T(8,128)S(1)}, f32[2,264,128]{2,1,0:T(8,128)S(1)}, u32[]{:S(2)}, u32[]{:S(2)}) %collective-permute-start.2) | collective-permute-done | bytes 270368 | tf_op jit(solution)/shard_map/ppermute | solution.py:268
  38.3 0.1 send_blocks.11
  38.4 2.1 %collective-permute-start.3 = (f32[1,264,128]{2,1,0:T(8,128)S(1)}, f32[1,264,128]{2,1,0:T(8,128)S(1)}, u32[]{:S(2)}, u32[]{:S(2)}) collective-permute-start(f32[1,264,128]{2,1,0:T(8,128)S(1)} %send_blocks.11), channel_id=1, source_target_pairs={{0,2},{1,3},{2,0},{3,1},{4,6},{5,7},{6,4},{7,5},{8,10},{9,11},{10,... | collective-permute-start | bytes 405512 | tf_op jit(solution)/shard_map/ppermute | solution.py:268
  40.5 0.1 send_blocks.15
  40.6 2.7 %collective-permute-start.8 = (f32[1,264,128]{2,1,0:T(8,128)S(1)}, f32[1,264,128]{2,1,0:T(8,128)S(1)}, u32[]{:S(2)}, u32[]{:S(2)}) collective-permute-start(f32[1,264,128]{2,1,0:T(8,128)S(1)} %send_blocks.15), channel_id=1, source_target_pairs={{0,4},{1,5},{2,6},{3,7},{4,0},{5,1},{6,2},{7,3},{8,12},{9,13},{10,... | collective-permute-start | bytes 405512 | tf_op jit(solution)/shard_map/ppermute | solution.py:268
  43.3 0.2 collective-permute-done.3.refs_7_
  43.5 4.5 %collective-permute-done.8.refs_8_ = f32[1,264,128]{2,1,0:T(8,128)S(1)} collective-permute-done((f32[1,264,128]{2,1,0:T(8,128)S(1)}, f32[1,264,128]{2,1,0:T(8,128)S(1)}, u32[]{:S(2)}, u32[]{:S(2)}) %collective-permute-start.8) | collective-permute-done | bytes 135200 | tf_op jit(solution)/shard_map/ppermute | solution.py:268
  48.0 0.8 %finish.1 = (f32[128,256]{1,0:T(8,128)}, f32[1,128]{1,0:T(1,128)}) custom-call(f32[12288,128]{1,0:T(8,128)S(1)} %get-tuple-element.9.refs_0_, f32[12288,128]{1,0:T(8,128)S(1)} %get-tuple-element.10.refs_1_, f32[12288,128]{1,0:T(8,128)S(1)} %get-tuple-element.11.refs_2_, f32[12288,128]{1,0:T(8,128)S(1)} %get-tuple-element.12.refs_3_, ...), custom_call_target="tpu_custom_call" | custom-call | tf_op jit(solution)/shard_map/finish/pallas_call | solution.py:246
  (4 shorter events, 0.1 us)
Async XLA Ops:
  9.4 2.9 %collective-permute-start.4 = (f32[8,264,128]{2,1,0:T(8,128)S(1)}, f32[8,264,128]{2,1,0:T(8,128)S(1)}, u32[]{:S(2)}, u32[]{:S(2)}) collective-permute-start(f32[8,264,128]{2,1,0:T(8,128)S(1)} %get-tuple-element.13), channel_id=1, source_target_pairs={{0,8},{1,9},{2,10},{3,11},{4,12},{5,13},{6,14},{7,15},{8,0},{9,1},... | collective-permute-start | bytes 3244040 | tf_op jit(solution)/shard_map/ppermute | solution.py:268
  10.5 5.0 %collective-permute-start = (f32[8,264,128]{2,1,0:T(8,128)S(1)}, f32[8,264,128]{2,1,0:T(8,128)S(1)}, u32[]{:S(2)}, u32[]{:S(2)}) collective-permute-start(f32[8,264,128]{2,1,0:T(8,128)S(1)} %send_blocks.8), channel_id=1, source_target_pairs={{0,8},{1,9},{2,10},{3,11},{4,12},{5,13},{6,14},{7,15},{8,0},{9,1},... | collective-permute-start | bytes 3244040 | tf_op jit(solution)/shard_map/ppermute | solution.py:268
  12.6 10.3 %collective-permute-start.5 = (f32[4,264,128]{2,1,0:T(8,128)S(1)}, f32[4,264,128]{2,1,0:T(8,128)S(1)}, u32[]{:S(2)}, u32[]{:S(2)}) collective-permute-start(f32[4,264,128]{2,1,0:T(8,128)S(1)} %send_blocks.12), channel_id=1, source_target_pairs={{0,16},{1,17},{2,18},{3,19},{4,20},{5,21},{6,22},{7,23},{8,9},{9,8... | collective-permute-start | bytes 1622024 | tf_op jit(solution)/shard_map/ppermute | solution.py:268
  15.8 15.7 %collective-permute-start.1 = (f32[4,264,128]{2,1,0:T(8,128)S(1)}, f32[4,264,128]{2,1,0:T(8,128)S(1)}, u32[]{:S(2)}, u32[]{:S(2)}) collective-permute-start(f32[4,264,128]{2,1,0:T(8,128)S(1)} %send_blocks.9), channel_id=1, source_target_pairs={{0,16},{1,17},{2,18},{3,19},{4,20},{5,21},{6,22},{7,23},{8,9},{9,8... | collective-permute-start | bytes 1622024 | tf_op jit(solution)/shard_map/ppermute | solution.py:268
  23.1 10.7 %collective-permute-start.6 = (f32[2,264,128]{2,1,0:T(8,128)S(1)}, f32[2,264,128]{2,1,0:T(8,128)S(1)}, u32[]{:S(2)}, u32[]{:S(2)}) collective-permute-start(f32[2,264,128]{2,1,0:T(8,128)S(1)} %send_blocks.13), channel_id=1, source_target_pairs={{0,1},{1,0},{2,3},{3,2},{4,5},{5,4},{6,7},{7,6},{8,24},{9,25},{10,... | collective-permute-start | bytes 811016 | tf_op jit(solution)/shard_map/ppermute | solution.py:268
  31.7 6.5 %collective-permute-start.2 = (f32[2,264,128]{2,1,0:T(8,128)S(1)}, f32[2,264,128]{2,1,0:T(8,128)S(1)}, u32[]{:S(2)}, u32[]{:S(2)}) collective-permute-start(f32[2,264,128]{2,1,0:T(8,128)S(1)} %send_blocks.10), channel_id=1, source_target_pairs={{0,1},{1,0},{2,3},{3,2},{4,5},{5,4},{6,7},{7,6},{8,24},{9,25},{10,... | collective-permute-start | bytes 811016 | tf_op jit(solution)/shard_map/ppermute | solution.py:268
  33.9 6.6 %collective-permute-start.7 = (f32[1,264,128]{2,1,0:T(8,128)S(1)}, f32[1,264,128]{2,1,0:T(8,128)S(1)}, u32[]{:S(2)}, u32[]{:S(2)}) collective-permute-start(f32[1,264,128]{2,1,0:T(8,128)S(1)} %send_blocks.14), channel_id=1, source_target_pairs={{0,2},{1,3},{2,0},{3,1},{4,6},{5,7},{6,4},{7,5},{8,10},{9,11},{10,... | collective-permute-start | bytes 405512 | tf_op jit(solution)/shard_map/ppermute | solution.py:268
  38.4 5.1 %collective-permute-start.3 = (f32[1,264,128]{2,1,0:T(8,128)S(1)}, f32[1,264,128]{2,1,0:T(8,128)S(1)}, u32[]{:S(2)}, u32[]{:S(2)}) collective-permute-start(f32[1,264,128]{2,1,0:T(8,128)S(1)} %send_blocks.11), channel_id=1, source_target_pairs={{0,2},{1,3},{2,0},{3,1},{4,6},{5,7},{6,4},{7,5},{8,10},{9,11},{10,... | collective-permute-start | bytes 405512 | tf_op jit(solution)/shard_map/ppermute | solution.py:268
  40.6 7.4 %collective-permute-start.8 = (f32[1,264,128]{2,1,0:T(8,128)S(1)}, f32[1,264,128]{2,1,0:T(8,128)S(1)}, u32[]{:S(2)}, u32[]{:S(2)}) collective-permute-start(f32[1,264,128]{2,1,0:T(8,128)S(1)} %send_blocks.15), channel_id=1, source_target_pairs={{0,4},{1,5},{2,6},{3,7},{4,0},{5,1},{6,2},{7,3},{8,12},{9,13},{10,... | collective-permute-start | bytes 405512 | tf_op jit(solution)/shard_map/ppermute | solution.py:268

commit v3 on v2

--- a/solution.py
+++ b/solution.py
@@ -32,10 +32,11 @@
         self.unit = self.part + SUB
         rep = bits_of(n_rep)
         dom = [len(rep) + b for b in bits_of(n_dom)]
-        self.core, self.second, self.third, *self.middle, self.last = dom + rep
-        self.even = [self.core, self.last, self.second, self.third, *self.middle]
-        self.odd = [self.core, self.last, self.third, self.second, *self.middle]
-        self.chunk = self.devices // 4
+        self.core, self.second, self.third, self.near, *self.middle, self.far = dom + rep
+        head = [self.core, self.far, self.near]
+        self.even = [*head, self.second, self.third, *self.middle]
+        self.odd = [*head, self.third, self.second, *self.middle]
+        self.chunk = self.devices // 8
 
     def virtual(self, place, order):
         out = jnp.zeros_like(place)
@@ -75,7 +76,7 @@
     out[at, to, :] = total
 
 
-def table_kernel(plan, me_ref, owner, offset, facts, sent, *rest):
+def table_kernel(plan, n_rep, owner, offset, facts, sent, *rest):
     tables = rest[:TABLES]
     buf, owner_v, offset_v, addr_v, addr_s, same_v, same_s, sem, small = rest[TABLES:]
     n = plan.rows // LANES
@@ -112,7 +113,7 @@
     zero(tables[: TABLES // 2])
     for copy in copies:
         copy.wait()
-    me = me_ref[0]
+    me = lax.axis_index(AXES[0]) * n_rep + lax.axis_index(AXES[1])
     key = owner_v[...] * plan.span + offset_v[...]
     shift = plan.block.bit_length() - 1
     owner_core = (key >> (shift + plan.core)) & 1
@@ -160,13 +161,13 @@
     lax.fori_loop(0, half, add_rows, 0)
 
     def send(i, _):
-        sum_block(plan, tables, 3 * plan.chunk + i, sent, i, ())
+        sum_block(plan, tables, 7 * plan.chunk + i, sent, i, ())
         return 0
 
     lax.fori_loop(0, plan.chunk, send, 0)
 
 
-def make_table(plan, me, owner, offset, facts):
+def make_table(plan, n_rep, owner, offset, facts):
     rows = plan.rows
     view = facts.reshape(rows // SUB, SUB, plan.tiles, LANES).transpose(0, 2, 1, 3)
     view = view.reshape(rows // SUB, plan.tiles * SUB, LANES)
@@ -179,10 +180,10 @@
     hbm = pl.BlockSpec(memory_space=pltpu.HBM)
     table = jax.ShapeDtypeStruct((KEYS // SUB * plan.group, LANES), jnp.float32)
     return pl.pallas_call(
-        functools.partial(table_kernel, plan),
+        functools.partial(table_kernel, plan, n_rep),
         out_shape=[jax.ShapeDtypeStruct((plan.chunk, plan.unit, LANES), jnp.float32)]
         + [table] * TABLES,
-        in_specs=[pl.BlockSpec(memory_space=pltpu.SMEM), hbm, hbm, hbm],
+        in_specs=[hbm, hbm, hbm],
         out_specs=[VMEM] * (1 + TABLES),
         scratch_shapes=[
             pltpu.VMEM((rows // SUB, plan.group, LANES), jnp.float32),
@@ -197,7 +198,7 @@
         ],
         compiler_params=pltpu.CompilerParams(vmem_limit_bytes=12 << 20),
         name="make_table",
-    )(me, *far)
+    )(*far)
 
 
 def send_kernel(plan, base, first, n_got, *refs):
@@ -261,25 +262,29 @@
 def per_device(facts, row_owner, key_offset):
     n_dom, n_rep = lax.axis_size("dom"), lax.axis_size("rep")
     plan = Plan(n_dom, n_rep, *facts.shape)
-    me = (lax.axis_index("dom") * n_rep + lax.axis_index("rep")).astype(jnp.int32).reshape(1)
 
     def swap(x, even_bit, odd_bit=None):
         odd_bit = even_bit if odd_bit is None else odd_bit
         return lax.ppermute(x, AXES, plan.pairs(even_bit, odd_bit))
 
-    sent, *tables = make_table(plan, me, row_owner[:, 0], key_offset, facts)
-    chunk = plan.chunk
-    got_q = [swap(sent, plan.core)]
-    got_p = [swap(send_blocks(plan, tables, [], 2 * chunk, 0, chunk), plan.core)]
+    sent, *tables = make_table(plan, n_rep, row_owner[:, 0], key_offset, facts)
+    size = plan.chunk
+    got = [[] for _ in range(4)]
+    for c in reversed(range(4)):
+        if c < 3:
+            sent = send_blocks(plan, tables, [], (4 + c) * size, 0, size)
+        got[c].append(swap(sent, plan.core))
     stages = [(plan.second, plan.third), (plan.third, plan.second)]
     stages += [(bit, bit) for bit in plan.middle]
-    size = chunk
     for stage in stages:
         size //= 2
-        for got, base in ((got_q, chunk), (got_p, 0)):
-            got.append(swap(send_blocks(plan, tables, got, base, size, size), *stage))
-    got_p.append(swap(send_blocks(plan, tables, got_q, chunk, 0, 1), plan.last))
-    return finish(plan, tables, got_p)
+        for c in reversed(range(4)):
+            sent = send_blocks(plan, tables, got[c], c * plan.chunk, size, size)
+            got[c].append(swap(sent, *stage))
+    for c, to, bit in ((3, 2, plan.near), (1, 0, plan.near), (2, 0, plan.far)):
+        sent = send_blocks(plan, tables, got[c], c * plan.chunk, 0, 1)
+        got[to].append(swap(sent, bit))
+    return finish(plan, tables, got[0])
 
 
 def solution(mesh):

time: 49 us -> 44.4 us (0.906)
  waiting for transfers between devices: 21.5 us -> 10.8 us
  starting transfers between devices: 15.4 us -> 21.5 us
    ppermute x9 -> x15, waiting for transfers between devices: 21.5 us -> 10.8 us  [swap(): return lax.ppermute(x, AXES, plan.pairs(even_bit, odd_bit))]
    ppermute x9 -> x15, starting transfers between devices: 15.4 us -> 21.5 us  [swap(): return lax.ppermute(x, AXES, plan.pairs(even_bit, odd_bit))]
    pallas_call x8 -> x14, Pallas kernels: 1.72 us -> 1.72 us  [send_blocks(): pl.pallas_call(functools.partial(send_kernel, plan, base, first, len(got)...]
  transfers between devices with their start and end apart: 9 -> 15, of which waited for: 6 -> 7; matrix products, arithmetic and copies ran while one was open for 0% -> 0% of each run, Pallas kernels for 4% -> 4%
where the time goes in v3:
time: 44.4 us; the launch traced here: 44 us
  starting transfers between devices  21.5 us (48%)
  Pallas kernels  11 us (25%)
  waiting for transfers between devices  10.8 us (24%)
  between operations  0.67 us (2%)
    ppermute x15, starting transfers between devices, swap(): return lax.ppermute(x, AXES, plan.pairs(even_bit, odd_bit))  21.5 us
    ppermute x15, waiting for transfers between devices, swap(): return lax.ppermute(x, AXES, plan.pairs(even_bit, odd_bit))  10.8 us
    pallas_call x1, Pallas kernels, make_table(): pl.pallas_call(functools.partial(table_kernel, plan, n_rep), out_shape=[j...  8.49 us
    pallas_call x14, Pallas kernels, send_blocks(): pl.pallas_call(functools.partial(send_kernel, plan, base, first, len(got)...  1.72 us
  transfers between devices with their start and end apart: 15, of which 7 were waited for; matrix products, arithmetic and copies ran while one was open for 0% of the time, Pallas kernels for 4%

profile of v3, /device:TPU:0, one launch (start us, length us, event | category | flops | bytes accessed | tf_op | source)
XLA Modules:
  0.0 44.0 jit_solution(229651721335982989)
XLA Ops:
  0.6 8.5 %make_table.1 = (f32[4,264,128]{2,1,0:T(8,128)S(1)}, f32[12288,128]{1,0:T(8,128)S(1)}, f32[12288,128]{1,0:T(8,128)S(1)}, f32[12288,128]{1,0:T(8,128)S(1)}, f32[12288,128]{1,0:T(8,128)S(1)}) custom-call(s32[32,128]{1,0:T(8,128)} %bitcast.9, s32[32,128]{1,0:T(8,128)} %bitcast.10, f32[512,16,128]{2,1,0:T(8,128)} %bitcast.8), custom_call_target="tpu_custom_call" | custom-call | tf_op jit(solution)/shard_map/make_table/pallas_call | solution.py:182
  9.1 0.6 %collective-permute-start.10 = (f32[4,264,128]{2,1,0:T(8,128)S(1)}, f32[4,264,128]{2,1,0:T(8,128)S(1)}, u32[]{:S(2)}, u32[]{:S(2)}) collective-permute-start(f32[4,264,128]{2,1,0:T(8,128)S(1)} %get-tuple-element.13), channel_id=1, source_target_pairs={{0,8},{1,9},{2,10},{3,11},{4,12},{5,13},{6,14},{7,15},{8,0},{9,1},... | collective-permute-start | bytes 1622024 | tf_op jit(solution)/shard_map/ppermute | solution.py:268
  9.7 0.2 send_blocks.17
  10.0 0.2 send_blocks.21
  10.2 0.6 %collective-permute-start.7 = (f32[4,264,128]{2,1,0:T(8,128)S(1)}, f32[4,264,128]{2,1,0:T(8,128)S(1)}, u32[]{:S(2)}, u32[]{:S(2)}) collective-permute-start(f32[4,264,128]{2,1,0:T(8,128)S(1)} %send_blocks.21), channel_id=1, source_target_pairs={{0,8},{1,9},{2,10},{3,11},{4,12},{5,13},{6,14},{7,15},{8,0},{9,1},... | collective-permute-start | bytes 1622024 | tf_op jit(solution)/shard_map/ppermute | solution.py:268
  10.8 0.2 send_blocks.14
  11.4 2.9 %collective-permute-start.11 = (f32[2,264,128]{2,1,0:T(8,128)S(1)}, f32[2,264,128]{2,1,0:T(8,128)S(1)}, u32[]{:S(2)}, u32[]{:S(2)}) collective-permute-start(f32[2,264,128]{2,1,0:T(8,128)S(1)} %send_blocks.24), channel_id=1, source_target_pairs={{0,16},{1,17},{2,18},{3,19},{4,20},{5,21},{6,22},{7,23},{8,9},{9,8... | collective-permute-start | bytes 811016 | tf_op jit(solution)/shard_map/ppermute | solution.py:268
  14.5 0.6 %collective-permute-start.4 = (f32[2,264,128]{2,1,0:T(8,128)S(1)}, f32[2,264,128]{2,1,0:T(8,128)S(1)}, u32[]{:S(2)}, u32[]{:S(2)}) collective-permute-start(f32[2,264,128]{2,1,0:T(8,128)S(1)} %send_blocks.18), channel_id=1, source_target_pairs={{0,16},{1,17},{2,18},{3,19},{4,20},{5,21},{6,22},{7,23},{8,9},{9,8... | collective-permute-start | bytes 811016 | tf_op jit(solution)/shard_map/ppermute | solution.py:268
  15.2 1.5 %collective-permute-start.8 = (f32[2,264,128]{2,1,0:T(8,128)S(1)}, f32[2,264,128]{2,1,0:T(8,128)S(1)}, u32[]{:S(2)}, u32[]{:S(2)}) collective-permute-start(f32[2,264,128]{2,1,0:T(8,128)S(1)} %send_blocks.22), channel_id=1, source_target_pairs={{0,16},{1,17},{2,18},{3,19},{4,20},{5,21},{6,22},{7,23},{8,9},{9,8... | collective-permute-start | bytes 811016 | tf_op jit(solution)/shard_map/ppermute | solution.py:268
  16.9 0.6 %collective-permute-start.1 = (f32[2,264,128]{2,1,0:T(8,128)S(1)}, f32[2,264,128]{2,1,0:T(8,128)S(1)}, u32[]{:S(2)}, u32[]{:S(2)}) collective-permute-start(f32[2,264,128]{2,1,0:T(8,128)S(1)} %send_blocks.15), channel_id=1, source_target_pairs={{0,16},{1,17},{2,18},{3,19},{4,20},{5,21},{6,22},{7,23},{8,9},{9,8... | collective-permute-start | bytes 811016 | tf_op jit(solution)/shard_map/ppermute | solution.py:268
  17.5 1.3 %collective-permute-done.11.refs_5_ = f32[2,264,128]{2,1,0:T(8,128)S(1)} collective-permute-done((f32[2,264,128]{2,1,0:T(8,128)S(1)}, f32[2,264,128]{2,1,0:T(8,128)S(1)}, u32[]{:S(2)}, u32[]{:S(2)}) %collective-permute-start.11) | collective-permute-done | bytes 270368 | tf_op jit(solution)/shard_map/ppermute | solution.py:268
  18.8 2.1 %collective-permute-start.12 = (f32[1,264,128]{2,1,0:T(8,128)S(1)}, f32[1,264,128]{2,1,0:T(8,128)S(1)}, u32[]{:S(2)}, u32[]{:S(2)}) collective-permute-start(f32[1,264,128]{2,1,0:T(8,128)S(1)} %send_blocks.25), channel_id=1, source_target_pairs={{0,1},{1,0},{2,3},{3,2},{4,5},{5,4},{6,7},{7,6},{8,24},{9,25},{10,... | collective-permute-start | bytes 405512 | tf_op jit(solution)/shard_map/ppermute | solution.py:268
  20.9 1.4 %collective-permute-done.4.refs_5_ = f32[2,264,128]{2,1,0:T(8,128)S(1)} collective-permute-done((f32[2,264,128]{2,1,0:T(8,128)S(1)}, f32[2,264,128]{2,1,0:T(8,128)S(1)}, u32[]{:S(2)}, u32[]{:S(2)}) %collective-permute-start.4) | collective-permute-done | bytes 270368 | tf_op jit(solution)/shard_map/ppermute | solution.py:268
  22.3 2.3 %collective-permute-start.5 = (f32[1,264,128]{2,1,0:T(8,128)S(1)}, f32[1,264,128]{2,1,0:T(8,128)S(1)}, u32[]{:S(2)}, u32[]{:S(2)}) collective-permute-start(f32[1,264,128]{2,1,0:T(8,128)S(1)} %send_blocks.19), channel_id=1, source_target_pairs={{0,1},{1,0},{2,3},{3,2},{4,5},{5,4},{6,7},{7,6},{8,24},{9,25},{10,... | collective-permute-start | bytes 405512 | tf_op jit(solution)/shard_map/ppermute | solution.py:268
  24.7 2.8 %collective-permute-done.8.refs_5_ = f32[2,264,128]{2,1,0:T(8,128)S(1)} collective-permute-done((f32[2,264,128]{2,1,0:T(8,128)S(1)}, f32[2,264,128]{2,1,0:T(8,128)S(1)}, u32[]{:S(2)}, u32[]{:S(2)}) %collective-permute-start.8) | collective-permute-done | bytes 270368 | tf_op jit(solution)/shard_map/ppermute | solution.py:268
  27.5 2.1 %collective-permute-start.9 = (f32[1,264,128]{2,1,0:T(8,128)S(1)}, f32[1,264,128]{2,1,0:T(8,128)S(1)}, u32[]{:S(2)}, u32[]{:S(2)}) collective-permute-start(f32[1,264,128]{2,1,0:T(8,128)S(1)} %send_blocks.23), channel_id=1, source_target_pairs={{0,1},{1,0},{2,3},{3,2},{4,5},{5,4},{6,7},{7,6},{8,24},{9,25},{10,... | collective-permute-start | bytes 405512 | tf_op jit(solution)/shard_map/ppermute | solution.py:268
  29.7 1.6 %collective-permute-start.13 = (f32[1,264,128]{2,1,0:T(8,128)S(1)}, f32[1,264,128]{2,1,0:T(8,128)S(1)}, u32[]{:S(2)}, u32[]{:S(2)}) collective-permute-start(f32[1,264,128]{2,1,0:T(8,128)S(1)} %send_blocks.26), channel_id=1, source_target_pairs={{0,2},{1,3},{2,0},{3,1},{4,6},{5,7},{6,4},{7,5},{8,10},{9,11},{10,... | collective-permute-start | bytes 405512 | tf_op jit(solution)/shard_map/ppermute | solution.py:268
  31.3 0.5 %collective-permute-done.1.refs_5_ = f32[2,264,128]{2,1,0:T(8,128)S(1)} collective-permute-done((f32[2,264,128]{2,1,0:T(8,128)S(1)}, f32[2,264,128]{2,1,0:T(8,128)S(1)}, u32[]{:S(2)}, u32[]{:S(2)}) %collective-permute-start.1) | collective-permute-done | bytes 270368 | tf_op jit(solution)/shard_map/ppermute | solution.py:268
  31.9 2.1 %collective-permute-start.2 = (f32[1,264,128]{2,1,0:T(8,128)S(1)}, f32[1,264,128]{2,1,0:T(8,128)S(1)}, u32[]{:S(2)}, u32[]{:S(2)}) collective-permute-start(f32[1,264,128]{2,1,0:T(8,128)S(1)} %send_blocks.16), channel_id=1, source_target_pairs={{0,1},{1,0},{2,3},{3,2},{4,5},{5,4},{6,7},{7,6},{8,24},{9,25},{10,... | collective-permute-start | bytes 405512 | tf_op jit(solution)/shard_map/ppermute | solution.py:268
  34.0 1.6 %collective-permute-start.6 = (f32[1,264,128]{2,1,0:T(8,128)S(1)}, f32[1,264,128]{2,1,0:T(8,128)S(1)}, u32[]{:S(2)}, u32[]{:S(2)}) collective-permute-start(f32[1,264,128]{2,1,0:T(8,128)S(1)} %send_blocks.20), channel_id=1, source_target_pairs={{0,2},{1,3},{2,0},{3,1},{4,6},{5,7},{6,4},{7,5},{8,10},{9,11},{10,... | collective-permute-start | bytes 405512 | tf_op jit(solution)/shard_map/ppermute | solution.py:268
  35.8 2.6 %collective-permute-start.14 = (f32[1,264,128]{2,1,0:T(8,128)S(1)}, f32[1,264,128]{2,1,0:T(8,128)S(1)}, u32[]{:S(2)}, u32[]{:S(2)}) collective-permute-start(f32[1,264,128]{2,1,0:T(8,128)S(1)} %send_blocks.27), channel_id=1, source_target_pairs={{0,4},{1,5},{2,6},{3,7},{4,0},{5,1},{6,2},{7,3},{8,12},{9,13},{10,... | collective-permute-start | bytes 405512 | tf_op jit(solution)/shard_map/ppermute | solution.py:268
  38.4 1.1 %collective-permute-done.6.refs_7_ = f32[1,264,128]{2,1,0:T(8,128)S(1)} collective-permute-done((f32[1,264,128]{2,1,0:T(8,128)S(1)}, f32[1,264,128]{2,1,0:T(8,128)S(1)}, u32[]{:S(2)}, u32[]{:S(2)}) %collective-permute-start.6) | collective-permute-done | bytes 135200 | tf_op jit(solution)/shard_map/ppermute | solution.py:268
  39.5 3.7 %collective-permute-done.14.refs_8_ = f32[1,264,128]{2,1,0:T(8,128)S(1)} collective-permute-done((f32[1,264,128]{2,1,0:T(8,128)S(1)}, f32[1,264,128]{2,1,0:T(8,128)S(1)}, u32[]{:S(2)}, u32[]{:S(2)}) %collective-permute-start.14) | collective-permute-done | bytes 135200 | tf_op jit(solution)/shard_map/ppermute | solution.py:268
  43.2 0.8 %finish.1 = (f32[128,256]{1,0:T(8,128)}, f32[1,128]{1,0:T(1,128)}) custom-call(f32[12288,128]{1,0:T(8,128)S(1)} %get-tuple-element.9.refs_0_, f32[12288,128]{1,0:T(8,128)S(1)} %get-tuple-element.10.refs_1_, f32[12288,128]{1,0:T(8,128)S(1)} %get-tuple-element.11.refs_2_, f32[12288,128]{1,0:T(8,128)S(1)} %get-tuple-element.12.refs_3_, ...), custom_call_target="tpu_custom_call" | custom-call | tf_op jit(solution)/shard_map/finish/pallas_call | solution.py:247
  (22 shorter events, 1.4 us)
Async XLA Ops:
  9.1 2.1 %collective-permute-start.10 = (f32[4,264,128]{2,1,0:T(8,128)S(1)}, f32[4,264,128]{2,1,0:T(8,128)S(1)}, u32[]{:S(2)}, u32[]{:S(2)}) collective-permute-start(f32[4,264,128]{2,1,0:T(8,128)S(1)} %get-tuple-element.13), channel_id=1, source_target_pairs={{0,8},{1,9},{2,10},{3,11},{4,12},{5,13},{6,14},{7,15},{8,0},{9,1},... | collective-permute-start | bytes 1622024 | tf_op jit(solution)/shard_map/ppermute | solution.py:268
  9.9 4.4 %collective-permute-start.3 = (f32[4,264,128]{2,1,0:T(8,128)S(1)}, f32[4,264,128]{2,1,0:T(8,128)S(1)}, u32[]{:S(2)}, u32[]{:S(2)}) collective-permute-start(f32[4,264,128]{2,1,0:T(8,128)S(1)} %send_blocks.17), channel_id=1, source_target_pairs={{0,8},{1,9},{2,10},{3,11},{4,12},{5,13},{6,14},{7,15},{8,0},{9,1},... | collective-permute-start | bytes 1622024 | tf_op jit(solution)/shard_map/ppermute | solution.py:268
  10.2 4.9 %collective-permute-start.7 = (f32[4,264,128]{2,1,0:T(8,128)S(1)}, f32[4,264,128]{2,1,0:T(8,128)S(1)}, u32[]{:S(2)}, u32[]{:S(2)}) collective-permute-start(f32[4,264,128]{2,1,0:T(8,128)S(1)} %send_blocks.21), channel_id=1, source_target_pairs={{0,8},{1,9},{2,10},{3,11},{4,12},{5,13},{6,14},{7,15},{8,0},{9,1},... | collective-permute-start | bytes 1622024 | tf_op jit(solution)/shard_map/ppermute | solution.py:268
  11.0 5.8 %collective-permute-start = (f32[4,264,128]{2,1,0:T(8,128)S(1)}, f32[4,264,128]{2,1,0:T(8,128)S(1)}, u32[]{:S(2)}, u32[]{:S(2)}) collective-permute-start(f32[4,264,128]{2,1,0:T(8,128)S(1)} %send_blocks.14), channel_id=1, source_target_pairs={{0,8},{1,9},{2,10},{3,11},{4,12},{5,13},{6,14},{7,15},{8,0},{9,1},... | collective-permute-start | bytes 1622024 | tf_op jit(solution)/shard_map/ppermute | solution.py:268
  11.4 7.4 %collective-permute-start.11 = (f32[2,264,128]{2,1,0:T(8,128)S(1)}, f32[2,264,128]{2,1,0:T(8,128)S(1)}, u32[]{:S(2)}, u32[]{:S(2)}) collective-permute-start(f32[2,264,128]{2,1,0:T(8,128)S(1)} %send_blocks.24), channel_id=1, source_target_pairs={{0,16},{1,17},{2,18},{3,19},{4,20},{5,21},{6,22},{7,23},{8,9},{9,8... | collective-permute-start | bytes 811016 | tf_op jit(solution)/shard_map/ppermute | solution.py:268
  14.5 7.8 %collective-permute-start.4 = (f32[2,264,128]{2,1,0:T(8,128)S(1)}, f32[2,264,128]{2,1,0:T(8,128)S(1)}, u32[]{:S(2)}, u32[]{:S(2)}) collective-permute-start(f32[2,264,128]{2,1,0:T(8,128)S(1)} %send_blocks.18), channel_id=1, source_target_pairs={{0,16},{1,17},{2,18},{3,19},{4,20},{5,21},{6,22},{7,23},{8,9},{9,8... | collective-permute-start | bytes 811016 | tf_op jit(solution)/shard_map/ppermute | solution.py:268
  15.2 12.2 %collective-permute-start.8 = (f32[2,264,128]{2,1,0:T(8,128)S(1)}, f32[2,264,128]{2,1,0:T(8,128)S(1)}, u32[]{:S(2)}, u32[]{:S(2)}) collective-permute-start(f32[2,264,128]{2,1,0:T(8,128)S(1)} %send_blocks.22), channel_id=1, source_target_pairs={{0,16},{1,17},{2,18},{3,19},{4,20},{5,21},{6,22},{7,23},{8,9},{9,8... | collective-permute-start | bytes 811016 | tf_op jit(solution)/shard_map/ppermute | solution.py:268
  16.9 14.9 %collective-permute-start.1 = (f32[2,264,128]{2,1,0:T(8,128)S(1)}, f32[2,264,128]{2,1,0:T(8,128)S(1)}, u32[]{:S(2)}, u32[]{:S(2)}) collective-permute-start(f32[2,264,128]{2,1,0:T(8,128)S(1)} %send_blocks.15), channel_id=1, source_target_pairs={{0,16},{1,17},{2,18},{3,19},{4,20},{5,21},{6,22},{7,23},{8,9},{9,8... | collective-permute-start | bytes 811016 | tf_op jit(solution)/shard_map/ppermute | solution.py:268
  18.8 10.7 %collective-permute-start.12 = (f32[1,264,128]{2,1,0:T(8,128)S(1)}, f32[1,264,128]{2,1,0:T(8,128)S(1)}, u32[]{:S(2)}, u32[]{:S(2)}) collective-permute-start(f32[1,264,128]{2,1,0:T(8,128)S(1)} %send_blocks.25), channel_id=1, source_target_pairs={{0,1},{1,0},{2,3},{3,2},{4,5},{5,4},{6,7},{7,6},{8,24},{9,25},{10,... | collective-permute-start | bytes 405512 | tf_op jit(solution)/shard_map/ppermute | solution.py:268
  22.3 11.6 %collective-permute-start.5 = (f32[1,264,128]{2,1,0:T(8,128)S(1)}, f32[1,264,128]{2,1,0:T(8,128)S(1)}, u32[]{:S(2)}, u32[]{:S(2)}) collective-permute-start(f32[1,264,128]{2,1,0:T(8,128)S(1)} %send_blocks.19), channel_id=1, source_target_pairs={{0,1},{1,0},{2,3},{3,2},{4,5},{5,4},{6,7},{7,6},{8,24},{9,25},{10,... | collective-permute-start | bytes 405512 | tf_op jit(solution)/shard_map/ppermute | solution.py:268
  27.5 8.1 %collective-permute-start.9 = (f32[1,264,128]{2,1,0:T(8,128)S(1)}, f32[1,264,128]{2,1,0:T(8,128)S(1)}, u32[]{:S(2)}, u32[]{:S(2)}) collective-permute-start(f32[1,264,128]{2,1,0:T(8,128)S(1)} %send_blocks.23), channel_id=1, source_target_pairs={{0,1},{1,0},{2,3},{3,2},{4,5},{5,4},{6,7},{7,6},{8,24},{9,25},{10,... | collective-permute-start | bytes 405512 | tf_op jit(solution)/shard_map/ppermute | solution.py:268
  29.7 6.0 %collective-permute-start.13 = (f32[1,264,128]{2,1,0:T(8,128)S(1)}, f32[1,264,128]{2,1,0:T(8,128)S(1)}, u32[]{:S(2)}, u32[]{:S(2)}) collective-permute-start(f32[1,264,128]{2,1,0:T(8,128)S(1)} %send_blocks.26), channel_id=1, source_target_pairs={{0,2},{1,3},{2,0},{3,1},{4,6},{5,7},{6,4},{7,5},{8,10},{9,11},{10,... | collective-permute-start | bytes 405512 | tf_op jit(solution)/shard_map/ppermute | solution.py:268
  31.9 6.5 %collective-permute-start.2 = (f32[1,264,128]{2,1,0:T(8,128)S(1)}, f32[1,264,128]{2,1,0:T(8,128)S(1)}, u32[]{:S(2)}, u32[]{:S(2)}) collective-permute-start(f32[1,264,128]{2,1,0:T(8,128)S(1)} %send_blocks.16), channel_id=1, source_target_pairs={{0,1},{1,0},{2,3},{3,2},{4,5},{5,4},{6,7},{7,6},{8,24},{9,25},{10,... | collective-permute-start | bytes 405512 | tf_op jit(solution)/shard_map/ppermute | solution.py:268
  34.0 5.5 %collective-permute-start.6 = (f32[1,264,128]{2,1,0:T(8,128)S(1)}, f32[1,264,128]{2,1,0:T(8,128)S(1)}, u32[]{:S(2)}, u32[]{:S(2)}) collective-permute-start(f32[1,264,128]{2,1,0:T(8,128)S(1)} %send_blocks.20), channel_id=1, source_target_pairs={{0,2},{1,3},{2,0},{3,1},{4,6},{5,7},{6,4},{7,5},{8,10},{9,11},{10,... | collective-permute-start | bytes 405512 | tf_op jit(solution)/shard_map/ppermute | solution.py:268
  35.8 7.4 %collective-permute-start.14 = (f32[1,264,128]{2,1,0:T(8,128)S(1)}, f32[1,264,128]{2,1,0:T(8,128)S(1)}, u32[]{:S(2)}, u32[]{:S(2)}) collective-permute-start(f32[1,264,128]{2,1,0:T(8,128)S(1)} %send_blocks.27), channel_id=1, source_target_pairs={{0,4},{1,5},{2,6},{3,7},{4,0},{5,1},{6,2},{7,3},{8,12},{9,13},{10,... | collective-permute-start | bytes 405512 | tf_op jit(solution)/shard_map/ppermute | solution.py:268

commit v4 on v3

--- a/solution.py
+++ b/solution.py
@@ -6,6 +6,7 @@
 from jax.experimental import pallas as pl
 from jax.experimental.pallas import tpu as pltpu
 from jax.sharding import PartitionSpec as P
+
 
 KEYS = 4096
 LANES = 128
@@ -30,13 +31,27 @@
         self.groups = self.block // SUB
         self.part = self.block * self.tiles
         self.unit = self.part + SUB
+        self.all = tuple(range(self.tiles))
         rep = bits_of(n_rep)
         dom = [len(rep) + b for b in bits_of(n_dom)]
         self.core, self.second, self.third, self.near, *self.middle, self.far = dom + rep
         head = [self.core, self.far, self.near]
         self.even = [*head, self.second, self.third, *self.middle]
         self.odd = [*head, self.third, self.second, *self.middle]
-        self.chunk = self.devices // 8
+
+    def blocks(self, **fixed):
+        names = ["core", "far", "near", "first", "then"]
+        names += [f"middle{i}" for i in range(len(self.middle))]
+        weight = {n: 1 << at for at, n in enumerate(reversed(names))}
+        return [
+            b
+            for b in range(self.devices)
+            if all(bool(b & weight[n]) == bool(v) for n, v in fixed.items())
+        ], weight
+
+    def payload(self, blocks, cols, counted):
+        lines = self.block * len(cols) + (SUB if counted else 0)
+        return jax.ShapeDtypeStruct((len(blocks), lines, LANES), jnp.float32)
 
     def virtual(self, place, order):
         out = jnp.zeros_like(place)
@@ -51,32 +66,40 @@
         ]
 
 
-def sum_block(plan, tables, base, out, at, arrived):
-    row = lax.broadcasted_iota(jnp.int32, (SUB, LANES), 0)
-    lane = lax.broadcasted_iota(jnp.int32, (SUB, LANES), 1)
+def sum_block(plan, tables, base, out, at, arrived, cols, counted):
     first = pl.multiple_of(base * (plan.groups * plan.group), SUB)
-    counts = jnp.zeros((SUB, LANES), jnp.float32)
+
+    def table_sum(g, t):
+        d = pl.ds(first + g * plan.group + t * SUB, SUB)
+        total = tables[0][d, :]
+        for table in tables[1:]:
+            total = total + table[d, :]
+        return total
+
     for g in range(plan.groups):
-        for t in range(plan.tiles + 1):
-            d = pl.ds(first + g * plan.group + t * SUB, SUB)
-            total = tables[0][d, :]
-            for table in tables[1:]:
-                total = total + table[d, :]
-            if t == plan.tiles:
-                counts = jnp.where(lane == row + g * SUB, total, counts)
-                continue
-            to = pl.ds((g * plan.tiles + t) * SUB, SUB)
-            for ref, where in arrived:
-                total = total + ref[where, to, :]
-            out[at, to, :] = total
-    to = pl.ds(plan.part, SUB)
-    total = jnp.broadcast_to(jnp.sum(counts, axis=0, keepdims=True), (SUB, LANES))
-    for ref, where in arrived:
-        total = total + ref[where, to, :]
-    out[at, to, :] = total
-
-
-def table_kernel(plan, n_rep, owner, offset, facts, sent, *rest):
+        for t in cols:
+            total = table_sum(g, t)
+            for ref, where, own in arrived:
+                if t in own:
+                    line = (g * len(own) + own.index(t)) * SUB
+                    total = total + ref[where, pl.ds(line, SUB), :]
+            line = (g * len(cols) + cols.index(t)) * SUB
+            out[at, pl.ds(line, SUB), :] = total
+    if counted:
+        row = lax.broadcasted_iota(jnp.int32, (SUB, LANES), 0)
+        lane = lax.broadcasted_iota(jnp.int32, (SUB, LANES), 1)
+        counts = jnp.zeros((SUB, LANES), jnp.float32)
+        for g in range(plan.groups):
+            counts = jnp.where(lane == row + g * SUB, table_sum(g, plan.tiles), counts)
+        total = jnp.broadcast_to(jnp.sum(counts, axis=0, keepdims=True), (SUB, LANES))
+        for ref, where, own in arrived:
+            line = plan.block * len(own)
+            if ref.shape[1] > line:
+                total = total + ref[where, pl.ds(line, SUB), :]
+        out[at, pl.ds(plan.block * len(cols), SUB), :] = total
+
+
+def table_kernel(plan, n_rep, entries, cols, counted, owner, offset, facts, sent, *rest):
     tables = rest[:TABLES]
     buf, owner_v, offset_v, addr_v, addr_s, same_v, same_s, sem, small = rest[TABLES:]
     n = plan.rows // LANES
@@ -160,14 +183,10 @@
 
     lax.fori_loop(0, half, add_rows, 0)
 
-    def send(i, _):
-        sum_block(plan, tables, 7 * plan.chunk + i, sent, i, ())
-        return 0
-
-    lax.fori_loop(0, plan.chunk, send, 0)
-
-
-def make_table(plan, n_rep, owner, offset, facts):
+    send_runs(plan, tables, (), sent, entries, cols, counted)
+
+
+def make_table(plan, n_rep, owner, offset, facts, blocks, cols, counted):
     rows = plan.rows
     view = facts.reshape(rows // SUB, SUB, plan.tiles, LANES).transpose(0, 2, 1, 3)
     view = view.reshape(rows // SUB, plan.tiles * SUB, LANES)
@@ -180,8 +199,10 @@
     hbm = pl.BlockSpec(memory_space=pltpu.HBM)
     table = jax.ShapeDtypeStruct((KEYS // SUB * plan.group, LANES), jnp.float32)
     return pl.pallas_call(
-        functools.partial(table_kernel, plan, n_rep),
-        out_shape=[jax.ShapeDtypeStruct((plan.chunk, plan.unit, LANES), jnp.float32)]
+        functools.partial(
+            table_kernel, plan, n_rep, [(b, ()) for b in blocks], cols, counted
+        ),
+        out_shape=[plan.payload(blocks, cols, counted)]
         + [table] * TABLES,
         in_specs=[hbm, hbm, hbm],
         out_specs=[VMEM] * (1 + TABLES),
@@ -201,21 +222,36 @@
     )(*far)
 
 
-def send_kernel(plan, base, first, n_got, *refs):
+def send_runs(plan, tables, arrays, out, entries, cols, counted):
+    def follows(a, b):
+        return b[0] == a[0] + 1 and [(k, u + 1, o) for k, u, o in a[1]] == list(b[1])
+
+    start = 0
+    while start < len(entries):
+        end = start + 1
+        while end < len(entries) and follows(entries[end - 1], entries[end]):
+            end += 1
+        block, terms = entries[start]
+
+        def body(i, _):
+            arrived = [(arrays[k], u + i, own) for k, u, own in terms]
+            sum_block(plan, tables, block + i, out, start + i, arrived, cols, counted)
+            return 0
+
+        lax.fori_loop(0, end - start, body, 0)
+        start = end
+
+
+def send_kernel(plan, n_got, entries, cols, counted, *refs):
     tables, got, out = refs[:TABLES], refs[TABLES : TABLES + n_got], refs[-1]
-
-    def body(i, _):
-        sum_block(plan, tables, base + first + i, out, i, [(g, first + i) for g in got])
-        return 0
-
-    lax.fori_loop(0, out.shape[0], body, 0)
-
-
-def send_blocks(plan, tables, got, base, first, count):
+    send_runs(plan, tables, got, out, entries, cols, counted)
+
+
+def send_blocks(plan, tables, got, entries, cols, counted):
     n = len(tables) + len(got)
     return pl.pallas_call(
-        functools.partial(send_kernel, plan, base, first, len(got)),
-        out_shape=jax.ShapeDtypeStruct((count, plan.unit, LANES), jnp.float32),
+        functools.partial(send_kernel, plan, len(got), entries, cols, counted),
+        out_shape=plan.payload(entries, cols, counted),
         in_specs=[VMEM] * n,
         out_specs=VMEM,
         compiler_params=pltpu.CompilerParams(vmem_limit_bytes=4 << 20),
@@ -223,10 +259,11 @@
     )(*tables, *got)
 
 
-def finish_kernel(plan, n_got, *refs):
+def finish_kernel(plan, n_got, terms, *refs):
     tables, got = refs[:TABLES], refs[TABLES : TABLES + n_got]
     means, counts, total = refs[TABLES + n_got :]
-    sum_block(plan, tables, 0, total, 0, [(g, 0) for g in got])
+    arrived = [(got[k], u, own) for k, u, own in terms]
+    sum_block(plan, tables, 0, total, 0, arrived, plan.all, True)
     row = total[0, pl.ds(plan.part, 1), :]
     counts[...] = row[:, : plan.block]
     shape = (plan.block, LANES)
@@ -243,9 +280,9 @@
             )
 
 
-def finish(plan, tables, got):
+def finish(plan, tables, got, terms):
     means, counts = pl.pallas_call(
-        functools.partial(finish_kernel, plan, len(got)),
+        functools.partial(finish_kernel, plan, len(got), terms),
         out_shape=[
             jax.ShapeDtypeStruct((plan.block, plan.tiles * LANES), jnp.float32),
             jax.ShapeDtypeStruct((1, plan.block), jnp.float32),
@@ -262,33 +299,95 @@
 def per_device(facts, row_owner, key_offset):
     n_dom, n_rep = lax.axis_size("dom"), lax.axis_size("rep")
     plan = Plan(n_dom, n_rep, *facts.shape)
-
-    def swap(x, even_bit, odd_bit=None):
-        odd_bit = even_bit if odd_bit is None else odd_bit
-        return lax.ppermute(x, AXES, plan.pairs(even_bit, odd_bit))
-
-    sent, *tables = make_table(plan, n_rep, row_owner[:, 0], key_offset, facts)
-    size = plan.chunk
-    got = [[] for _ in range(4)]
-    for c in reversed(range(4)):
-        if c < 3:
-            sent = send_blocks(plan, tables, [], (4 + c) * size, 0, size)
-        got[c].append(swap(sent, plan.core))
-    stages = [(plan.second, plan.third), (plan.third, plan.second)]
-    stages += [(bit, bit) for bit in plan.middle]
-    for stage in stages:
-        size //= 2
-        for c in reversed(range(4)):
-            sent = send_blocks(plan, tables, got[c], c * plan.chunk, size, size)
-            got[c].append(swap(sent, *stage))
-    for c, to, bit in ((3, 2, plan.near), (1, 0, plan.near), (2, 0, plan.far)):
-        sent = send_blocks(plan, tables, got[c], c * plan.chunk, 0, 1)
-        got[to].append(swap(sent, bit))
-    return finish(plan, tables, got[0])
+    pairs = {
+        "core": (plan.core, plan.core),
+        "first": (plan.second, plan.third),
+        "then": (plan.third, plan.second),
+        "near": (plan.near, plan.near),
+        "far": (plan.far, plan.far),
+    }
+    extra = middle_names(len(plan.middle))
+    pairs |= {n: (bit, bit) for n, bit in zip(extra, plan.middle)}
+    middle = len(plan.all) // 2
+    left, right = plan.all[:middle], plan.all[middle:]
+    arrived = {}
+    tables = None
+
+    def entries_of(blocks, cols):
+        got, entries = [], []
+        for b in blocks:
+            terms = []
+            for array, unit, own in arrived.get(b, []):
+                if not set(own) & set(cols):
+                    continue
+                at = [i for i, g in enumerate(got) if g is array]
+                if not at:
+                    at = [len(got)]
+                    got.append(array)
+                terms.append((at[0], unit, own))
+            entries.append((b, tuple(terms)))
+        return got, entries
+
+    parts = {"left": (left, True), "right": (right, False), "whole": (plan.all, True)}
+    for bit, which, fixed in schedule(extra):
+        cols, counted = parts[which]
+        blocks, weight = plan.blocks(**{bit: 1}, **fixed)
+        if tables is None:
+            sent, *tables = make_table(
+                plan, n_rep, row_owner[:, 0], key_offset, facts, blocks, cols, counted
+            )
+        else:
+            got, entries = entries_of(blocks, cols)
+            sent = send_blocks(plan, tables, got, entries, cols, counted)
+        array = lax.ppermute(sent, AXES, plan.pairs(*pairs[bit]))
+        for unit, b in enumerate(blocks):
+            arrived.setdefault(b - weight[bit], []).append((array, unit, cols))
+    got, [(_, terms)] = entries_of([0], plan.all)
+    return finish(plan, tables, got, terms)
+
+
+def middle_names(n):
+    return [f"middle{i}" for i in range(n)]
+
+
+def schedule(extra):
+    moves = []
+
+    def move(bit, which, **fixed):
+        moves.append((bit, which, fixed))
+
+    def thin(which, **fixed):
+        for i, n in enumerate(extra):
+            move(n, which, core=0, first=0, then=0, **{m: 0 for m in extra[:i]}, **fixed)
+
+    end = dict(core=0, first=0, then=0, **{n: 0 for n in extra})
+    move("core", "left", far=1)
+    move("core", "right", far=1)
+    move("core", "whole", far=0, near=1)
+    move("core", "whole", far=0, near=0)
+    move("first", "left", core=0, far=1)
+    move("first", "right", core=0, far=1)
+    move("near", "whole", core=0, far=0, first=1)
+    move("then", "whole", core=0, far=0, near=1, first=0)
+    move("then", "left", core=0, far=1, first=0)
+    thin("left", far=1)
+    thin("whole", far=0, near=1)
+    move("near", "whole", far=0, **end)
+    move("then", "right", core=0, far=1, first=0)
+    thin("right", far=1)
+    move("near", "left", far=1, **end)
+    move("first", "whole", core=0, far=0, near=0)
+    move("near", "right", far=1, **end)
+    move("far", "left", near=0, **end)
+    move("then", "whole", core=0, far=0, near=0, first=0)
+    thin("whole", far=0, near=0)
+    move("far", "right", near=0, **end)
+    return moves
 
 
 def solution(mesh):
     placed = (P(AXES, None), P(AXES, None), P(AXES))
+
     return jax.shard_map(
         per_device,
         mesh=mesh,

time: 44.4 us -> 45.6 us (1.027)
  starting transfers between devices: 21.5 us -> 22.6 us
    ppermute x15 -> x17, starting transfers between devices: 21.5 us -> 22.6 us  [per_device(): array = lax.ppermute(sent, AXES, plan.pairs(*pairs[bit]))]
    ppermute x15 -> x17, waiting for transfers between devices: 10.8 us -> 11.2 us  [per_device(): array = lax.ppermute(sent, AXES, plan.pairs(*pairs[bit]))]
    pallas_call x16 -> x18, Pallas kernels: 11 us -> 11 us  [the longest x1 8.55 us: make_table(): pl.pallas_call(functools.partial(table_kernel, plan, n_rep, [(b, ()) for...]
  transfers between devices with their start and end apart: 15 -> 17, of which waited for: 7 -> 5; matrix products, arithmetic and copies ran while one was open for 0% -> 0% of each run, Pallas kernels for 4% -> 3%
where the time goes in v4:
time: 45.6 us; the launch traced here: 45.5 us
  starting transfers between devices  22.6 us (50%)
  waiting for transfers between devices  11.2 us (25%)
  Pallas kernels  11 us (24%)
  between operations  0.69 us (2%)
    ppermute x17, starting transfers between devices, per_device(): array = lax.ppermute(sent, AXES, plan.pairs(*pairs[bit]))  22.6 us
    ppermute x17, waiting for transfers between devices, per_device(): array = lax.ppermute(sent, AXES, plan.pairs(*pairs[bit]))  11.2 us
    pallas_call x1, Pallas kernels, make_table(): pl.pallas_call(functools.partial(table_kernel, plan, n_rep, [(b, ()) for...  8.55 us
    pallas_call x16, Pallas kernels, send_blocks(): pl.pallas_call(functools.partial(send_kernel, plan, len(got), entries, co...  1.6 us
  transfers between devices with their start and end apart: 17, of which 5 were waited for; matrix products, arithmetic and copies ran while one was open for 0% of the time, Pallas kernels for 3%

profile of v4, /device:TPU:0, one launch (start us, length us, event | category | flops | bytes accessed | tf_op | source)
XLA Modules:
  0.0 45.5 jit_solution(6404461089059236348)
XLA Ops:
  0.6 8.6 %make_table.1 = (f32[8,136,128]{2,1,0:T(8,128)S(1)}, f32[12288,128]{1,0:T(8,128)S(1)}, f32[12288,128]{1,0:T(8,128)S(1)}, f32[12288,128]{1,0:T(8,128)S(1)}, f32[12288,128]{1,0:T(8,128)S(1)}) custom-call(s32[32,128]{1,0:T(8,128)} %bitcast.9, s32[32,128]{1,0:T(8,128)} %bitcast.10, f32[512,16,128]{2,1,0:T(8,128)} %bitcast.8), custom_call_target="tpu_custom_call" | custom-call | tf_op jit(solution)/shard_map/make_table/pallas_call | solution.py:201
  9.2 0.2 send_blocks.17
  9.4 0.6 %collective-permute-start.1 = (f32[4,264,128]{2,1,0:T(8,128)S(1)}, f32[4,264,128]{2,1,0:T(8,128)S(1)}, u32[]{:S(2)}, u32[]{:S(2)}) collective-permute-start(f32[4,264,128]{2,1,0:T(8,128)S(1)} %send_blocks.17), channel_id=1, source_target_pairs={{0,8},{1,9},{2,10},{3,11},{4,12},{5,13},{6,14},{7,15},{8,0},{9,1},... | collective-permute-start | bytes 1622024 | tf_op jit(solution)/shard_map/ppermute | solution.py:342
  10.2 0.5 %collective-permute-start.12 = (f32[8,128,128]{2,1,0:T(8,128)S(1)}, f32[8,128,128]{2,1,0:T(8,128)S(1)}, u32[]{:S(2)}, u32[]{:S(2)}) collective-permute-start(f32[8,128,128]{2,1,0:T(8,128)S(1)} %send_blocks.27), channel_id=1, source_target_pairs={{0,8},{1,9},{2,10},{3,11},{4,12},{5,13},{6,14},{7,15},{8,0},{9,1},... | collective-permute-start | bytes 1572872 | tf_op jit(solution)/shard_map/ppermute | solution.py:342
  10.7 0.2 send_blocks.16
  11.0 0.5 %collective-permute-done.1.refs_4_ = f32[4,264,128]{2,1,0:T(8,128)S(1)} collective-permute-done((f32[4,264,128]{2,1,0:T(8,128)S(1)}, f32[4,264,128]{2,1,0:T(8,128)S(1)}, u32[]{:S(2)}, u32[]{:S(2)}) %collective-permute-start.1) | collective-permute-done | bytes 540704 | tf_op jit(solution)/shard_map/ppermute | solution.py:342
  11.7 3.0 %collective-permute-start.4 = (f32[2,264,128]{2,1,0:T(8,128)S(1)}, f32[2,264,128]{2,1,0:T(8,128)S(1)}, u32[]{:S(2)}, u32[]{:S(2)}) collective-permute-start(f32[2,264,128]{2,1,0:T(8,128)S(1)} %send_blocks.20), channel_id=1, source_target_pairs={{0,2},{1,3},{2,0},{3,1},{4,6},{5,7},{6,4},{7,5},{8,10},{9,11},{10,... | collective-permute-start | bytes 811016 | tf_op jit(solution)/shard_map/ppermute | solution.py:342
  14.8 1.6 %collective-permute-start.7 = (f32[4,136,128]{2,1,0:T(8,128)S(1)}, f32[4,136,128]{2,1,0:T(8,128)S(1)}, u32[]{:S(2)}, u32[]{:S(2)}) collective-permute-start(f32[4,136,128]{2,1,0:T(8,128)S(1)} %send_blocks.22), channel_id=1, source_target_pairs={{0,16},{1,17},{2,18},{3,19},{4,20},{5,21},{6,22},{7,23},{8,9},{9,8... | collective-permute-start | bytes 835592 | tf_op jit(solution)/shard_map/ppermute | solution.py:342
  16.5 0.6 %collective-permute-start.13 = (f32[4,128,128]{2,1,0:T(8,128)S(1)}, f32[4,128,128]{2,1,0:T(8,128)S(1)}, u32[]{:S(2)}, u32[]{:S(2)}) collective-permute-start(f32[4,128,128]{2,1,0:T(8,128)S(1)} %send_blocks.28), channel_id=1, source_target_pairs={{0,16},{1,17},{2,18},{3,19},{4,20},{5,21},{6,22},{7,23},{8,9},{9,8... | collective-permute-start | bytes 786440 | tf_op jit(solution)/shard_map/ppermute | solution.py:342
  17.1 4.4 %collective-permute-done.4.refs_5_ = f32[2,264,128]{2,1,0:T(8,128)S(1)} collective-permute-done((f32[2,264,128]{2,1,0:T(8,128)S(1)}, f32[2,264,128]{2,1,0:T(8,128)S(1)}, u32[]{:S(2)}, u32[]{:S(2)}) %collective-permute-start.4) | collective-permute-done | bytes 270368 | tf_op jit(solution)/shard_map/ppermute | solution.py:342
  21.6 1.8 %collective-permute-start.5 = (f32[2,264,128]{2,1,0:T(8,128)S(1)}, f32[2,264,128]{2,1,0:T(8,128)S(1)}, u32[]{:S(2)}, u32[]{:S(2)}) collective-permute-start(f32[2,264,128]{2,1,0:T(8,128)S(1)} %send_blocks.21), channel_id=1, source_target_pairs={{0,16},{1,17},{2,18},{3,19},{4,20},{5,21},{6,22},{7,23},{8,9},{9,8... | collective-permute-start | bytes 811016 | tf_op jit(solution)/shard_map/ppermute | solution.py:342
  23.4 1.5 %collective-permute-start.8 = (f32[2,136,128]{2,1,0:T(8,128)S(1)}, f32[2,136,128]{2,1,0:T(8,128)S(1)}, u32[]{:S(2)}, u32[]{:S(2)}) collective-permute-start(f32[2,136,128]{2,1,0:T(8,128)S(1)} %send_blocks.23), channel_id=1, source_target_pairs={{0,1},{1,0},{2,3},{3,2},{4,5},{5,4},{6,7},{7,6},{8,24},{9,25},{10,... | collective-permute-start | bytes 417800 | tf_op jit(solution)/shard_map/ppermute | solution.py:342
  25.0 0.6 %collective-permute-start.2 = (f32[1,264,128]{2,1,0:T(8,128)S(1)}, f32[1,264,128]{2,1,0:T(8,128)S(1)}, u32[]{:S(2)}, u32[]{:S(2)}) collective-permute-start(f32[1,264,128]{2,1,0:T(8,128)S(1)} %send_blocks.18), channel_id=1, source_target_pairs={{0,1},{1,0},{2,3},{3,2},{4,5},{5,4},{6,7},{7,6},{8,24},{9,25},{10,... | collective-permute-start | bytes 405512 | tf_op jit(solution)/shard_map/ppermute | solution.py:342
  25.7 1.5 %collective-permute-start.14 = (f32[2,128,128]{2,1,0:T(8,128)S(1)}, f32[2,128,128]{2,1,0:T(8,128)S(1)}, u32[]{:S(2)}, u32[]{:S(2)}) collective-permute-start(f32[2,128,128]{2,1,0:T(8,128)S(1)} %send_blocks.29), channel_id=1, source_target_pairs={{0,1},{1,0},{2,3},{3,2},{4,5},{5,4},{6,7},{7,6},{8,24},{9,25},{10,... | collective-permute-start | bytes 393224 | tf_op jit(solution)/shard_map/ppermute | solution.py:342
  27.3 1.3 %collective-permute-done.8.refs_6_ = f32[2,136,128]{2,1,0:T(8,128)S(1)} collective-permute-done((f32[2,136,128]{2,1,0:T(8,128)S(1)}, f32[2,136,128]{2,1,0:T(8,128)S(1)}, u32[]{:S(2)}, u32[]{:S(2)}) %collective-permute-start.8) | collective-permute-done | bytes 139296 | tf_op jit(solution)/shard_map/ppermute | solution.py:342
  28.6 1.6 %collective-permute-start.9 = (f32[1,136,128]{2,1,0:T(8,128)S(1)}, f32[1,136,128]{2,1,0:T(8,128)S(1)}, u32[]{:S(2)}, u32[]{:S(2)}) collective-permute-start(f32[1,136,128]{2,1,0:T(8,128)S(1)} %send_blocks.24), channel_id=1, source_target_pairs={{0,2},{1,3},{2,0},{3,1},{4,6},{5,7},{6,4},{7,5},{8,10},{9,11},{10,... | collective-permute-start | bytes 208904 | tf_op jit(solution)/shard_map/ppermute | solution.py:342
  30.3 1.5 %collective-permute-start.3 = (f32[1,264,128]{2,1,0:T(8,128)S(1)}, f32[1,264,128]{2,1,0:T(8,128)S(1)}, u32[]{:S(2)}, u32[]{:S(2)}) collective-permute-start(f32[1,264,128]{2,1,0:T(8,128)S(1)} %send_blocks.19), channel_id=1, source_target_pairs={{0,2},{1,3},{2,0},{3,1},{4,6},{5,7},{6,4},{7,5},{8,10},{9,11},{10,... | collective-permute-start | bytes 405512 | tf_op jit(solution)/shard_map/ppermute | solution.py:342
  31.9 1.4 %collective-permute-start.11 = (f32[1,264,128]{2,1,0:T(8,128)S(1)}, f32[1,264,128]{2,1,0:T(8,128)S(1)}, u32[]{:S(2)}, u32[]{:S(2)}) collective-permute-start(f32[1,264,128]{2,1,0:T(8,128)S(1)} %send_blocks.26), channel_id=1, source_target_pairs={{0,1},{1,0},{2,3},{3,2},{4,5},{5,4},{6,7},{7,6},{8,24},{9,25},{10,... | collective-permute-start | bytes 405512 | tf_op jit(solution)/shard_map/ppermute | solution.py:342
  33.4 1.1 %collective-permute-start.15 = (f32[1,128,128]{2,1,0:T(8,128)S(1)}, f32[1,128,128]{2,1,0:T(8,128)S(1)}, u32[]{:S(2)}, u32[]{:S(2)}) collective-permute-start(f32[1,128,128]{2,1,0:T(8,128)S(1)} %send_blocks.30), channel_id=1, source_target_pairs={{0,2},{1,3},{2,0},{3,1},{4,6},{5,7},{6,4},{7,5},{8,10},{9,11},{10,... | collective-permute-start | bytes 196616 | tf_op jit(solution)/shard_map/ppermute | solution.py:342
  34.6 2.6 %collective-permute-start.10 = (f32[1,136,128]{2,1,0:T(8,128)S(1)}, f32[1,136,128]{2,1,0:T(8,128)S(1)}, u32[]{:S(2)}, u32[]{:S(2)}) collective-permute-start(f32[1,136,128]{2,1,0:T(8,128)S(1)} %send_blocks.25), channel_id=1, source_target_pairs={{0,4},{1,5},{2,6},{3,7},{4,0},{5,1},{6,2},{7,3},{8,12},{9,13},{10,... | collective-permute-start | bytes 208904 | tf_op jit(solution)/shard_map/ppermute | solution.py:342
  37.2 1.5 %collective-permute-done.15.refs_7_ = f32[1,128,128]{2,1,0:T(8,128)S(1)} collective-permute-done((f32[1,128,128]{2,1,0:T(8,128)S(1)}, f32[1,128,128]{2,1,0:T(8,128)S(1)}, u32[]{:S(2)}, u32[]{:S(2)}) %collective-permute-start.15) | collective-permute-done | bytes 65568 | tf_op jit(solution)/shard_map/ppermute | solution.py:342
  38.7 2.4 %collective-permute-start.16 = (f32[1,128,128]{2,1,0:T(8,128)S(1)}, f32[1,128,128]{2,1,0:T(8,128)S(1)}, u32[]{:S(2)}, u32[]{:S(2)}) collective-permute-start(f32[1,128,128]{2,1,0:T(8,128)S(1)} %send_blocks.31), channel_id=1, source_target_pairs={{0,4},{1,5},{2,6},{3,7},{4,0},{5,1},{6,2},{7,3},{8,12},{9,13},{10,... | collective-permute-start | bytes 196616 | tf_op jit(solution)/shard_map/ppermute | solution.py:342
  41.1 3.5 %collective-permute-done.16.refs_9_ = f32[1,128,128]{2,1,0:T(8,128)S(1)} collective-permute-done((f32[1,128,128]{2,1,0:T(8,128)S(1)}, f32[1,128,128]{2,1,0:T(8,128)S(1)}, u32[]{:S(2)}, u32[]{:S(2)}) %collective-permute-start.16) | collective-permute-done | bytes 65568 | tf_op jit(solution)/shard_map/ppermute | solution.py:342
  44.7 0.8 %finish.1 = (f32[128,256]{1,0:T(8,128)}, f32[1,128]{1,0:T(1,128)}) custom-call(f32[12288,128]{1,0:T(8,128)S(1)} %get-tuple-element.9.refs_0_, f32[12288,128]{1,0:T(8,128)S(1)} %get-tuple-element.10.refs_1_, f32[12288,128]{1,0:T(8,128)S(1)} %get-tuple-element.11.refs_2_, f32[12288,128]{1,0:T(8,128)S(1)} %get-tuple-element.12.refs_3_, ...), custom_call_target="tpu_custom_call" | custom-call | tf_op jit(solution)/shard_map/finish/pallas_call | solution.py:284
  (28 shorter events, 1.4 us)
Async XLA Ops:
  9.4 2.1 %collective-permute-start.1 = (f32[4,264,128]{2,1,0:T(8,128)S(1)}, f32[4,264,128]{2,1,0:T(8,128)S(1)}, u32[]{:S(2)}, u32[]{:S(2)}) collective-permute-start(f32[4,264,128]{2,1,0:T(8,128)S(1)} %send_blocks.17), channel_id=1, source_target_pairs={{0,8},{1,9},{2,10},{3,11},{4,12},{5,13},{6,14},{7,15},{8,0},{9,1},... | collective-permute-start | bytes 1622024 | tf_op jit(solution)/shard_map/ppermute | solution.py:342
  10.0 4.7 %collective-permute-start.6 = (f32[8,136,128]{2,1,0:T(8,128)S(1)}, f32[8,136,128]{2,1,0:T(8,128)S(1)}, u32[]{:S(2)}, u32[]{:S(2)}) collective-permute-start(f32[8,136,128]{2,1,0:T(8,128)S(1)} %get-tuple-element.13), channel_id=1, source_target_pairs={{0,8},{1,9},{2,10},{3,11},{4,12},{5,13},{6,14},{7,15},{8,0},{9,1},... | collective-permute-start | bytes 1671176 | tf_op jit(solution)/shard_map/ppermute | solution.py:342
  10.2 6.2 %collective-permute-start.12 = (f32[8,128,128]{2,1,0:T(8,128)S(1)}, f32[8,128,128]{2,1,0:T(8,128)S(1)}, u32[]{:S(2)}, u32[]{:S(2)}) collective-permute-start(f32[8,128,128]{2,1,0:T(8,128)S(1)} %send_blocks.27), channel_id=1, source_target_pairs={{0,8},{1,9},{2,10},{3,11},{4,12},{5,13},{6,14},{7,15},{8,0},{9,1},... | collective-permute-start | bytes 1572872 | tf_op jit(solution)/shard_map/ppermute | solution.py:342
  10.9 6.2 %collective-permute-start = (f32[4,264,128]{2,1,0:T(8,128)S(1)}, f32[4,264,128]{2,1,0:T(8,128)S(1)}, u32[]{:S(2)}, u32[]{:S(2)}) collective-permute-start(f32[4,264,128]{2,1,0:T(8,128)S(1)} %send_blocks.16), channel_id=1, source_target_pairs={{0,8},{1,9},{2,10},{3,11},{4,12},{5,13},{6,14},{7,15},{8,0},{9,1},... | collective-permute-start | bytes 1622024 | tf_op jit(solution)/shard_map/ppermute | solution.py:342
  11.7 9.8 %collective-permute-start.4 = (f32[2,264,128]{2,1,0:T(8,128)S(1)}, f32[2,264,128]{2,1,0:T(8,128)S(1)}, u32[]{:S(2)}, u32[]{:S(2)}) collective-permute-start(f32[2,264,128]{2,1,0:T(8,128)S(1)} %send_blocks.20), channel_id=1, source_target_pairs={{0,2},{1,3},{2,0},{3,1},{4,6},{5,7},{6,4},{7,5},{8,10},{9,11},{10,... | collective-permute-start | bytes 811016 | tf_op jit(solution)/shard_map/ppermute | solution.py:342
  14.8 8.5 %collective-permute-start.7 = (f32[4,136,128]{2,1,0:T(8,128)S(1)}, f32[4,136,128]{2,1,0:T(8,128)S(1)}, u32[]{:S(2)}, u32[]{:S(2)}) collective-permute-start(f32[4,136,128]{2,1,0:T(8,128)S(1)} %send_blocks.22), channel_id=1, source_target_pairs={{0,16},{1,17},{2,18},{3,19},{4,20},{5,21},{6,22},{7,23},{8,9},{9,8... | collective-permute-start | bytes 835592 | tf_op jit(solution)/shard_map/ppermute | solution.py:342
  16.5 9.2 %collective-permute-start.13 = (f32[4,128,128]{2,1,0:T(8,128)S(1)}, f32[4,128,128]{2,1,0:T(8,128)S(1)}, u32[]{:S(2)}, u32[]{:S(2)}) collective-permute-start(f32[4,128,128]{2,1,0:T(8,128)S(1)} %send_blocks.28), channel_id=1, source_target_pairs={{0,16},{1,17},{2,18},{3,19},{4,20},{5,21},{6,22},{7,23},{8,9},{9,8... | collective-permute-start | bytes 786440 | tf_op jit(solution)/shard_map/ppermute | solution.py:342
  21.6 10.2 %collective-permute-start.5 = (f32[2,264,128]{2,1,0:T(8,128)S(1)}, f32[2,264,128]{2,1,0:T(8,128)S(1)}, u32[]{:S(2)}, u32[]{:S(2)}) collective-permute-start(f32[2,264,128]{2,1,0:T(8,128)S(1)} %send_blocks.21), channel_id=1, source_target_pairs={{0,16},{1,17},{2,18},{3,19},{4,20},{5,21},{6,22},{7,23},{8,9},{9,8... | collective-permute-start | bytes 811016 | tf_op jit(solution)/shard_map/ppermute | solution.py:342
  23.4 5.1 %collective-permute-start.8 = (f32[2,136,128]{2,1,0:T(8,128)S(1)}, f32[2,136,128]{2,1,0:T(8,128)S(1)}, u32[]{:S(2)}, u32[]{:S(2)}) collective-permute-start(f32[2,136,128]{2,1,0:T(8,128)S(1)} %send_blocks.23), channel_id=1, source_target_pairs={{0,1},{1,0},{2,3},{3,2},{4,5},{5,4},{6,7},{7,6},{8,24},{9,25},{10,... | collective-permute-start | bytes 417800 | tf_op jit(solution)/shard_map/ppermute | solution.py:342
  25.0 5.2 %collective-permute-start.2 = (f32[1,264,128]{2,1,0:T(8,128)S(1)}, f32[1,264,128]{2,1,0:T(8,128)S(1)}, u32[]{:S(2)}, u32[]{:S(2)}) collective-permute-start(f32[1,264,128]{2,1,0:T(8,128)S(1)} %send_blocks.18), channel_id=1, source_target_pairs={{0,1},{1,0},{2,3},{3,2},{4,5},{5,4},{6,7},{7,6},{8,24},{9,25},{10,... | collective-permute-start | bytes 405512 | tf_op jit(solution)/shard_map/ppermute | solution.py:342
  25.7 7.6 %collective-permute-start.14 = (f32[2,128,128]{2,1,0:T(8,128)S(1)}, f32[2,128,128]{2,1,0:T(8,128)S(1)}, u32[]{:S(2)}, u32[]{:S(2)}) collective-permute-start(f32[2,128,128]{2,1,0:T(8,128)S(1)} %send_blocks.29), channel_id=1, source_target_pairs={{0,1},{1,0},{2,3},{3,2},{4,5},{5,4},{6,7},{7,6},{8,24},{9,25},{10,... | collective-permute-start | bytes 393224 | tf_op jit(solution)/shard_map/ppermute | solution.py:342
  28.6 5.9 %collective-permute-start.9 = (f32[1,136,128]{2,1,0:T(8,128)S(1)}, f32[1,136,128]{2,1,0:T(8,128)S(1)}, u32[]{:S(2)}, u32[]{:S(2)}) collective-permute-start(f32[1,136,128]{2,1,0:T(8,128)S(1)} %send_blocks.24), channel_id=1, source_target_pairs={{0,2},{1,3},{2,0},{3,1},{4,6},{5,7},{6,4},{7,5},{8,10},{9,11},{10,... | collective-permute-start | bytes 208904 | tf_op jit(solution)/shard_map/ppermute | solution.py:342
  30.3 10.8 %collective-permute-start.3 = (f32[1,264,128]{2,1,0:T(8,128)S(1)}, f32[1,264,128]{2,1,0:T(8,128)S(1)}, u32[]{:S(2)}, u32[]{:S(2)}) collective-permute-start(f32[1,264,128]{2,1,0:T(8,128)S(1)} %send_blocks.19), channel_id=1, source_target_pairs={{0,2},{1,3},{2,0},{3,1},{4,6},{5,7},{6,4},{7,5},{8,10},{9,11},{10,... | collective-permute-start | bytes 405512 | tf_op jit(solution)/shard_map/ppermute | solution.py:342
  31.9 12.7 %collective-permute-start.11 = (f32[1,264,128]{2,1,0:T(8,128)S(1)}, f32[1,264,128]{2,1,0:T(8,128)S(1)}, u32[]{:S(2)}, u32[]{:S(2)}) collective-permute-start(f32[1,264,128]{2,1,0:T(8,128)S(1)} %send_blocks.26), channel_id=1, source_target_pairs={{0,1},{1,0},{2,3},{3,2},{4,5},{5,4},{6,7},{7,6},{8,24},{9,25},{10,... | collective-permute-start | bytes 405512 | tf_op jit(solution)/shard_map/ppermute | solution.py:342
  33.4 5.3 %collective-permute-start.15 = (f32[1,128,128]{2,1,0:T(8,128)S(1)}, f32[1,128,128]{2,1,0:T(8,128)S(1)}, u32[]{:S(2)}, u32[]{:S(2)}) collective-permute-start(f32[1,128,128]{2,1,0:T(8,128)S(1)} %send_blocks.30), channel_id=1, source_target_pairs={{0,2},{1,3},{2,0},{3,1},{4,6},{5,7},{6,4},{7,5},{8,10},{9,11},{10,... | collective-permute-start | bytes 196616 | tf_op jit(solution)/shard_map/ppermute | solution.py:342
  34.6 10.1 %collective-permute-start.10 = (f32[1,136,128]{2,1,0:T(8,128)S(1)}, f32[1,136,128]{2,1,0:T(8,128)S(1)}, u32[]{:S(2)}, u32[]{:S(2)}) collective-permute-start(f32[1,136,128]{2,1,0:T(8,128)S(1)} %send_blocks.25), channel_id=1, source_target_pairs={{0,4},{1,5},{2,6},{3,7},{4,0},{5,1},{6,2},{7,3},{8,12},{9,13},{10,... | collective-permute-start | bytes 208904 | tf_op jit(solution)/shard_map/ppermute | solution.py:342
  38.7 5.9 %collective-permute-start.16 = (f32[1,128,128]{2,1,0:T(8,128)S(1)}, f32[1,128,128]{2,1,0:T(8,128)S(1)}, u32[]{:S(2)}, u32[]{:S(2)}) collective-permute-start(f32[1,128,128]{2,1,0:T(8,128)S(1)} %send_blocks.31), channel_id=1, source_target_pairs={{0,4},{1,5},{2,6},{3,7},{4,0},{5,1},{6,2},{7,3},{8,12},{9,13},{10,... | collective-permute-start | bytes 196616 | tf_op jit(solution)/shard_map/ppermute | solution.py:342

commit v5 on v4

--- a/solution.py
+++ b/solution.py
@@ -11,7 +11,7 @@
 KEYS = 4096
 LANES = 128
 SUB = 8
-TABLES = 4
+TABLES = 3
 AXES = ("dom", "rep")
 VMEM = pl.BlockSpec(memory_space=pltpu.VMEM)
 
@@ -104,12 +104,11 @@
     buf, owner_v, offset_v, addr_v, addr_s, same_v, same_s, sem, small = rest[TABLES:]
     n = plan.rows // LANES
     half = n // 2
-    per = LANES // SUB
-    wide = plan.tiles * SUB
+    lines = LANES * plan.tiles
 
     def fetch(i):
-        d = pl.ds(i * per, per)
-        return pltpu.make_async_copy(facts.at[d], buf.at[d, pl.ds(0, wide)], sem.at[i])
+        d = pl.ds(i * lines, lines)
+        return pltpu.make_async_copy(facts.at[d], buf.at[d], sem.at[i])
 
     copies = [
         pltpu.make_async_copy(owner, owner_v, small.at[0]),
@@ -122,7 +121,7 @@
         fetch(half + i).start()
 
     def zero(refs):
-        step = SUB * SUB
+        step = 4 * SUB * SUB
 
         def body(i, _):
             for t in refs:
@@ -155,26 +154,24 @@
     for copy in copies:
         copy.start()
     zero(tables[TABLES // 2 :])
-
-    def ones(i, _):
-        for j in range(per):
-            buf[i * per + j, pl.ds(wide, SUB), :] = jnp.ones((SUB, LANES), jnp.float32)
-        return 0
-
-    lax.fori_loop(0, n, ones, 0)
     for copy in copies:
         copy.wait()
+
+    width = plan.tiles + 1
+    counted_line = lax.broadcasted_iota(jnp.int32, (width, LANES), 0) == plan.tiles
+
+    def fact(i, j):
+        at = pl.ds(i * lines + (j // SUB) * plan.tiles * SUB + j % SUB, width, stride=SUB)
+        return jnp.where(counted_line, 1.0, buf[at, :])
 
     def add_rows(i, _):
         fetch(i).wait()
         fetch(half + i).wait()
         for j in range(LANES):
             table = tables[j % TABLES]
-            one = pl.ds(addr_s[i, j], plan.tiles + 1, stride=SUB)
-            two = pl.ds(addr_s[half + i, j], plan.tiles + 1, stride=SUB)
-            lines = pl.ds(j % SUB, plan.tiles + 1, stride=SUB)
-            row_one = buf[i * per + j // SUB, lines, :]
-            row_two = buf[(half + i) * per + j // SUB, lines, :]
+            one = pl.ds(addr_s[i, j], width, stride=SUB)
+            two = pl.ds(addr_s[half + i, j], width, stride=SUB)
+            row_one, row_two = fact(i, j), fact(half + i, j)
             old_one = table[one, :]
             old_two = table[two, :]
             table[one, :] = old_one + row_one
@@ -189,7 +186,7 @@
 def make_table(plan, n_rep, owner, offset, facts, blocks, cols, counted):
     rows = plan.rows
     view = facts.reshape(rows // SUB, SUB, plan.tiles, LANES).transpose(0, 2, 1, 3)
-    view = view.reshape(rows // SUB, plan.tiles * SUB, LANES)
+    view = view.reshape(rows * plan.tiles, LANES)
     lanes = (rows // LANES, LANES)
     half = (rows // LANES // 2, LANES)
     far = [
@@ -207,7 +204,7 @@
         in_specs=[hbm, hbm, hbm],
         out_specs=[VMEM] * (1 + TABLES),
         scratch_shapes=[
-            pltpu.VMEM((rows // SUB, plan.group, LANES), jnp.float32),
+            pltpu.VMEM((rows * plan.tiles + 2 * SUB, LANES), jnp.float32),
             pltpu.VMEM(lanes, jnp.int32),
             pltpu.VMEM(lanes, jnp.int32),
             pltpu.VMEM(lanes, jnp.int32),
@@ -308,8 +305,6 @@
     }
     extra = middle_names(len(plan.middle))
     pairs |= {n: (bit, bit) for n, bit in zip(extra, plan.middle)}
-    middle = len(plan.all) // 2
-    left, right = plan.all[:middle], plan.all[middle:]
     arrived = {}
     tables = None
 
@@ -328,7 +323,7 @@
             entries.append((b, tuple(terms)))
         return got, entries
 
-    parts = {"left": (left, True), "right": (right, False), "whole": (plan.all, True)}
+    parts = {"whole": (plan.all, True)}
     for bit, which, fixed in schedule(extra):
         cols, counted = parts[which]
         blocks, weight = plan.blocks(**{bit: 1}, **fixed)
@@ -353,35 +348,30 @@
 def schedule(extra):
     moves = []
 
-    def move(bit, which, **fixed):
-        moves.append((bit, which, fixed))
-
-    def thin(which, **fixed):
+    def move(bit, **fixed):
+        moves.append((bit, "whole", fixed))
+
+    def then(**fixed):
+        move("then", core=0, first=0, **fixed)
         for i, n in enumerate(extra):
-            move(n, which, core=0, first=0, then=0, **{m: 0 for m in extra[:i]}, **fixed)
+            move(n, core=0, first=0, then=0, **{m: 0 for m in extra[:i]}, **fixed)
 
     end = dict(core=0, first=0, then=0, **{n: 0 for n in extra})
-    move("core", "left", far=1)
-    move("core", "right", far=1)
-    move("core", "whole", far=0, near=1)
-    move("core", "whole", far=0, near=0)
-    move("first", "left", core=0, far=1)
-    move("first", "right", core=0, far=1)
-    move("near", "whole", core=0, far=0, first=1)
-    move("then", "whole", core=0, far=0, near=1, first=0)
-    move("then", "left", core=0, far=1, first=0)
-    thin("left", far=1)
-    thin("whole", far=0, near=1)
-    move("near", "whole", far=0, **end)
-    move("then", "right", core=0, far=1, first=0)
-    thin("right", far=1)
-    move("near", "left", far=1, **end)
-    move("first", "whole", core=0, far=0, near=0)
-    move("near", "right", far=1, **end)
-    move("far", "left", near=0, **end)
-    move("then", "whole", core=0, far=0, near=0, first=0)
-    thin("whole", far=0, near=0)
-    move("far", "right", near=0, **end)
+    move("core", far=1, first=1)
+    move("core", far=1, first=0)
+    move("core", far=0, near=1)
+    move("core", far=0, near=0)
+    move("first", core=0, far=1, near=1)
+    move("first", core=0, far=1, near=0)
+    move("near", core=0, far=0, first=1)
+    then(far=1, near=1)
+    then(far=0, near=1)
+    then(far=1, near=0)
+    move("near", far=1, **end)
+    move("first", core=0, far=0, near=0)
+    move("near", far=0, **end)
+    move("far", near=0, **end)
+    then(far=0, near=0)
     return moves
 
 

time: 45.6 us -> 41.2 us (0.904)
  starting transfers between devices: 22.6 us -> 18.6 us
  Pallas kernels: 11 us -> 10.2 us
    ppermute x17 -> x15, starting transfers between devices: 22.6 us -> 18.6 us  [per_device(): array = lax.ppermute(sent, AXES, plan.pairs(*pairs[bit]))]
    pallas_call x1, Pallas kernels: 8.55 us -> 8.02 us  [make_table(): pl.pallas_call(functools.partial(table_kernel, plan, n_rep, [(b, ()) for...]
    ppermute x17 -> x15, waiting for transfers between devices: 11.2 us -> 11.6 us  [per_device(): array = lax.ppermute(sent, AXES, plan.pairs(*pairs[bit]))]
    pallas_call x16 -> x14, Pallas kernels: 1.6 us -> 1.43 us  [send_blocks(): pl.pallas_call(functools.partial(send_kernel, plan, len(got), entries, co...]
  transfers between devices with their start and end apart: 17 -> 15, of which waited for: 5 -> 8; matrix products, arithmetic and copies ran while one was open for 0% -> 0% of each run, Pallas kernels for 3% -> 3%
where the time goes in v5:
time: 41.2 us; the launch traced here: 41 us
  starting transfers between devices  18.6 us (45%)
  waiting for transfers between devices  11.6 us (28%)
  Pallas kernels  10.2 us (25%)
  between operations  0.67 us (2%)
    ppermute x15, starting transfers between devices, per_device(): array = lax.ppermute(sent, AXES, plan.pairs(*pairs[bit]))  18.6 us
    ppermute x15, waiting for transfers between devices, per_device(): array = lax.ppermute(sent, AXES, plan.pairs(*pairs[bit]))  11.6 us
    pallas_call x1, Pallas kernels, make_table(): pl.pallas_call(functools.partial(table_kernel, plan, n_rep, [(b, ()) for...  8.02 us
    pallas_call x14, Pallas kernels, send_blocks(): pl.pallas_call(functools.partial(send_kernel, plan, len(got), entries, co...  1.43 us
  transfers between devices with their start and end apart: 15, of which 8 were waited for; matrix products, arithmetic and copies ran while one was open for 0% of the time, Pallas kernels for 3%

profile of v5, /device:TPU:0, one launch (start us, length us, event | category | flops | bytes accessed | tf_op | source)
XLA Modules:
  0.0 41.0 jit_solution(12649308964695548633)
XLA Ops:
  0.6 8.0 %make_table.1 = (f32[4,264,128]{2,1,0:T(8,128)S(1)}, f32[12288,128]{1,0:T(8,128)S(1)}, f32[12288,128]{1,0:T(8,128)S(1)}, f32[12288,128]{1,0:T(8,128)S(1)}) custom-call(s32[32,128]{1,0:T(8,128)} %bitcast.9, s32[32,128]{1,0:T(8,128)} %bitcast.10, f32[8192,128]{1,0:T(8,128)} %bitcast.8), custom_call_target="tpu_custom_call" | custom-call | tf_op jit(solution)/shard_map/make_table/pallas_call | solution.py:198
  8.7 0.6 %collective-permute-start.7 = (f32[4,264,128]{2,1,0:T(8,128)S(1)}, f32[4,264,128]{2,1,0:T(8,128)S(1)}, u32[]{:S(2)}, u32[]{:S(2)}) collective-permute-start(f32[4,264,128]{2,1,0:T(8,128)S(1)} %get-tuple-element.11), channel_id=1, source_target_pairs={{0,8},{1,9},{2,10},{3,11},{4,12},{5,13},{6,14},{7,15},{8,0},{9,1},... | collective-permute-start | bytes 1622024 | tf_op jit(solution)/shard_map/ppermute | solution.py:337
  9.2 0.2 send_blocks.15
  9.6 0.6 %collective-permute-start.6 = (f32[4,264,128]{2,1,0:T(8,128)S(1)}, f32[4,264,128]{2,1,0:T(8,128)S(1)}, u32[]{:S(2)}, u32[]{:S(2)}) collective-permute-start(f32[4,264,128]{2,1,0:T(8,128)S(1)} %send_blocks.20), channel_id=1, source_target_pairs={{0,8},{1,9},{2,10},{3,11},{4,12},{5,13},{6,14},{7,15},{8,0},{9,1},... | collective-permute-start | bytes 1622024 | tf_op jit(solution)/shard_map/ppermute | solution.py:337
  10.4 0.3 collective-permute-done.7.refs_3_
  10.9 2.9 %collective-permute-start.10 = (f32[2,264,128]{2,1,0:T(8,128)S(1)}, f32[2,264,128]{2,1,0:T(8,128)S(1)}, u32[]{:S(2)}, u32[]{:S(2)}) collective-permute-start(f32[2,264,128]{2,1,0:T(8,128)S(1)} %send_blocks.23), channel_id=1, source_target_pairs={{0,16},{1,17},{2,18},{3,19},{4,20},{5,21},{6,22},{7,23},{8,9},{9,8... | collective-permute-start | bytes 811016 | tf_op jit(solution)/shard_map/ppermute | solution.py:337
  13.9 1.6 %collective-permute-start.2 = (f32[2,264,128]{2,1,0:T(8,128)S(1)}, f32[2,264,128]{2,1,0:T(8,128)S(1)}, u32[]{:S(2)}, u32[]{:S(2)}) collective-permute-start(f32[2,264,128]{2,1,0:T(8,128)S(1)} %send_blocks.16), channel_id=1, source_target_pairs={{0,2},{1,3},{2,0},{3,1},{4,6},{5,7},{6,4},{7,5},{8,10},{9,11},{10,... | collective-permute-start | bytes 811016 | tf_op jit(solution)/shard_map/ppermute | solution.py:337
  15.7 0.7 %collective-permute-start.8 = (f32[2,264,128]{2,1,0:T(8,128)S(1)}, f32[2,264,128]{2,1,0:T(8,128)S(1)}, u32[]{:S(2)}, u32[]{:S(2)}) collective-permute-start(f32[2,264,128]{2,1,0:T(8,128)S(1)} %send_blocks.21), channel_id=1, source_target_pairs={{0,16},{1,17},{2,18},{3,19},{4,20},{5,21},{6,22},{7,23},{8,9},{9,8... | collective-permute-start | bytes 811016 | tf_op jit(solution)/shard_map/ppermute | solution.py:337
  16.4 1.9 %collective-permute-done.10.refs_4_ = f32[2,264,128]{2,1,0:T(8,128)S(1)} collective-permute-done((f32[2,264,128]{2,1,0:T(8,128)S(1)}, f32[2,264,128]{2,1,0:T(8,128)S(1)}, u32[]{:S(2)}, u32[]{:S(2)}) %collective-permute-start.10) | collective-permute-done | bytes 270368 | tf_op jit(solution)/shard_map/ppermute | solution.py:337
  18.3 2.1 %collective-permute-start.11 = (f32[1,264,128]{2,1,0:T(8,128)S(1)}, f32[1,264,128]{2,1,0:T(8,128)S(1)}, u32[]{:S(2)}, u32[]{:S(2)}) collective-permute-start(f32[1,264,128]{2,1,0:T(8,128)S(1)} %send_blocks.24), channel_id=1, source_target_pairs={{0,1},{1,0},{2,3},{3,2},{4,5},{5,4},{6,7},{7,6},{8,24},{9,25},{10,... | collective-permute-start | bytes 405512 | tf_op jit(solution)/shard_map/ppermute | solution.py:337
  20.4 1.8 %collective-permute-done.2.refs_4_ = f32[2,264,128]{2,1,0:T(8,128)S(1)} collective-permute-done((f32[2,264,128]{2,1,0:T(8,128)S(1)}, f32[2,264,128]{2,1,0:T(8,128)S(1)}, u32[]{:S(2)}, u32[]{:S(2)}) %collective-permute-start.2) | collective-permute-done | bytes 270368 | tf_op jit(solution)/shard_map/ppermute | solution.py:337
  22.4 1.6 %collective-permute-start.3 = (f32[2,264,128]{2,1,0:T(8,128)S(1)}, f32[2,264,128]{2,1,0:T(8,128)S(1)}, u32[]{:S(2)}, u32[]{:S(2)}) collective-permute-start(f32[2,264,128]{2,1,0:T(8,128)S(1)} %send_blocks.17), channel_id=1, source_target_pairs={{0,16},{1,17},{2,18},{3,19},{4,20},{5,21},{6,22},{7,23},{8,9},{9,8... | collective-permute-start | bytes 811016 | tf_op jit(solution)/shard_map/ppermute | solution.py:337
  24.0 0.9 %collective-permute-start.4 = (f32[1,264,128]{2,1,0:T(8,128)S(1)}, f32[1,264,128]{2,1,0:T(8,128)S(1)}, u32[]{:S(2)}, u32[]{:S(2)}) collective-permute-start(f32[1,264,128]{2,1,0:T(8,128)S(1)} %send_blocks.18), channel_id=1, source_target_pairs={{0,1},{1,0},{2,3},{3,2},{4,5},{5,4},{6,7},{7,6},{8,24},{9,25},{10,... | collective-permute-start | bytes 405512 | tf_op jit(solution)/shard_map/ppermute | solution.py:337
  25.0 1.2 %collective-permute-start.9 = (f32[1,264,128]{2,1,0:T(8,128)S(1)}, f32[1,264,128]{2,1,0:T(8,128)S(1)}, u32[]{:S(2)}, u32[]{:S(2)}) collective-permute-start(f32[1,264,128]{2,1,0:T(8,128)S(1)} %send_blocks.22), channel_id=1, source_target_pairs={{0,1},{1,0},{2,3},{3,2},{4,5},{5,4},{6,7},{7,6},{8,24},{9,25},{10,... | collective-permute-start | bytes 405512 | tf_op jit(solution)/shard_map/ppermute | solution.py:337
  26.3 1.6 %collective-permute-start.12 = (f32[1,264,128]{2,1,0:T(8,128)S(1)}, f32[1,264,128]{2,1,0:T(8,128)S(1)}, u32[]{:S(2)}, u32[]{:S(2)}) collective-permute-start(f32[1,264,128]{2,1,0:T(8,128)S(1)} %send_blocks.25), channel_id=1, source_target_pairs={{0,2},{1,3},{2,0},{3,1},{4,6},{5,7},{6,4},{7,5},{8,10},{9,11},{10,... | collective-permute-start | bytes 405512 | tf_op jit(solution)/shard_map/ppermute | solution.py:337
  27.9 1.1 %collective-permute-done.4.refs_4_ = f32[1,264,128]{2,1,0:T(8,128)S(1)} collective-permute-done((f32[1,264,128]{2,1,0:T(8,128)S(1)}, f32[1,264,128]{2,1,0:T(8,128)S(1)}, u32[]{:S(2)}, u32[]{:S(2)}) %collective-permute-start.4) | collective-permute-done | bytes 135200 | tf_op jit(solution)/shard_map/ppermute | solution.py:337
  29.1 1.6 %collective-permute-start.5 = (f32[1,264,128]{2,1,0:T(8,128)S(1)}, f32[1,264,128]{2,1,0:T(8,128)S(1)}, u32[]{:S(2)}, u32[]{:S(2)}) collective-permute-start(f32[1,264,128]{2,1,0:T(8,128)S(1)} %send_blocks.19), channel_id=1, source_target_pairs={{0,2},{1,3},{2,0},{3,1},{4,6},{5,7},{6,4},{7,5},{8,10},{9,11},{10,... | collective-permute-start | bytes 405512 | tf_op jit(solution)/shard_map/ppermute | solution.py:337
  30.8 1.5 %collective-permute-done.12.refs_6_ = f32[1,264,128]{2,1,0:T(8,128)S(1)} collective-permute-done((f32[1,264,128]{2,1,0:T(8,128)S(1)}, f32[1,264,128]{2,1,0:T(8,128)S(1)}, u32[]{:S(2)}, u32[]{:S(2)}) %collective-permute-start.12) | collective-permute-done | bytes 135200 | tf_op jit(solution)/shard_map/ppermute | solution.py:337
  32.4 2.7 %collective-permute-start.13 = (f32[1,264,128]{2,1,0:T(8,128)S(1)}, f32[1,264,128]{2,1,0:T(8,128)S(1)}, u32[]{:S(2)}, u32[]{:S(2)}) collective-permute-start(f32[1,264,128]{2,1,0:T(8,128)S(1)} %send_blocks.26), channel_id=1, source_target_pairs={{0,4},{1,5},{2,6},{3,7},{4,0},{5,1},{6,2},{7,3},{8,12},{9,13},{10,... | collective-permute-start | bytes 405512 | tf_op jit(solution)/shard_map/ppermute | solution.py:337
  35.2 0.2 collective-permute-start.14
  35.4 0.3 collective-permute-done.5.refs_5_
  35.7 4.1 %collective-permute-done.13.refs_6_ = f32[1,264,128]{2,1,0:T(8,128)S(1)} collective-permute-done((f32[1,264,128]{2,1,0:T(8,128)S(1)}, f32[1,264,128]{2,1,0:T(8,128)S(1)}, u32[]{:S(2)}, u32[]{:S(2)}) %collective-permute-start.13) | collective-permute-done | bytes 135200 | tf_op jit(solution)/shard_map/ppermute | solution.py:337
  39.8 0.5 %collective-permute-done.14.refs_7_ = f32[1,264,128]{2,1,0:T(8,128)S(1)} collective-permute-done((f32[1,264,128]{2,1,0:T(8,128)S(1)}, f32[1,264,128]{2,1,0:T(8,128)S(1)}, u32[]{:S(2)}, u32[]{:S(2)}) %collective-permute-start.14) | collective-permute-done | bytes 135200 | tf_op jit(solution)/shard_map/ppermute | solution.py:337
  40.2 0.8 %finish.1 = (f32[128,256]{1,0:T(8,128)}, f32[1,128]{1,0:T(1,128)}) custom-call(f32[12288,128]{1,0:T(8,128)S(1)} %get-tuple-element.8.refs_0_, f32[12288,128]{1,0:T(8,128)S(1)} %get-tuple-element.9.refs_1_, f32[12288,128]{1,0:T(8,128)S(1)} %get-tuple-element.10.refs_2_, f32[4,264,128]{2,1,0:T(8,128)S(1)} %collective-permute-done.refs_3_, ...), custom_call_target="tpu_custom_call" | custom-call | tf_op jit(solution)/shard_map/finish/pallas_call | solution.py:281
  (22 shorter events, 1.5 us)
Async XLA Ops:
  8.7 2.1 %collective-permute-start.7 = (f32[4,264,128]{2,1,0:T(8,128)S(1)}, f32[4,264,128]{2,1,0:T(8,128)S(1)}, u32[]{:S(2)}, u32[]{:S(2)}) collective-permute-start(f32[4,264,128]{2,1,0:T(8,128)S(1)} %get-tuple-element.11), channel_id=1, source_target_pairs={{0,8},{1,9},{2,10},{3,11},{4,12},{5,13},{6,14},{7,15},{8,0},{9,1},... | collective-permute-start | bytes 1622024 | tf_op jit(solution)/shard_map/ppermute | solution.py:337
  9.4 4.5 %collective-permute-start.1 = (f32[4,264,128]{2,1,0:T(8,128)S(1)}, f32[4,264,128]{2,1,0:T(8,128)S(1)}, u32[]{:S(2)}, u32[]{:S(2)}) collective-permute-start(f32[4,264,128]{2,1,0:T(8,128)S(1)} %send_blocks.15), channel_id=1, source_target_pairs={{0,8},{1,9},{2,10},{3,11},{4,12},{5,13},{6,14},{7,15},{8,0},{9,1},... | collective-permute-start | bytes 1622024 | tf_op jit(solution)/shard_map/ppermute | solution.py:337
  9.6 6.7 %collective-permute-start.6 = (f32[4,264,128]{2,1,0:T(8,128)S(1)}, f32[4,264,128]{2,1,0:T(8,128)S(1)}, u32[]{:S(2)}, u32[]{:S(2)}) collective-permute-start(f32[4,264,128]{2,1,0:T(8,128)S(1)} %send_blocks.20), channel_id=1, source_target_pairs={{0,8},{1,9},{2,10},{3,11},{4,12},{5,13},{6,14},{7,15},{8,0},{9,1},... | collective-permute-start | bytes 1622024 | tf_op jit(solution)/shard_map/ppermute | solution.py:337
  10.3 10.1 %collective-permute-start = (f32[4,264,128]{2,1,0:T(8,128)S(1)}, f32[4,264,128]{2,1,0:T(8,128)S(1)}, u32[]{:S(2)}, u32[]{:S(2)}) collective-permute-start(f32[4,264,128]{2,1,0:T(8,128)S(1)} %send_blocks.14), channel_id=1, source_target_pairs={{0,8},{1,9},{2,10},{3,11},{4,12},{5,13},{6,14},{7,15},{8,0},{9,1},... | collective-permute-start | bytes 1622024 | tf_op jit(solution)/shard_map/ppermute | solution.py:337
  10.9 7.4 %collective-permute-start.10 = (f32[2,264,128]{2,1,0:T(8,128)S(1)}, f32[2,264,128]{2,1,0:T(8,128)S(1)}, u32[]{:S(2)}, u32[]{:S(2)}) collective-permute-start(f32[2,264,128]{2,1,0:T(8,128)S(1)} %send_blocks.23), channel_id=1, source_target_pairs={{0,16},{1,17},{2,18},{3,19},{4,20},{5,21},{6,22},{7,23},{8,9},{9,8... | collective-permute-start | bytes 811016 | tf_op jit(solution)/shard_map/ppermute | solution.py:337
  13.9 8.3 %collective-permute-start.2 = (f32[2,264,128]{2,1,0:T(8,128)S(1)}, f32[2,264,128]{2,1,0:T(8,128)S(1)}, u32[]{:S(2)}, u32[]{:S(2)}) collective-permute-start(f32[2,264,128]{2,1,0:T(8,128)S(1)} %send_blocks.16), channel_id=1, source_target_pairs={{0,2},{1,3},{2,0},{3,1},{4,6},{5,7},{6,4},{7,5},{8,10},{9,11},{10,... | collective-permute-start | bytes 811016 | tf_op jit(solution)/shard_map/ppermute | solution.py:337
  15.7 9.2 %collective-permute-start.8 = (f32[2,264,128]{2,1,0:T(8,128)S(1)}, f32[2,264,128]{2,1,0:T(8,128)S(1)}, u32[]{:S(2)}, u32[]{:S(2)}) collective-permute-start(f32[2,264,128]{2,1,0:T(8,128)S(1)} %send_blocks.21), channel_id=1, source_target_pairs={{0,16},{1,17},{2,18},{3,19},{4,20},{5,21},{6,22},{7,23},{8,9},{9,8... | collective-permute-start | bytes 811016 | tf_op jit(solution)/shard_map/ppermute | solution.py:337
  18.3 7.9 %collective-permute-start.11 = (f32[1,264,128]{2,1,0:T(8,128)S(1)}, f32[1,264,128]{2,1,0:T(8,128)S(1)}, u32[]{:S(2)}, u32[]{:S(2)}) collective-permute-start(f32[1,264,128]{2,1,0:T(8,128)S(1)} %send_blocks.24), channel_id=1, source_target_pairs={{0,1},{1,0},{2,3},{3,2},{4,5},{5,4},{6,7},{7,6},{8,24},{9,25},{10,... | collective-permute-start | bytes 405512 | tf_op jit(solution)/shard_map/ppermute | solution.py:337
  22.4 12.7 %collective-permute-start.3 = (f32[2,264,128]{2,1,0:T(8,128)S(1)}, f32[2,264,128]{2,1,0:T(8,128)S(1)}, u32[]{:S(2)}, u32[]{:S(2)}) collective-permute-start(f32[2,264,128]{2,1,0:T(8,128)S(1)} %send_blocks.17), channel_id=1, source_target_pairs={{0,16},{1,17},{2,18},{3,19},{4,20},{5,21},{6,22},{7,23},{8,9},{9,8... | collective-permute-start | bytes 811016 | tf_op jit(solution)/shard_map/ppermute | solution.py:337
  24.0 5.1 %collective-permute-start.4 = (f32[1,264,128]{2,1,0:T(8,128)S(1)}, f32[1,264,128]{2,1,0:T(8,128)S(1)}, u32[]{:S(2)}, u32[]{:S(2)}) collective-permute-start(f32[1,264,128]{2,1,0:T(8,128)S(1)} %send_blocks.18), channel_id=1, source_target_pairs={{0,1},{1,0},{2,3},{3,2},{4,5},{5,4},{6,7},{7,6},{8,24},{9,25},{10,... | collective-permute-start | bytes 405512 | tf_op jit(solution)/shard_map/ppermute | solution.py:337
  25.0 5.8 %collective-permute-start.9 = (f32[1,264,128]{2,1,0:T(8,128)S(1)}, f32[1,264,128]{2,1,0:T(8,128)S(1)}, u32[]{:S(2)}, u32[]{:S(2)}) collective-permute-start(f32[1,264,128]{2,1,0:T(8,128)S(1)} %send_blocks.22), channel_id=1, source_target_pairs={{0,1},{1,0},{2,3},{3,2},{4,5},{5,4},{6,7},{7,6},{8,24},{9,25},{10,... | collective-permute-start | bytes 405512 | tf_op jit(solution)/shard_map/ppermute | solution.py:337
  26.3 6.0 %collective-permute-start.12 = (f32[1,264,128]{2,1,0:T(8,128)S(1)}, f32[1,264,128]{2,1,0:T(8,128)S(1)}, u32[]{:S(2)}, u32[]{:S(2)}) collective-permute-start(f32[1,264,128]{2,1,0:T(8,128)S(1)} %send_blocks.25), channel_id=1, source_target_pairs={{0,2},{1,3},{2,0},{3,1},{4,6},{5,7},{6,4},{7,5},{8,10},{9,11},{10,... | collective-permute-start | bytes 405512 | tf_op jit(solution)/shard_map/ppermute | solution.py:337
  29.1 6.5 %collective-permute-start.5 = (f32[1,264,128]{2,1,0:T(8,128)S(1)}, f32[1,264,128]{2,1,0:T(8,128)S(1)}, u32[]{:S(2)}, u32[]{:S(2)}) collective-permute-start(f32[1,264,128]{2,1,0:T(8,128)S(1)} %send_blocks.19), channel_id=1, source_target_pairs={{0,2},{1,3},{2,0},{3,1},{4,6},{5,7},{6,4},{7,5},{8,10},{9,11},{10,... | collective-permute-start | bytes 405512 | tf_op jit(solution)/shard_map/ppermute | solution.py:337
  32.4 7.4 %collective-permute-start.13 = (f32[1,264,128]{2,1,0:T(8,128)S(1)}, f32[1,264,128]{2,1,0:T(8,128)S(1)}, u32[]{:S(2)}, u32[]{:S(2)}) collective-permute-start(f32[1,264,128]{2,1,0:T(8,128)S(1)} %send_blocks.26), channel_id=1, source_target_pairs={{0,4},{1,5},{2,6},{3,7},{4,0},{5,1},{6,2},{7,3},{8,12},{9,13},{10,... | collective-permute-start | bytes 405512 | tf_op jit(solution)/shard_map/ppermute | solution.py:337
  35.2 5.1 %collective-permute-start.14 = (f32[1,264,128]{2,1,0:T(8,128)S(1)}, f32[1,264,128]{2,1,0:T(8,128)S(1)}, u32[]{:S(2)}, u32[]{:S(2)}) collective-permute-start(f32[1,264,128]{2,1,0:T(8,128)S(1)} %send_blocks.27), channel_id=1, source_target_pairs={{0,1},{1,0},{2,3},{3,2},{4,5},{5,4},{6,7},{7,6},{8,24},{9,25},{10,... | collective-permute-start | bytes 405512 | tf_op jit(solution)/shard_map/ppermute | solution.py:337

commit v6 on v5

--- a/solution.py
+++ b/solution.py
@@ -101,7 +101,7 @@
 
 def table_kernel(plan, n_rep, entries, cols, counted, owner, offset, facts, sent, *rest):
     tables = rest[:TABLES]
-    buf, owner_v, offset_v, addr_v, addr_s, same_v, same_s, sem, small = rest[TABLES:]
+    buf, owner_v, offset_v, addr_v, one_s, two_s, same_v, same_s, sem, small = rest[TABLES:]
     n = plan.rows // LANES
     half = n // 2
     lines = LANES * plan.tiles
@@ -132,7 +132,7 @@
 
         lax.fori_loop(0, refs[0].shape[0] // step, body, 0)
 
-    zero(tables[: TABLES // 2])
+    zero(tables[: (TABLES + 1) // 2])
     for copy in copies:
         copy.wait()
     me = lax.axis_index(AXES[0]) * n_rep + lax.axis_index(AXES[1])
@@ -148,30 +148,41 @@
     addr_v[...] = addr
     same_v[...] = jnp.where(addr[:half] == addr[half:], 1.0, 0.0)
     copies = [
-        pltpu.make_async_copy(addr_v, addr_s, small.at[2]),
-        pltpu.make_async_copy(same_v, same_s, small.at[3]),
+        pltpu.make_async_copy(addr_v.at[pl.ds(0, half)], one_s, small.at[2]),
+        pltpu.make_async_copy(addr_v.at[pl.ds(half, half)], two_s, small.at[3]),
+        pltpu.make_async_copy(same_v, same_s, small.at[4]),
     ]
     for copy in copies:
         copy.start()
-    zero(tables[TABLES // 2 :])
+    zero(tables[(TABLES + 1) // 2 :])
     for copy in copies:
         copy.wait()
 
     width = plan.tiles + 1
-    counted_line = lax.broadcasted_iota(jnp.int32, (width, LANES), 0) == plan.tiles
-
-    def fact(i, j):
-        at = pl.ds(i * lines + (j // SUB) * plan.tiles * SUB + j % SUB, width, stride=SUB)
-        return jnp.where(counted_line, 1.0, buf[at, :])
+    line = lax.broadcasted_iota(jnp.int32, (SUB, LANES), 0)
+
+    def eight_facts(i, g):
+        base = i * lines + g * (SUB * plan.tiles)
+        return [
+            buf[pl.ds(pl.multiple_of(base + t * SUB, SUB), SUB), :] for t in range(plan.tiles)
+        ]
+
+    def fact(parts, j):
+        row = jnp.ones((SUB, LANES), jnp.float32)
+        for t, part in enumerate(parts):
+            row = jnp.where(line == t, pltpu.roll(part, (t - j) % SUB, 0), row)
+        return row[:width]
 
     def add_rows(i, _):
         fetch(i).wait()
         fetch(half + i).wait()
         for j in range(LANES):
+            if j % SUB == 0:
+                first, then = eight_facts(i, j // SUB), eight_facts(half + i, j // SUB)
             table = tables[j % TABLES]
-            one = pl.ds(addr_s[i, j], width, stride=SUB)
-            two = pl.ds(addr_s[half + i, j], width, stride=SUB)
-            row_one, row_two = fact(i, j), fact(half + i, j)
+            one = pl.ds(one_s[i, j], width, stride=SUB)
+            two = pl.ds(two_s[i, j], width, stride=SUB)
+            row_one, row_two = fact(first, j % SUB), fact(then, j % SUB)
             old_one = table[one, :]
             old_two = table[two, :]
             table[one, :] = old_one + row_one
@@ -208,11 +219,12 @@
             pltpu.VMEM(lanes, jnp.int32),
             pltpu.VMEM(lanes, jnp.int32),
             pltpu.VMEM(lanes, jnp.int32),
-            pltpu.SMEM(lanes, jnp.int32),
+            pltpu.SMEM(half, jnp.int32),
+            pltpu.SMEM(half, jnp.int32),
             pltpu.VMEM(half, jnp.float32),
             pltpu.SMEM(half, jnp.float32),
             pltpu.SemaphoreType.DMA((rows // LANES,)),
-            pltpu.SemaphoreType.DMA((4,)),
+            pltpu.SemaphoreType.DMA((5,)),
         ],
         compiler_params=pltpu.CompilerParams(vmem_limit_bytes=12 << 20),
         name="make_table",
@@ -323,9 +335,8 @@
             entries.append((b, tuple(terms)))
         return got, entries
 
-    parts = {"whole": (plan.all, True)}
-    for bit, which, fixed in schedule(extra):
-        cols, counted = parts[which]
+    cols, counted = plan.all, True
+    for bit, fixed in schedule(extra):
         blocks, weight = plan.blocks(**{bit: 1}, **fixed)
         if tables is None:
             sent, *tables = make_table(
@@ -349,7 +360,7 @@
     moves = []
 
     def move(bit, **fixed):
-        moves.append((bit, "whole", fixed))
+        moves.append((bit, fixed))
 
     def then(**fixed):
         move("then", core=0, first=0, **fixed)
@@ -361,14 +372,16 @@
     move("core", far=1, first=0)
     move("core", far=0, near=1)
     move("core", far=0, near=0)
-    move("first", core=0, far=1, near=1)
-    move("first", core=0, far=1, near=0)
-    move("near", core=0, far=0, first=1)
+    move("first", core=0, far=1, then=1)
+    move("first", core=0, far=1, then=0)
+    move("near", core=0, far=0, first=1, then=1)
+    move("near", core=0, far=0, first=1, then=0)
     then(far=1, near=1)
+    then(far=1, near=0)
     then(far=0, near=1)
-    then(far=1, near=0)
     move("near", far=1, **end)
-    move("first", core=0, far=0, near=0)
+    move("first", core=0, far=0, near=0, then=1)
+    move("first", core=0, far=0, near=0, then=0)
     move("near", far=0, **end)
     move("far", near=0, **end)
     then(far=0, near=0)

time: 41.2 us -> 40.2 us (0.976)
  waiting for transfers between devices: 11.6 us -> 8.15 us
  starting transfers between devices: 18.6 us -> 21.4 us
    ppermute x15 -> x17, waiting for transfers between devices: 11.6 us -> 8.15 us  [per_device(): array = lax.ppermute(sent, AXES, plan.pairs(*pairs[bit]))]
    ppermute x15 -> x17, starting transfers between devices: 18.6 us -> 21.4 us  [per_device(): array = lax.ppermute(sent, AXES, plan.pairs(*pairs[bit]))]
    pallas_call x1, Pallas kernels: 8.02 us -> 7.6 us  [make_table(): pl.pallas_call(functools.partial(table_kernel, plan, n_rep, [(b, ()) for...]
    pallas_call x14 -> x16, Pallas kernels: 1.43 us -> 1.41 us  [send_blocks(): pl.pallas_call(functools.partial(send_kernel, plan, len(got), entries, co...]
  transfers between devices with their start and end apart: 15 -> 17, of which waited for: 8 -> 5; matrix products, arithmetic and copies ran while one was open for 0% -> 0% of each run, Pallas kernels for 3% -> 4%
where the time goes in v6:
time: 40.2 us; the launch traced here: 40 us
  starting transfers between devices  21.4 us (53%)
  Pallas kernels  9.8 us (24%)
  waiting for transfers between devices  8.15 us (20%)
  between operations  0.69 us (2%)
    ppermute x17, starting transfers between devices, per_device(): array = lax.ppermute(sent, AXES, plan.pairs(*pairs[bit]))  21.4 us
    ppermute x17, waiting for transfers between devices, per_device(): array = lax.ppermute(sent, AXES, plan.pairs(*pairs[bit]))  8.15 us
    pallas_call x1, Pallas kernels, make_table(): pl.pallas_call(functools.partial(table_kernel, plan, n_rep, [(b, ()) for...  7.6 us
    pallas_call x16, Pallas kernels, send_blocks(): pl.pallas_call(functools.partial(send_kernel, plan, len(got), entries, co...  1.41 us
  transfers between devices with their start and end apart: 17, of which 5 were waited for; matrix products, arithmetic and copies ran while one was open for 0% of the time, Pallas kernels for 4%

profile of v6, /device:TPU:0, one launch (start us, length us, event | category | flops | bytes accessed | tf_op | source)
XLA Modules:
  0.0 40.0 jit_solution(9175513322357597000)
XLA Ops:
  0.6 7.6 %make_table.1 = (f32[4,264,128]{2,1,0:T(8,128)S(1)}, f32[12288,128]{1,0:T(8,128)S(1)}, f32[12288,128]{1,0:T(8,128)S(1)}, f32[12288,128]{1,0:T(8,128)S(1)}) custom-call(s32[32,128]{1,0:T(8,128)} %bitcast.9, s32[32,128]{1,0:T(8,128)} %bitcast.10, f32[8192,128]{1,0:T(8,128)} %bitcast.8), custom_call_target="tpu_custom_call" | custom-call | tf_op jit(solution)/shard_map/make_table/pallas_call | solution.py:209
  8.2 0.6 %collective-permute-start.7 = (f32[4,264,128]{2,1,0:T(8,128)S(1)}, f32[4,264,128]{2,1,0:T(8,128)S(1)}, u32[]{:S(2)}, u32[]{:S(2)}) collective-permute-start(f32[4,264,128]{2,1,0:T(8,128)S(1)} %get-tuple-element.11), channel_id=1, source_target_pairs={{0,8},{1,9},{2,10},{3,11},{4,12},{5,13},{6,14},{7,15},{8,0},{9,1},... | collective-permute-start | bytes 1622024 | tf_op jit(solution)/shard_map/ppermute | solution.py:348
  8.8 0.2 send_blocks.17
  9.0 0.2 send_blocks.22
  9.2 0.6 %collective-permute-start.6 = (f32[4,264,128]{2,1,0:T(8,128)S(1)}, f32[4,264,128]{2,1,0:T(8,128)S(1)}, u32[]{:S(2)}, u32[]{:S(2)}) collective-permute-start(f32[4,264,128]{2,1,0:T(8,128)S(1)} %send_blocks.22), channel_id=1, source_target_pairs={{0,8},{1,9},{2,10},{3,11},{4,12},{5,13},{6,14},{7,15},{8,0},{9,1},... | collective-permute-start | bytes 1622024 | tf_op jit(solution)/shard_map/ppermute | solution.py:348
  9.8 0.2 send_blocks.16
  10.0 0.3 collective-permute-done.7.refs_3_
  10.5 2.9 %collective-permute-start.9 = (f32[2,264,128]{2,1,0:T(8,128)S(1)}, f32[2,264,128]{2,1,0:T(8,128)S(1)}, u32[]{:S(2)}, u32[]{:S(2)}) collective-permute-start(f32[2,264,128]{2,1,0:T(8,128)S(1)} %send_blocks.24), channel_id=1, source_target_pairs={{0,16},{1,17},{2,18},{3,19},{4,20},{5,21},{6,22},{7,23},{8,9},{9,8... | collective-permute-start | bytes 811016 | tf_op jit(solution)/shard_map/ppermute | solution.py:348
  13.6 2.1 %collective-permute-start.14 = (f32[1,264,128]{2,1,0:T(8,128)S(1)}, f32[1,264,128]{2,1,0:T(8,128)S(1)}, u32[]{:S(2)}, u32[]{:S(2)}) collective-permute-start(f32[1,264,128]{2,1,0:T(8,128)S(1)} %send_blocks.29), channel_id=1, source_target_pairs={{0,2},{1,3},{2,0},{3,1},{4,6},{5,7},{6,4},{7,5},{8,10},{9,11},{10,... | collective-permute-start | bytes 405512 | tf_op jit(solution)/shard_map/ppermute | solution.py:348
  15.8 2.1 %collective-permute-done.9.refs_4_ = f32[2,264,128]{2,1,0:T(8,128)S(1)} collective-permute-done((f32[2,264,128]{2,1,0:T(8,128)S(1)}, f32[2,264,128]{2,1,0:T(8,128)S(1)}, u32[]{:S(2)}, u32[]{:S(2)}) %collective-permute-start.9) | collective-permute-done | bytes 270368 | tf_op jit(solution)/shard_map/ppermute | solution.py:348
  17.9 2.1 %collective-permute-start.11 = (f32[1,264,128]{2,1,0:T(8,128)S(1)}, f32[1,264,128]{2,1,0:T(8,128)S(1)}, u32[]{:S(2)}, u32[]{:S(2)}) collective-permute-start(f32[1,264,128]{2,1,0:T(8,128)S(1)} %send_blocks.26), channel_id=1, source_target_pairs={{0,1},{1,0},{2,3},{3,2},{4,5},{5,4},{6,7},{7,6},{8,24},{9,25},{10,... | collective-permute-start | bytes 405512 | tf_op jit(solution)/shard_map/ppermute | solution.py:348
  20.0 1.6 %collective-permute-start.2 = (f32[1,264,128]{2,1,0:T(8,128)S(1)}, f32[1,264,128]{2,1,0:T(8,128)S(1)}, u32[]{:S(2)}, u32[]{:S(2)}) collective-permute-start(f32[1,264,128]{2,1,0:T(8,128)S(1)} %send_blocks.18), channel_id=1, source_target_pairs={{0,2},{1,3},{2,0},{3,1},{4,6},{5,7},{6,4},{7,5},{8,10},{9,11},{10,... | collective-permute-start | bytes 405512 | tf_op jit(solution)/shard_map/ppermute | solution.py:348
  21.7 0.6 %collective-permute-start.4 = (f32[1,264,128]{2,1,0:T(8,128)S(1)}, f32[1,264,128]{2,1,0:T(8,128)S(1)}, u32[]{:S(2)}, u32[]{:S(2)}) collective-permute-start(f32[1,264,128]{2,1,0:T(8,128)S(1)} %send_blocks.20), channel_id=1, source_target_pairs={{0,1},{1,0},{2,3},{3,2},{4,5},{5,4},{6,7},{7,6},{8,24},{9,25},{10,... | collective-permute-start | bytes 405512 | tf_op jit(solution)/shard_map/ppermute | solution.py:348
  22.4 1.6 %collective-permute-start.15 = (f32[1,264,128]{2,1,0:T(8,128)S(1)}, f32[1,264,128]{2,1,0:T(8,128)S(1)}, u32[]{:S(2)}, u32[]{:S(2)}) collective-permute-start(f32[1,264,128]{2,1,0:T(8,128)S(1)} %send_blocks.30), channel_id=1, source_target_pairs={{0,16},{1,17},{2,18},{3,19},{4,20},{5,21},{6,22},{7,23},{8,9},{9,8... | collective-permute-start | bytes 405512 | tf_op jit(solution)/shard_map/ppermute | solution.py:348
  24.1 1.6 %collective-permute-start.10 = (f32[1,264,128]{2,1,0:T(8,128)S(1)}, f32[1,264,128]{2,1,0:T(8,128)S(1)}, u32[]{:S(2)}, u32[]{:S(2)}) collective-permute-start(f32[1,264,128]{2,1,0:T(8,128)S(1)} %send_blocks.25), channel_id=1, source_target_pairs={{0,1},{1,0},{2,3},{3,2},{4,5},{5,4},{6,7},{7,6},{8,24},{9,25},{10,... | collective-permute-start | bytes 405512 | tf_op jit(solution)/shard_map/ppermute | solution.py:348
  25.7 0.8 %collective-permute-start.12 = (f32[1,264,128]{2,1,0:T(8,128)S(1)}, f32[1,264,128]{2,1,0:T(8,128)S(1)}, u32[]{:S(2)}, u32[]{:S(2)}) collective-permute-start(f32[1,264,128]{2,1,0:T(8,128)S(1)} %send_blocks.27), channel_id=1, source_target_pairs={{0,2},{1,3},{2,0},{3,1},{4,6},{5,7},{6,4},{7,5},{8,10},{9,11},{10,... | collective-permute-start | bytes 405512 | tf_op jit(solution)/shard_map/ppermute | solution.py:348
  26.5 1.4 %collective-permute-start.3 = (f32[1,264,128]{2,1,0:T(8,128)S(1)}, f32[1,264,128]{2,1,0:T(8,128)S(1)}, u32[]{:S(2)}, u32[]{:S(2)}) collective-permute-start(f32[1,264,128]{2,1,0:T(8,128)S(1)} %send_blocks.19), channel_id=1, source_target_pairs={{0,16},{1,17},{2,18},{3,19},{4,20},{5,21},{6,22},{7,23},{8,9},{9,8... | collective-permute-start | bytes 405512 | tf_op jit(solution)/shard_map/ppermute | solution.py:348
  28.0 0.5 %collective-permute-start.5 = (f32[1,264,128]{2,1,0:T(8,128)S(1)}, f32[1,264,128]{2,1,0:T(8,128)S(1)}, u32[]{:S(2)}, u32[]{:S(2)}) collective-permute-start(f32[1,264,128]{2,1,0:T(8,128)S(1)} %send_blocks.21), channel_id=1, source_target_pairs={{0,2},{1,3},{2,0},{3,1},{4,6},{5,7},{6,4},{7,5},{8,10},{9,11},{10,... | collective-permute-start | bytes 405512 | tf_op jit(solution)/shard_map/ppermute | solution.py:348
  28.6 1.1 %collective-permute-start.16 = (f32[1,264,128]{2,1,0:T(8,128)S(1)}, f32[1,264,128]{2,1,0:T(8,128)S(1)}, u32[]{:S(2)}, u32[]{:S(2)}) collective-permute-start(f32[1,264,128]{2,1,0:T(8,128)S(1)} %send_blocks.31), channel_id=1, source_target_pairs={{0,1},{1,0},{2,3},{3,2},{4,5},{5,4},{6,7},{7,6},{8,24},{9,25},{10,... | collective-permute-start | bytes 405512 | tf_op jit(solution)/shard_map/ppermute | solution.py:348
  29.7 0.1 collective-permute-done.10.refs_5_
  29.9 1.3 %collective-permute-done.12.refs_6_ = f32[1,264,128]{2,1,0:T(8,128)S(1)} collective-permute-done((f32[1,264,128]{2,1,0:T(8,128)S(1)}, f32[1,264,128]{2,1,0:T(8,128)S(1)}, u32[]{:S(2)}, u32[]{:S(2)}) %collective-permute-start.12) | collective-permute-done | bytes 135200 | tf_op jit(solution)/shard_map/ppermute | solution.py:348
  31.3 3.7 %collective-permute-start.13 = (f32[1,264,128]{2,1,0:T(8,128)S(1)}, f32[1,264,128]{2,1,0:T(8,128)S(1)}, u32[]{:S(2)}, u32[]{:S(2)}) collective-permute-start(f32[1,264,128]{2,1,0:T(8,128)S(1)} %send_blocks.28), channel_id=1, source_target_pairs={{0,4},{1,5},{2,6},{3,7},{4,0},{5,1},{6,2},{7,3},{8,12},{9,13},{10,... | collective-permute-start | bytes 405512 | tf_op jit(solution)/shard_map/ppermute | solution.py:348
  35.0 4.2 %collective-permute-done.13.refs_6_ = f32[1,264,128]{2,1,0:T(8,128)S(1)} collective-permute-done((f32[1,264,128]{2,1,0:T(8,128)S(1)}, f32[1,264,128]{2,1,0:T(8,128)S(1)}, u32[]{:S(2)}, u32[]{:S(2)}) %collective-permute-start.13) | collective-permute-done | bytes 135200 | tf_op jit(solution)/shard_map/ppermute | solution.py:348
  39.2 0.8 %finish.1 = (f32[128,256]{1,0:T(8,128)}, f32[1,128]{1,0:T(1,128)}) custom-call(f32[12288,128]{1,0:T(8,128)S(1)} %get-tuple-element.8.refs_0_, f32[12288,128]{1,0:T(8,128)S(1)} %get-tuple-element.9.refs_1_, f32[12288,128]{1,0:T(8,128)S(1)} %get-tuple-element.10.refs_2_, f32[4,264,128]{2,1,0:T(8,128)S(1)} %collective-permute-done.refs_3_, ...), custom_call_target="tpu_custom_call" | custom-call | tf_op jit(solution)/shard_map/finish/pallas_call | solution.py:293
  (28 shorter events, 1.2 us)
Async XLA Ops:
  8.2 2.1 %collective-permute-start.7 = (f32[4,264,128]{2,1,0:T(8,128)S(1)}, f32[4,264,128]{2,1,0:T(8,128)S(1)}, u32[]{:S(2)}, u32[]{:S(2)}) collective-permute-start(f32[4,264,128]{2,1,0:T(8,128)S(1)} %get-tuple-element.11), channel_id=1, source_target_pairs={{0,8},{1,9},{2,10},{3,11},{4,12},{5,13},{6,14},{7,15},{8,0},{9,1},... | collective-permute-start | bytes 1622024 | tf_op jit(solution)/shard_map/ppermute | solution.py:348
  9.0 4.6 %collective-permute-start.1 = (f32[4,264,128]{2,1,0:T(8,128)S(1)}, f32[4,264,128]{2,1,0:T(8,128)S(1)}, u32[]{:S(2)}, u32[]{:S(2)}) collective-permute-start(f32[4,264,128]{2,1,0:T(8,128)S(1)} %send_blocks.17), channel_id=1, source_target_pairs={{0,8},{1,9},{2,10},{3,11},{4,12},{5,13},{6,14},{7,15},{8,0},{9,1},... | collective-permute-start | bytes 1622024 | tf_op jit(solution)/shard_map/ppermute | solution.py:348
  9.2 6.6 %collective-permute-start.6 = (f32[4,264,128]{2,1,0:T(8,128)S(1)}, f32[4,264,128]{2,1,0:T(8,128)S(1)}, u32[]{:S(2)}, u32[]{:S(2)}) collective-permute-start(f32[4,264,128]{2,1,0:T(8,128)S(1)} %send_blocks.22), channel_id=1, source_target_pairs={{0,8},{1,9},{2,10},{3,11},{4,12},{5,13},{6,14},{7,15},{8,0},{9,1},... | collective-permute-start | bytes 1622024 | tf_op jit(solution)/shard_map/ppermute | solution.py:348
  9.9 11.8 %collective-permute-start = (f32[4,264,128]{2,1,0:T(8,128)S(1)}, f32[4,264,128]{2,1,0:T(8,128)S(1)}, u32[]{:S(2)}, u32[]{:S(2)}) collective-permute-start(f32[4,264,128]{2,1,0:T(8,128)S(1)} %send_blocks.16), channel_id=1, source_target_pairs={{0,8},{1,9},{2,10},{3,11},{4,12},{5,13},{6,14},{7,15},{8,0},{9,1},... | collective-permute-start | bytes 1622024 | tf_op jit(solution)/shard_map/ppermute | solution.py:348
  10.5 7.4 %collective-permute-start.9 = (f32[2,264,128]{2,1,0:T(8,128)S(1)}, f32[2,264,128]{2,1,0:T(8,128)S(1)}, u32[]{:S(2)}, u32[]{:S(2)}) collective-permute-start(f32[2,264,128]{2,1,0:T(8,128)S(1)} %send_blocks.24), channel_id=1, source_target_pairs={{0,16},{1,17},{2,18},{3,19},{4,20},{5,21},{6,22},{7,23},{8,9},{9,8... | collective-permute-start | bytes 811016 | tf_op jit(solution)/shard_map/ppermute | solution.py:348
  13.5 10.6 %collective-permute-start.8 = (f32[2,264,128]{2,1,0:T(8,128)S(1)}, f32[2,264,128]{2,1,0:T(8,128)S(1)}, u32[]{:S(2)}, u32[]{:S(2)}) collective-permute-start(f32[2,264,128]{2,1,0:T(8,128)S(1)} %send_blocks.23), channel_id=1, source_target_pairs={{0,16},{1,17},{2,18},{3,19},{4,20},{5,21},{6,22},{7,23},{8,9},{9,8... | collective-permute-start | bytes 811016 | tf_op jit(solution)/shard_map/ppermute | solution.py:348
  13.6 8.7 %collective-permute-start.14 = (f32[1,264,128]{2,1,0:T(8,128)S(1)}, f32[1,264,128]{2,1,0:T(8,128)S(1)}, u32[]{:S(2)}, u32[]{:S(2)}) collective-permute-start(f32[1,264,128]{2,1,0:T(8,128)S(1)} %send_blocks.29), channel_id=1, source_target_pairs={{0,2},{1,3},{2,0},{3,1},{4,6},{5,7},{6,4},{7,5},{8,10},{9,11},{10,... | collective-permute-start | bytes 405512 | tf_op jit(solution)/shard_map/ppermute | solution.py:348
  17.9 7.7 %collective-permute-start.11 = (f32[1,264,128]{2,1,0:T(8,128)S(1)}, f32[1,264,128]{2,1,0:T(8,128)S(1)}, u32[]{:S(2)}, u32[]{:S(2)}) collective-permute-start(f32[1,264,128]{2,1,0:T(8,128)S(1)} %send_blocks.26), channel_id=1, source_target_pairs={{0,1},{1,0},{2,3},{3,2},{4,5},{5,4},{6,7},{7,6},{8,24},{9,25},{10,... | collective-permute-start | bytes 405512 | tf_op jit(solution)/shard_map/ppermute | solution.py:348
  20.0 6.5 %collective-permute-start.2 = (f32[1,264,128]{2,1,0:T(8,128)S(1)}, f32[1,264,128]{2,1,0:T(8,128)S(1)}, u32[]{:S(2)}, u32[]{:S(2)}) collective-permute-start(f32[1,264,128]{2,1,0:T(8,128)S(1)} %send_blocks.18), channel_id=1, source_target_pairs={{0,2},{1,3},{2,0},{3,1},{4,6},{5,7},{6,4},{7,5},{8,10},{9,11},{10,... | collective-permute-start | bytes 405512 | tf_op jit(solution)/shard_map/ppermute | solution.py:348
  21.7 6.2 %collective-permute-start.4 = (f32[1,264,128]{2,1,0:T(8,128)S(1)}, f32[1,264,128]{2,1,0:T(8,128)S(1)}, u32[]{:S(2)}, u32[]{:S(2)}) collective-permute-start(f32[1,264,128]{2,1,0:T(8,128)S(1)} %send_blocks.20), channel_id=1, source_target_pairs={{0,1},{1,0},{2,3},{3,2},{4,5},{5,4},{6,7},{7,6},{8,24},{9,25},{10,... | collective-permute-start | bytes 405512 | tf_op jit(solution)/shard_map/ppermute | solution.py:348
  22.4 6.2 %collective-permute-start.15 = (f32[1,264,128]{2,1,0:T(8,128)S(1)}, f32[1,264,128]{2,1,0:T(8,128)S(1)}, u32[]{:S(2)}, u32[]{:S(2)}) collective-permute-start(f32[1,264,128]{2,1,0:T(8,128)S(1)} %send_blocks.30), channel_id=1, source_target_pairs={{0,16},{1,17},{2,18},{3,19},{4,20},{5,21},{6,22},{7,23},{8,9},{9,8... | collective-permute-start | bytes 405512 | tf_op jit(solution)/shard_map/ppermute | solution.py:348
  24.1 5.8 %collective-permute-start.10 = (f32[1,264,128]{2,1,0:T(8,128)S(1)}, f32[1,264,128]{2,1,0:T(8,128)S(1)}, u32[]{:S(2)}, u32[]{:S(2)}) collective-permute-start(f32[1,264,128]{2,1,0:T(8,128)S(1)} %send_blocks.25), channel_id=1, source_target_pairs={{0,1},{1,0},{2,3},{3,2},{4,5},{5,4},{6,7},{7,6},{8,24},{9,25},{10,... | collective-permute-start | bytes 405512 | tf_op jit(solution)/shard_map/ppermute | solution.py:348
  25.7 5.5 %collective-permute-start.12 = (f32[1,264,128]{2,1,0:T(8,128)S(1)}, f32[1,264,128]{2,1,0:T(8,128)S(1)}, u32[]{:S(2)}, u32[]{:S(2)}) collective-permute-start(f32[1,264,128]{2,1,0:T(8,128)S(1)} %send_blocks.27), channel_id=1, source_target_pairs={{0,2},{1,3},{2,0},{3,1},{4,6},{5,7},{6,4},{7,5},{8,10},{9,11},{10,... | collective-permute-start | bytes 405512 | tf_op jit(solution)/shard_map/ppermute | solution.py:348
  26.5 8.4 %collective-permute-start.3 = (f32[1,264,128]{2,1,0:T(8,128)S(1)}, f32[1,264,128]{2,1,0:T(8,128)S(1)}, u32[]{:S(2)}, u32[]{:S(2)}) collective-permute-start(f32[1,264,128]{2,1,0:T(8,128)S(1)} %send_blocks.19), channel_id=1, source_target_pairs={{0,16},{1,17},{2,18},{3,19},{4,20},{5,21},{6,22},{7,23},{8,9},{9,8... | collective-permute-start | bytes 405512 | tf_op jit(solution)/shard_map/ppermute | solution.py:348
  28.0 6.9 %collective-permute-start.5 = (f32[1,264,128]{2,1,0:T(8,128)S(1)}, f32[1,264,128]{2,1,0:T(8,128)S(1)}, u32[]{:S(2)}, u32[]{:S(2)}) collective-permute-start(f32[1,264,128]{2,1,0:T(8,128)S(1)} %send_blocks.21), channel_id=1, source_target_pairs={{0,2},{1,3},{2,0},{3,1},{4,6},{5,7},{6,4},{7,5},{8,10},{9,11},{10,... | collective-permute-start | bytes 405512 | tf_op jit(solution)/shard_map/ppermute | solution.py:348
  28.6 6.3 %collective-permute-start.16 = (f32[1,264,128]{2,1,0:T(8,128)S(1)}, f32[1,264,128]{2,1,0:T(8,128)S(1)}, u32[]{:S(2)}, u32[]{:S(2)}) collective-permute-start(f32[1,264,128]{2,1,0:T(8,128)S(1)} %send_blocks.31), channel_id=1, source_target_pairs={{0,1},{1,0},{2,3},{3,2},{4,5},{5,4},{6,7},{7,6},{8,24},{9,25},{10,... | collective-permute-start | bytes 405512 | tf_op jit(solution)/shard_map/ppermute | solution.py:348
  31.3 7.9 %collective-permute-start.13 = (f32[1,264,128]{2,1,0:T(8,128)S(1)}, f32[1,264,128]{2,1,0:T(8,128)S(1)}, u32[]{:S(2)}, u32[]{:S(2)}) collective-permute-start(f32[1,264,128]{2,1,0:T(8,128)S(1)} %send_blocks.28), channel_id=1, source_target_pairs={{0,4},{1,5},{2,6},{3,7},{4,0},{5,1},{6,2},{7,3},{8,12},{9,13},{10,... | collective-permute-start | bytes 405512 | tf_op jit(solution)/shard_map/ppermute | solution.py:348

commit v7 on v6

--- a/solution.py
+++ b/solution.py
@@ -30,7 +30,6 @@
         self.group = SUB * (self.tiles + 1)
         self.groups = self.block // SUB
         self.part = self.block * self.tiles
-        self.unit = self.part + SUB
         self.all = tuple(range(self.tiles))
         rep = bits_of(n_rep)
         dom = [len(rep) + b for b in bits_of(n_dom)]
@@ -268,12 +267,16 @@
     )(*tables, *got)
 
 
-def finish_kernel(plan, n_got, terms, *refs):
-    tables, got = refs[:TABLES], refs[TABLES : TABLES + n_got]
-    means, counts, total = refs[TABLES + n_got :]
-    arrived = [(got[k], u, own) for k, u, own in terms]
-    sum_block(plan, tables, 0, total, 0, arrived, plan.all, True)
-    row = total[0, pl.ds(plan.part, 1), :]
+def finish_kernel(plan, units, *refs):
+    got, (means, counts) = refs[: len(units)], refs[len(units) :]
+
+    def total(line, size):
+        out = got[0][units[0], pl.ds(line, size), :]
+        for ref, unit in zip(got[1:], units[1:]):
+            out = out + ref[unit, pl.ds(line, size), :]
+        return out
+
+    row = total(plan.part, 1)
     counts[...] = row[:, : plan.block]
     shape = (plan.block, LANES)
     diagonal = lax.broadcasted_iota(jnp.int32, shape, 0) == lax.broadcasted_iota(
@@ -284,24 +287,23 @@
     for g in range(plan.groups):
         for t in range(plan.tiles):
             means[g * SUB : (g + 1) * SUB, t * LANES : (t + 1) * LANES] = (
-                total[0, pl.ds((g * plan.tiles + t) * SUB, SUB), :]
+                total((g * plan.tiles + t) * SUB, SUB)
                 / column[g * SUB : (g + 1) * SUB, :]
             )
 
 
-def finish(plan, tables, got, terms):
+def finish(plan, got, units):
     means, counts = pl.pallas_call(
-        functools.partial(finish_kernel, plan, len(got), terms),
+        functools.partial(finish_kernel, plan, units),
         out_shape=[
             jax.ShapeDtypeStruct((plan.block, plan.tiles * LANES), jnp.float32),
             jax.ShapeDtypeStruct((1, plan.block), jnp.float32),
         ],
-        in_specs=[VMEM] * (len(tables) + len(got)),
+        in_specs=[VMEM] * len(got),
         out_specs=[VMEM] * 2,
-        scratch_shapes=[pltpu.VMEM((1, plan.unit, LANES), jnp.float32)],
         compiler_params=pltpu.CompilerParams(vmem_limit_bytes=4 << 20),
         name="finish",
-    )(*tables, *got)
+    )(*got)
     return means, counts.reshape(plan.block)
 
 
@@ -348,8 +350,12 @@
         array = lax.ppermute(sent, AXES, plan.pairs(*pairs[bit]))
         for unit, b in enumerate(blocks):
             arrived.setdefault(b - weight[bit], []).append((array, unit, cols))
-    got, [(_, terms)] = entries_of([0], plan.all)
-    return finish(plan, tables, got, terms)
+    late = 2 + len(extra)
+    arrived[0], last = arrived[0][:-late], arrived[0][-late:]
+    got, entries = entries_of([0], cols)
+    early = send_blocks(plan, tables, got, entries, cols, counted)
+    arrays = [early] + [array for array, _, _ in last]
+    return finish(plan, arrays, [0] + [unit for _, unit, _ in last])
 
 
 def middle_names(n):
@@ -371,9 +377,9 @@
     move("core", far=1, first=1)
     move("core", far=1, first=0)
     move("core", far=0, near=1)
-    move("core", far=0, near=0)
     move("first", core=0, far=1, then=1)
     move("first", core=0, far=1, then=0)
+    move("core", far=0, near=0)
     move("near", core=0, far=0, first=1, then=1)
     move("near", core=0, far=0, first=1, then=0)
     then(far=1, near=1)

time: 40.2 us -> 40.1 us (level)
    pallas_call x16 -> x17, Pallas kernels: 1.41 us -> 1.47 us  [send_blocks(): pl.pallas_call(functools.partial(send_kernel, plan, len(got), entries, co...]
where the time goes in v7:
time: 40.1 us; the launch traced here: 40 us
  starting transfers between devices  21.4 us (53%)
  Pallas kernels  9.84 us (25%)
  waiting for transfers between devices  8.08 us (20%)
  between operations  0.69 us (2%)
    ppermute x17, starting transfers between devices, per_device(): array = lax.ppermute(sent, AXES, plan.pairs(*pairs[bit]))  21.4 us
    ppermute x17, waiting for transfers between devices, per_device(): array = lax.ppermute(sent, AXES, plan.pairs(*pairs[bit]))  8.08 us
    pallas_call x1, Pallas kernels, make_table(): pl.pallas_call(functools.partial(table_kernel, plan, n_rep, [(b, ()) for...  7.6 us
    pallas_call x17, Pallas kernels, send_blocks(): pl.pallas_call(functools.partial(send_kernel, plan, len(got), entries, co...  1.47 us
  transfers between devices with their start and end apart: 17, of which 5 were waited for; matrix products, arithmetic and copies ran while one was open for 0% of the time, Pallas kernels for 4%

profile of v7, /device:TPU:0, one launch (start us, length us, event | category | flops | bytes accessed | tf_op | source)
XLA Modules:
  0.0 40.0 jit_solution(4636155015184396196)
XLA Ops:
  0.6 7.6 %make_table.1 = (f32[4,264,128]{2,1,0:T(8,128)S(1)}, f32[12288,128]{1,0:T(8,128)S(1)}, f32[12288,128]{1,0:T(8,128)S(1)}, f32[12288,128]{1,0:T(8,128)S(1)}) custom-call(s32[32,128]{1,0:T(8,128)} %bitcast.9, s32[32,128]{1,0:T(8,128)} %bitcast.10, f32[8192,128]{1,0:T(8,128)} %bitcast.8), custom_call_target="tpu_custom_call" | custom-call | tf_op jit(solution)/shard_map/make_table/pallas_call | solution.py:208
  8.2 0.6 %collective-permute-start.7 = (f32[4,264,128]{2,1,0:T(8,128)S(1)}, f32[4,264,128]{2,1,0:T(8,128)S(1)}, u32[]{:S(2)}, u32[]{:S(2)}) collective-permute-start(f32[4,264,128]{2,1,0:T(8,128)S(1)} %get-tuple-element.11), channel_id=1, source_target_pairs={{0,8},{1,9},{2,10},{3,11},{4,12},{5,13},{6,14},{7,15},{8,0},{9,1},... | collective-permute-start | bytes 1622024 | tf_op jit(solution)/shard_map/ppermute | solution.py:350
  8.8 0.2 send_blocks.18
  9.0 0.2 send_blocks.24
  9.2 0.6 %collective-permute-start.6 = (f32[4,264,128]{2,1,0:T(8,128)S(1)}, f32[4,264,128]{2,1,0:T(8,128)S(1)}, u32[]{:S(2)}, u32[]{:S(2)}) collective-permute-start(f32[4,264,128]{2,1,0:T(8,128)S(1)} %send_blocks.24), channel_id=1, source_target_pairs={{0,8},{1,9},{2,10},{3,11},{4,12},{5,13},{6,14},{7,15},{8,0},{9,1},... | collective-permute-start | bytes 1622024 | tf_op jit(solution)/shard_map/ppermute | solution.py:350
  9.8 0.2 send_blocks.17
  10.0 0.3 collective-permute-done.7.refs_3_
  10.5 2.9 %collective-permute-start.9 = (f32[2,264,128]{2,1,0:T(8,128)S(1)}, f32[2,264,128]{2,1,0:T(8,128)S(1)}, u32[]{:S(2)}, u32[]{:S(2)}) collective-permute-start(f32[2,264,128]{2,1,0:T(8,128)S(1)} %send_blocks.26), channel_id=1, source_target_pairs={{0,16},{1,17},{2,18},{3,19},{4,20},{5,21},{6,22},{7,23},{8,9},{9,8... | collective-permute-start | bytes 811016 | tf_op jit(solution)/shard_map/ppermute | solution.py:350
  13.6 2.1 %collective-permute-start.14 = (f32[1,264,128]{2,1,0:T(8,128)S(1)}, f32[1,264,128]{2,1,0:T(8,128)S(1)}, u32[]{:S(2)}, u32[]{:S(2)}) collective-permute-start(f32[1,264,128]{2,1,0:T(8,128)S(1)} %send_blocks.31), channel_id=1, source_target_pairs={{0,2},{1,3},{2,0},{3,1},{4,6},{5,7},{6,4},{7,5},{8,10},{9,11},{10,... | collective-permute-start | bytes 405512 | tf_op jit(solution)/shard_map/ppermute | solution.py:350
  15.8 2.1 %collective-permute-done.9.refs_4_ = f32[2,264,128]{2,1,0:T(8,128)S(1)} collective-permute-done((f32[2,264,128]{2,1,0:T(8,128)S(1)}, f32[2,264,128]{2,1,0:T(8,128)S(1)}, u32[]{:S(2)}, u32[]{:S(2)}) %collective-permute-start.9) | collective-permute-done | bytes 270368 | tf_op jit(solution)/shard_map/ppermute | solution.py:350
  17.9 2.1 %collective-permute-start.11 = (f32[1,264,128]{2,1,0:T(8,128)S(1)}, f32[1,264,128]{2,1,0:T(8,128)S(1)}, u32[]{:S(2)}, u32[]{:S(2)}) collective-permute-start(f32[1,264,128]{2,1,0:T(8,128)S(1)} %send_blocks.28), channel_id=1, source_target_pairs={{0,1},{1,0},{2,3},{3,2},{4,5},{5,4},{6,7},{7,6},{8,24},{9,25},{10,... | collective-permute-start | bytes 405512 | tf_op jit(solution)/shard_map/ppermute | solution.py:350
  20.0 1.6 %collective-permute-start.2 = (f32[1,264,128]{2,1,0:T(8,128)S(1)}, f32[1,264,128]{2,1,0:T(8,128)S(1)}, u32[]{:S(2)}, u32[]{:S(2)}) collective-permute-start(f32[1,264,128]{2,1,0:T(8,128)S(1)} %send_blocks.19), channel_id=1, source_target_pairs={{0,2},{1,3},{2,0},{3,1},{4,6},{5,7},{6,4},{7,5},{8,10},{9,11},{10,... | collective-permute-start | bytes 405512 | tf_op jit(solution)/shard_map/ppermute | solution.py:350
  21.7 0.6 %collective-permute-start.4 = (f32[1,264,128]{2,1,0:T(8,128)S(1)}, f32[1,264,128]{2,1,0:T(8,128)S(1)}, u32[]{:S(2)}, u32[]{:S(2)}) collective-permute-start(f32[1,264,128]{2,1,0:T(8,128)S(1)} %send_blocks.21), channel_id=1, source_target_pairs={{0,1},{1,0},{2,3},{3,2},{4,5},{5,4},{6,7},{7,6},{8,24},{9,25},{10,... | collective-permute-start | bytes 405512 | tf_op jit(solution)/shard_map/ppermute | solution.py:350
  22.4 1.6 %collective-permute-start.15 = (f32[1,264,128]{2,1,0:T(8,128)S(1)}, f32[1,264,128]{2,1,0:T(8,128)S(1)}, u32[]{:S(2)}, u32[]{:S(2)}) collective-permute-start(f32[1,264,128]{2,1,0:T(8,128)S(1)} %send_blocks.32), channel_id=1, source_target_pairs={{0,16},{1,17},{2,18},{3,19},{4,20},{5,21},{6,22},{7,23},{8,9},{9,8... | collective-permute-start | bytes 405512 | tf_op jit(solution)/shard_map/ppermute | solution.py:350
  24.1 1.6 %collective-permute-start.10 = (f32[1,264,128]{2,1,0:T(8,128)S(1)}, f32[1,264,128]{2,1,0:T(8,128)S(1)}, u32[]{:S(2)}, u32[]{:S(2)}) collective-permute-start(f32[1,264,128]{2,1,0:T(8,128)S(1)} %send_blocks.27), channel_id=1, source_target_pairs={{0,1},{1,0},{2,3},{3,2},{4,5},{5,4},{6,7},{7,6},{8,24},{9,25},{10,... | collective-permute-start | bytes 405512 | tf_op jit(solution)/shard_map/ppermute | solution.py:350
  25.7 0.8 %collective-permute-start.12 = (f32[1,264,128]{2,1,0:T(8,128)S(1)}, f32[1,264,128]{2,1,0:T(8,128)S(1)}, u32[]{:S(2)}, u32[]{:S(2)}) collective-permute-start(f32[1,264,128]{2,1,0:T(8,128)S(1)} %send_blocks.29), channel_id=1, source_target_pairs={{0,2},{1,3},{2,0},{3,1},{4,6},{5,7},{6,4},{7,5},{8,10},{9,11},{10,... | collective-permute-start | bytes 405512 | tf_op jit(solution)/shard_map/ppermute | solution.py:350
  26.5 1.4 %collective-permute-start.3 = (f32[1,264,128]{2,1,0:T(8,128)S(1)}, f32[1,264,128]{2,1,0:T(8,128)S(1)}, u32[]{:S(2)}, u32[]{:S(2)}) collective-permute-start(f32[1,264,128]{2,1,0:T(8,128)S(1)} %send_blocks.20), channel_id=1, source_target_pairs={{0,16},{1,17},{2,18},{3,19},{4,20},{5,21},{6,22},{7,23},{8,9},{9,8... | collective-permute-start | bytes 405512 | tf_op jit(solution)/shard_map/ppermute | solution.py:350
  28.0 0.5 %collective-permute-start.5 = (f32[1,264,128]{2,1,0:T(8,128)S(1)}, f32[1,264,128]{2,1,0:T(8,128)S(1)}, u32[]{:S(2)}, u32[]{:S(2)}) collective-permute-start(f32[1,264,128]{2,1,0:T(8,128)S(1)} %send_blocks.22), channel_id=1, source_target_pairs={{0,2},{1,3},{2,0},{3,1},{4,6},{5,7},{6,4},{7,5},{8,10},{9,11},{10,... | collective-permute-start | bytes 405512 | tf_op jit(solution)/shard_map/ppermute | solution.py:350
  28.6 1.1 %collective-permute-start.16 = (f32[1,264,128]{2,1,0:T(8,128)S(1)}, f32[1,264,128]{2,1,0:T(8,128)S(1)}, u32[]{:S(2)}, u32[]{:S(2)}) collective-permute-start(f32[1,264,128]{2,1,0:T(8,128)S(1)} %send_blocks.33), channel_id=1, source_target_pairs={{0,1},{1,0},{2,3},{3,2},{4,5},{5,4},{6,7},{7,6},{8,24},{9,25},{10,... | collective-permute-start | bytes 405512 | tf_op jit(solution)/shard_map/ppermute | solution.py:350
  29.7 0.1 collective-permute-done.10.refs_5_
  29.9 1.3 %collective-permute-done.12.refs_6_ = f32[1,264,128]{2,1,0:T(8,128)S(1)} collective-permute-done((f32[1,264,128]{2,1,0:T(8,128)S(1)}, f32[1,264,128]{2,1,0:T(8,128)S(1)}, u32[]{:S(2)}, u32[]{:S(2)}) %collective-permute-start.12) | collective-permute-done | bytes 135200 | tf_op jit(solution)/shard_map/ppermute | solution.py:350
  31.3 3.7 %collective-permute-start.13 = (f32[1,264,128]{2,1,0:T(8,128)S(1)}, f32[1,264,128]{2,1,0:T(8,128)S(1)}, u32[]{:S(2)}, u32[]{:S(2)}) collective-permute-start(f32[1,264,128]{2,1,0:T(8,128)S(1)} %send_blocks.30), channel_id=1, source_target_pairs={{0,4},{1,5},{2,6},{3,7},{4,0},{5,1},{6,2},{7,3},{8,12},{9,13},{10,... | collective-permute-start | bytes 405512 | tf_op jit(solution)/shard_map/ppermute | solution.py:350
  35.0 4.2 %collective-permute-done.13.refs_1_ = f32[1,264,128]{2,1,0:T(8,128)S(1)} collective-permute-done((f32[1,264,128]{2,1,0:T(8,128)S(1)}, f32[1,264,128]{2,1,0:T(8,128)S(1)}, u32[]{:S(2)}, u32[]{:S(2)}) %collective-permute-start.13) | collective-permute-done | bytes 135200 | tf_op jit(solution)/shard_map/ppermute | solution.py:350
  39.2 0.8 %finish.1 = (f32[128,256]{1,0:T(8,128)}, f32[1,128]{1,0:T(1,128)}) custom-call(f32[1,264,128]{2,1,0:T(8,128)S(1)} %send_blocks.23.refs_0_, f32[1,264,128]{2,1,0:T(8,128)S(1)} %collective-permute-done.13.refs_1_, f32[1,264,128]{2,1,0:T(8,128)S(1)} %collective-permute-done.16.refs_2_), custom_call_target="tpu_custom_call" | custom-call | tf_op jit(solution)/shard_map/finish/pallas_call | solution.py:296
  (29 shorter events, 1.3 us)
Async XLA Ops:
  8.2 2.1 %collective-permute-start.7 = (f32[4,264,128]{2,1,0:T(8,128)S(1)}, f32[4,264,128]{2,1,0:T(8,128)S(1)}, u32[]{:S(2)}, u32[]{:S(2)}) collective-permute-start(f32[4,264,128]{2,1,0:T(8,128)S(1)} %get-tuple-element.11), channel_id=1, source_target_pairs={{0,8},{1,9},{2,10},{3,11},{4,12},{5,13},{6,14},{7,15},{8,0},{9,1},... | collective-permute-start | bytes 1622024 | tf_op jit(solution)/shard_map/ppermute | solution.py:350
  9.0 4.6 %collective-permute-start.1 = (f32[4,264,128]{2,1,0:T(8,128)S(1)}, f32[4,264,128]{2,1,0:T(8,128)S(1)}, u32[]{:S(2)}, u32[]{:S(2)}) collective-permute-start(f32[4,264,128]{2,1,0:T(8,128)S(1)} %send_blocks.18), channel_id=1, source_target_pairs={{0,8},{1,9},{2,10},{3,11},{4,12},{5,13},{6,14},{7,15},{8,0},{9,1},... | collective-permute-start | bytes 1622024 | tf_op jit(solution)/shard_map/ppermute | solution.py:350
  9.2 6.6 %collective-permute-start.6 = (f32[4,264,128]{2,1,0:T(8,128)S(1)}, f32[4,264,128]{2,1,0:T(8,128)S(1)}, u32[]{:S(2)}, u32[]{:S(2)}) collective-permute-start(f32[4,264,128]{2,1,0:T(8,128)S(1)} %send_blocks.24), channel_id=1, source_target_pairs={{0,8},{1,9},{2,10},{3,11},{4,12},{5,13},{6,14},{7,15},{8,0},{9,1},... | collective-permute-start | bytes 1622024 | tf_op jit(solution)/shard_map/ppermute | solution.py:350
  9.9 11.8 %collective-permute-start = (f32[4,264,128]{2,1,0:T(8,128)S(1)}, f32[4,264,128]{2,1,0:T(8,128)S(1)}, u32[]{:S(2)}, u32[]{:S(2)}) collective-permute-start(f32[4,264,128]{2,1,0:T(8,128)S(1)} %send_blocks.17), channel_id=1, source_target_pairs={{0,8},{1,9},{2,10},{3,11},{4,12},{5,13},{6,14},{7,15},{8,0},{9,1},... | collective-permute-start | bytes 1622024 | tf_op jit(solution)/shard_map/ppermute | solution.py:350
  10.5 7.4 %collective-permute-start.9 = (f32[2,264,128]{2,1,0:T(8,128)S(1)}, f32[2,264,128]{2,1,0:T(8,128)S(1)}, u32[]{:S(2)}, u32[]{:S(2)}) collective-permute-start(f32[2,264,128]{2,1,0:T(8,128)S(1)} %send_blocks.26), channel_id=1, source_target_pairs={{0,16},{1,17},{2,18},{3,19},{4,20},{5,21},{6,22},{7,23},{8,9},{9,8... | collective-permute-start | bytes 811016 | tf_op jit(solution)/shard_map/ppermute | solution.py:350
  13.5 10.6 %collective-permute-start.8 = (f32[2,264,128]{2,1,0:T(8,128)S(1)}, f32[2,264,128]{2,1,0:T(8,128)S(1)}, u32[]{:S(2)}, u32[]{:S(2)}) collective-permute-start(f32[2,264,128]{2,1,0:T(8,128)S(1)} %send_blocks.25), channel_id=1, source_target_pairs={{0,16},{1,17},{2,18},{3,19},{4,20},{5,21},{6,22},{7,23},{8,9},{9,8... | collective-permute-start | bytes 811016 | tf_op jit(solution)/shard_map/ppermute | solution.py:350
  13.6 8.7 %collective-permute-start.14 = (f32[1,264,128]{2,1,0:T(8,128)S(1)}, f32[1,264,128]{2,1,0:T(8,128)S(1)}, u32[]{:S(2)}, u32[]{:S(2)}) collective-permute-start(f32[1,264,128]{2,1,0:T(8,128)S(1)} %send_blocks.31), channel_id=1, source_target_pairs={{0,2},{1,3},{2,0},{3,1},{4,6},{5,7},{6,4},{7,5},{8,10},{9,11},{10,... | collective-permute-start | bytes 405512 | tf_op jit(solution)/shard_map/ppermute | solution.py:350
  17.9 7.7 %collective-permute-start.11 = (f32[1,264,128]{2,1,0:T(8,128)S(1)}, f32[1,264,128]{2,1,0:T(8,128)S(1)}, u32[]{:S(2)}, u32[]{:S(2)}) collective-permute-start(f32[1,264,128]{2,1,0:T(8,128)S(1)} %send_blocks.28), channel_id=1, source_target_pairs={{0,1},{1,0},{2,3},{3,2},{4,5},{5,4},{6,7},{7,6},{8,24},{9,25},{10,... | collective-permute-start | bytes 405512 | tf_op jit(solution)/shard_map/ppermute | solution.py:350
  20.0 6.5 %collective-permute-start.2 = (f32[1,264,128]{2,1,0:T(8,128)S(1)}, f32[1,264,128]{2,1,0:T(8,128)S(1)}, u32[]{:S(2)}, u32[]{:S(2)}) collective-permute-start(f32[1,264,128]{2,1,0:T(8,128)S(1)} %send_blocks.19), channel_id=1, source_target_pairs={{0,2},{1,3},{2,0},{3,1},{4,6},{5,7},{6,4},{7,5},{8,10},{9,11},{10,... | collective-permute-start | bytes 405512 | tf_op jit(solution)/shard_map/ppermute | solution.py:350
  21.7 6.2 %collective-permute-start.4 = (f32[1,264,128]{2,1,0:T(8,128)S(1)}, f32[1,264,128]{2,1,0:T(8,128)S(1)}, u32[]{:S(2)}, u32[]{:S(2)}) collective-permute-start(f32[1,264,128]{2,1,0:T(8,128)S(1)} %send_blocks.21), channel_id=1, source_target_pairs={{0,1},{1,0},{2,3},{3,2},{4,5},{5,4},{6,7},{7,6},{8,24},{9,25},{10,... | collective-permute-start | bytes 405512 | tf_op jit(solution)/shard_map/ppermute | solution.py:350
  22.4 6.2 %collective-permute-start.15 = (f32[1,264,128]{2,1,0:T(8,128)S(1)}, f32[1,264,128]{2,1,0:T(8,128)S(1)}, u32[]{:S(2)}, u32[]{:S(2)}) collective-permute-start(f32[1,264,128]{2,1,0:T(8,128)S(1)} %send_blocks.32), channel_id=1, source_target_pairs={{0,16},{1,17},{2,18},{3,19},{4,20},{5,21},{6,22},{7,23},{8,9},{9,8... | collective-permute-start | bytes 405512 | tf_op jit(solution)/shard_map/ppermute | solution.py:350
  24.1 5.8 %collective-permute-start.10 = (f32[1,264,128]{2,1,0:T(8,128)S(1)}, f32[1,264,128]{2,1,0:T(8,128)S(1)}, u32[]{:S(2)}, u32[]{:S(2)}) collective-permute-start(f32[1,264,128]{2,1,0:T(8,128)S(1)} %send_blocks.27), channel_id=1, source_target_pairs={{0,1},{1,0},{2,3},{3,2},{4,5},{5,4},{6,7},{7,6},{8,24},{9,25},{10,... | collective-permute-start | bytes 405512 | tf_op jit(solution)/shard_map/ppermute | solution.py:350
  25.7 5.5 %collective-permute-start.12 = (f32[1,264,128]{2,1,0:T(8,128)S(1)}, f32[1,264,128]{2,1,0:T(8,128)S(1)}, u32[]{:S(2)}, u32[]{:S(2)}) collective-permute-start(f32[1,264,128]{2,1,0:T(8,128)S(1)} %send_blocks.29), channel_id=1, source_target_pairs={{0,2},{1,3},{2,0},{3,1},{4,6},{5,7},{6,4},{7,5},{8,10},{9,11},{10,... | collective-permute-start | bytes 405512 | tf_op jit(solution)/shard_map/ppermute | solution.py:350
  26.5 8.4 %collective-permute-start.3 = (f32[1,264,128]{2,1,0:T(8,128)S(1)}, f32[1,264,128]{2,1,0:T(8,128)S(1)}, u32[]{:S(2)}, u32[]{:S(2)}) collective-permute-start(f32[1,264,128]{2,1,0:T(8,128)S(1)} %send_blocks.20), channel_id=1, source_target_pairs={{0,16},{1,17},{2,18},{3,19},{4,20},{5,21},{6,22},{7,23},{8,9},{9,8... | collective-permute-start | bytes 405512 | tf_op jit(solution)/shard_map/ppermute | solution.py:350
  28.0 6.9 %collective-permute-start.5 = (f32[1,264,128]{2,1,0:T(8,128)S(1)}, f32[1,264,128]{2,1,0:T(8,128)S(1)}, u32[]{:S(2)}, u32[]{:S(2)}) collective-permute-start(f32[1,264,128]{2,1,0:T(8,128)S(1)} %send_blocks.22), channel_id=1, source_target_pairs={{0,2},{1,3},{2,0},{3,1},{4,6},{5,7},{6,4},{7,5},{8,10},{9,11},{10,... | collective-permute-start | bytes 405512 | tf_op jit(solution)/shard_map/ppermute | solution.py:350
  28.6 6.4 %collective-permute-start.16 = (f32[1,264,128]{2,1,0:T(8,128)S(1)}, f32[1,264,128]{2,1,0:T(8,128)S(1)}, u32[]{:S(2)}, u32[]{:S(2)}) collective-permute-start(f32[1,264,128]{2,1,0:T(8,128)S(1)} %send_blocks.33), channel_id=1, source_target_pairs={{0,1},{1,0},{2,3},{3,2},{4,5},{5,4},{6,7},{7,6},{8,24},{9,25},{10,... | collective-permute-start | bytes 405512 | tf_op jit(solution)/shard_map/ppermute | solution.py:350
  31.3 7.9 %collective-permute-start.13 = (f32[1,264,128]{2,1,0:T(8,128)S(1)}, f32[1,264,128]{2,1,0:T(8,128)S(1)}, u32[]{:S(2)}, u32[]{:S(2)}) collective-permute-start(f32[1,264,128]{2,1,0:T(8,128)S(1)} %send_blocks.30), channel_id=1, source_target_pairs={{0,4},{1,5},{2,6},{3,7},{4,0},{5,1},{6,2},{7,3},{8,12},{9,13},{10,... | collective-permute-start | bytes 405512 | tf_op jit(solution)/shard_map/ppermute | solution.py:350
